TPU v7x, 256 devices: a whole 4x4x8 slice. The times are simulated.
256 devices in a mesh: gx: 16 (over z, y_lo), gy: 4 (over x), gz: 4 (over y_hi, core).
Axes of the slice: x: 4, y: 4 (y_hi: 2, y_lo: 2; y = y_hi * 2 + y_lo), z: 8, core: 2. Of those that a mesh axis runs over, the one named last changes fastest.
Arguments:
- positions: float32 [3, 32, 8, 8, 128], P(None, 'gx', 'gy', 'gz'), may hold values from 0 to 1
- velocities: float32 [3, 32, 8, 8, 128], P(None, 'gx', 'gy', 'gz'), may hold values from -1.8 to 1.8
- pressure_prev: float32 [32, 8, 8, 128], P('gx', 'gy', 'gz'), may hold values from 0 to 0.5
- counts: int32 [32, 8, 8], P('gx', 'gy', 'gz'), may hold values from 1 to 128, as said below
- out_positions: float32 [3, 16, 4, 4, 128], P(None, 'gx', 'gy', 'gz'), may hold values from 0 to 1
- out_velocities: float32 [3, 16, 4, 4, 128], P(None, 'gx', 'gy', 'gz'), may hold values from -1.8 to 1.8
- out_dir: int32 [16, 4, 4, 128], P('gx', 'gy', 'gz'), may hold values from 0 to 5, as said below
- out_cell: int32 [16, 4, 4, 128], P('gx', 'gy', 'gz'), may hold values from 0 to 7, as said below
- out_count: int32 [16, 4, 4], P('gx', 'gy', 'gz'), may hold values from 1 to 128, as said below
Outputs:
- pressure: float32 [32, 8, 8, 128], P('gx', 'gy', 'gz')
- velocity_new: float32 [3, 32, 8, 8, 128], P(None, 'gx', 'gy', 'gz')
- density_error: float32 [2], replicated
Inputs may be any that keep to these rules, and one draw needn't show every extreme that they name: `counts`: each cell's count plus the live outbox slots bound for it is at most 128. `out_dir`: 0 +x, 1 -x, 2 +y, 3 -y, 4 +z, 5 -z. `out_cell`: local index in the receiving block, of a cell on the face through which the particle enters. `out_count`: the live slots are the first ones.
All inputs are finite; a program needn't handle non-finite values.
Results may differ from a plain program's by a relative error of at most 0.0003.
Values sent between devices are 32-bit elements; how exact they have to be, the bound alone decides.
No kernel may reach another device: no remote copies, remote signals or barrier semaphores. Data moves between devices by JAX's collectives and lax.ppermute only.
A program may use at most 64 MiB of HBM per device.

v0:
```python
import jax
import jax.numpy as jnp
from jax import lax
from jax.sharding import Mesh
from jax.sharding import PartitionSpec as P

ITERS = 2
GX = ("gx_0", "gx_1")
GZ = ("gz_0", "gz_1")
GX_GY_GZ = ("gx_0", "gx_1", "gy", "gz_0", "gz_1")


kernel_var = 0.25
time_step = 2.0
particle_mass = 1.0 / 45.0
rest_density = 1.0
relaxation = 0.5
floor_value = 0.1
gravity = 0.1


def passed_along(x, axis, by):
    size = lax.axis_size(axis)
    pairs = [(i, i + by) for i in range(size) if 0 <= i + by < size]
    return lax.ppermute(x, axis, pairs)


def with_halo(block, sides, width):
    for axis, dim in sides:
        count = lax.axis_size(axis)
        forward = [(i, i + 1) for i in range(count - 1)]
        backward = [(target, source) for source, target in forward]
        low = lax.ppermute(
            lax.slice_in_dim(block, block.shape[dim] - width, None, axis=dim), axis, forward
        )
        high = lax.ppermute(lax.slice_in_dim(block, 0, width, axis=dim), axis, backward)
        block = jnp.concatenate([low, block, high], axis=dim)
    return block


def one_axis_at_a_time(x, axes):
    for axis in axes:
        x = lax.psum(x, axis)
    return x


def stencil_offsets():
    return [(a, b, c) for a in (-1, 0, 1) for b in (-1, 0, 1) for c in (-1, 0, 1)]


def window(padded, offset, extent):
    return padded[
        :,
        1 + offset[0] : 1 + offset[0] + extent[0],
        1 + offset[1] : 1 + offset[1] + extent[1],
        1 + offset[2] : 1 + offset[2] + extent[2],
        :,
    ]


def geometry(center_pos, other_pos, offset):
    deltas = [
        center_pos[k][..., :, None] - other_pos[k][..., None, :] - float(offset[k])
        for k in range(3)
    ]
    distance = deltas[0] * deltas[0] + deltas[1] * deltas[1] + deltas[2] * deltas[2]
    kernel = jnp.exp(-distance / kernel_var)
    factor = -2.0 / kernel_var * kernel
    return (kernel, [factor * d for d in deltas])


def setup_pass(center_pos, center_vel, near_pos, near_vel, near_mass):
    extent = center_pos.shape[1:4]
    zeros = jnp.zeros(center_pos.shape[1:], jnp.float32)
    density, divergence, grad_square = (zeros, zeros, zeros)
    grad_sum = [zeros, zeros, zeros]
    for offset in stencil_offsets():
        other_pos = window(near_pos, offset, extent)
        other_vel = window(near_vel, offset, extent)
        masses = window(near_mass, offset, extent)[0][..., None, :]
        kernel, grads = geometry(center_pos, other_pos, offset)
        density = density + jnp.sum(masses * kernel, -1)
        closing = sum(
            (
                (center_vel[k][..., :, None] - other_vel[k][..., None, :]) * grads[k]
                for k in range(3)
            )
        )
        divergence = divergence + jnp.sum(masses * closing, -1)
        grad_sum = [grad_sum[k] + jnp.sum(masses * grads[k], -1) for k in range(3)]
        grad_square = grad_square + jnp.sum(
            masses * (grads[0] * grads[0] + grads[1] * grads[1] + grads[2] * grads[2]), -1
        )
    return jnp.stack([density, divergence, grad_sum[0], grad_sum[1], grad_sum[2], grad_square])


def accel_pass(center_pos, center_scaled, near_pos, near_mass, near_scaled):
    extent = center_pos.shape[1:4]
    zeros = jnp.zeros(center_pos.shape[1:], jnp.float32)
    totals = [zeros, zeros, zeros]
    for offset in stencil_offsets():
        other_pos = window(near_pos, offset, extent)
        masses = window(near_mass, offset, extent)[0][..., None, :]
        others = window(near_scaled, offset, extent)[0][..., None, :]
        kernel, grads = geometry(center_pos, other_pos, offset)
        factor = masses * (center_scaled[0][..., :, None] + others)
        totals = [totals[k] + jnp.sum(factor * grads[k], -1) for k in range(3)]
    return -jnp.stack(totals)


def apply_pass(center_pos, center_acc, near_pos, near_mass, near_acc):
    extent = center_pos.shape[1:4]
    total = jnp.zeros(center_pos.shape[1:], jnp.float32)
    for offset in stencil_offsets():
        other_pos = window(near_pos, offset, extent)
        masses = window(near_mass, offset, extent)[0][..., None, :]
        other_acc = window(near_acc, offset, extent)
        kernel, grads = geometry(center_pos, other_pos, offset)
        closing = sum(
            (
                (center_acc[k][..., :, None] - other_acc[k][..., None, :]) * grads[k]
                for k in range(3)
            )
        )
        total = total + jnp.sum(masses * closing, -1)
    return (time_step * time_step * total)[None]


def payloads(out_positions, out_velocities, out_dir, out_cell, out_count):
    migrants = out_dir.shape[-1]
    living = jnp.arange(migrants, dtype=jnp.int32) < out_count[..., None]
    cargo = jnp.concatenate([out_positions, out_velocities], 0)
    result = []
    for d in range(6):
        tagged = jnp.where(living & (out_dir == d), out_cell + 1, 0).astype(jnp.float32)
        result.append(jnp.concatenate([cargo, tagged[None]], 0))
    return result


def insert(particle_state, counts, arrivals):
    cell_total = counts.size
    slots = particle_state.shape[-1]
    flat_state = particle_state.reshape(6, cell_total * slots)
    filled = counts.reshape(cell_total)
    tagged = arrivals[6].astype(jnp.int32) - 1
    onehot = (tagged[:, None] == jnp.arange(cell_total, dtype=jnp.int32)[None, :]).astype(jnp.int32)
    ranked = jnp.cumsum(onehot, 0, dtype=jnp.int32) - onehot
    start = jnp.sum(onehot * filled[None, :], 1, dtype=jnp.int32)
    within = jnp.sum(onehot * ranked, 1, dtype=jnp.int32)
    target = jnp.where(tagged >= 0, tagged * slots + start + within, cell_total * slots)
    placed = jax.ops.segment_sum(arrivals[:6].T, target, num_segments=cell_total * slots + 1)[
        : cell_total * slots
    ].T
    slot_index = jnp.arange(slots, dtype=jnp.int32)
    kept = (slot_index[None, :] < filled[:, None]).reshape(cell_total * slots)
    merged = jnp.where(kept[None, :], flat_state, placed)
    grown = filled + jnp.sum(onehot, 0, dtype=jnp.int32)
    return (merged.reshape(particle_state.shape), grown.reshape(counts.shape))


def on_device(
    positions,
    velocities,
    pressure_prev,
    counts,
    out_positions,
    out_velocities,
    out_dir,
    out_cell,
    out_count,
):
    cargo = payloads(out_positions, out_velocities, out_dir, out_cell, out_count)
    received = []
    for offset_sign, heading in ((1, 0), (-1, 1)):
        received.append(passed_along(cargo[heading], GX, offset_sign))
    for offset_sign, heading in ((1, 2), (-1, 3)):
        received.append(passed_along(cargo[heading], "gy", offset_sign))
    for offset_sign, heading in ((1, 4), (-1, 5)):
        received.append(passed_along(cargo[heading], GZ, offset_sign))
    arrivals = jnp.concatenate(received, -1).reshape(7, -1)
    particle_state, new_counts = insert(
        jnp.concatenate([positions, velocities], 0), counts, arrivals
    )
    slot_index = jnp.arange(positions.shape[-1], dtype=jnp.int32)
    occupied = slot_index < new_counts[..., None]
    was_there = slot_index < counts[..., None]
    masses = jnp.where(occupied, particle_mass, 0.0).astype(jnp.float32)[None]
    local_state = jnp.concatenate([particle_state, masses], 0)
    local_pos = particle_state[0:3]
    local_vel = particle_state[3:6]
    near_state = with_halo(local_state, ((GX, 1), ("gy", 2), (GZ, 3)), 1)
    near_pos = near_state[0:3]
    near_mass = near_state[6:7]
    summary = setup_pass(local_pos, local_vel, near_pos, near_state[3:6], near_mass)
    density, divergence, grad_square = (summary[0], summary[1], summary[5])
    safe = jnp.where(occupied, density, 1.0)
    source = jnp.where(occupied, rest_density - (density + time_step * divergence), 0.0)
    grad_norm = summary[2] * summary[2] + summary[3] * summary[3] + summary[4] * summary[4]
    diagonal = jnp.maximum(
        time_step * time_step * (grad_norm + masses[0] * grad_square) / (safe * safe), floor_value
    )
    pressure = jnp.where(was_there, pressure_prev, 0.0)
    total_slots = (
        positions.shape[1]
        * positions.shape[2]
        * positions.shape[3]
        * positions.shape[4]
        * lax.axis_size(GX)
        * lax.axis_size("gy")
        * lax.axis_size(GZ)
    )
    errors = []
    for _ in range(ITERS):
        scaled = jnp.where(occupied, pressure / (safe * safe), 0.0)[None]
        scaled_near = with_halo(scaled, ((GX, 1), ("gy", 2), (GZ, 3)), 1)
        accel_local = accel_pass(local_pos, scaled, near_pos, near_mass, scaled_near)
        accel_near = with_halo(accel_local, ((GX, 1), ("gy", 2), (GZ, 3)), 1)
        applied = apply_pass(local_pos, accel_local, near_pos, near_mass, accel_near)[0]
        residual = jnp.where(occupied, source - applied, 0.0)
        share_error = jnp.sum(jnp.abs(residual)) / total_slots
        errors.append(share_error)
        pressure = jnp.where(
            occupied, jnp.maximum(pressure + relaxation * (applied - source) / diagonal, 0.0), 0.0
        )
    density_error = one_axis_at_a_time(jnp.stack(errors), GX_GY_GZ)
    scaled = jnp.where(occupied, pressure / (safe * safe), 0.0)[None]
    scaled_near = with_halo(scaled, ((GX, 1), ("gy", 2), (GZ, 3)), 1)
    accel = accel_pass(local_pos, scaled, near_pos, near_mass, scaled_near)
    pulled = accel + jnp.array([0.0, 0.0, -gravity], jnp.float32)[:, None, None, None, None]
    velocity_new = jnp.where(occupied[None], local_vel + time_step * pulled, 0.0)
    return (pressure, velocity_new, density_error)


def solution(mesh):
    torus = Mesh(
        mesh.devices.reshape(8, 2, mesh.shape["gy"], 2, 2), ("gx_0", "gx_1", "gy", "gz_0", "gz_1")
    )
    in_specs = (
        P(None, GX, "gy", GZ, None),
        P(None, GX, "gy", GZ, None),
        P(GX, "gy", GZ, None),
        P(GX, "gy", GZ),
        P(None, GX, "gy", GZ, None),
        P(None, GX, "gy", GZ, None),
        P(GX, "gy", GZ, None),
        P(GX, "gy", GZ, None),
        P(GX, "gy", GZ),
    )
    out_specs = (P(GX, "gy", GZ, None), P(None, GX, "gy", GZ, None), P())
    return jax.shard_map(
        on_device, mesh=torus, in_specs=in_specs, out_specs=out_specs, check_vma=False
    )
```

profile of v0, /device:TPU:1, one launch (start us, length us, event | category | flops | bytes accessed | tf_op | source)
XLA Modules:
  0.0 420.0 jit_solution(3058559179890980939)
XLA Ops:
  2.7 5.1 %collective-permute-start.5 = (f32[7,1,1,1,128]{4,3,2,1,0:T(1,128)S(1)}, f32[7,1,1,1,128]{4,3,2,1,0:T(1,128)S(1)}, u32[]{:S(2)}, u32[]{:S(2)}) collective-permute-start(f32[7,1,1,1,128]{4,3,2,1,0:T(1,128)S(1)} %get-tuple-element.569), channel_id=1, source_target_pairs={{1,0},{2,1},{3,2},{5,4},{6,5},{7,6},{9,8},{10,9},{11,10},{13,12},{... | collective-permute-start | bytes 10760 | tf_op jit(solution)/shard_map/ppermute | solution.py:25
  7.8 3.0 collective-permute-start.4
  12.1 4.0 collective-permute-start.2
  16.1 3.0 collective-permute-start
  21.1 3.4 collective-permute-done.1
  27.5 7.1 %scatter_custom_fusion = f32[1025,6]{1,0:T(8,128)S(1)} fusion(s32[768]{0:T(1024)S(1)} %fusion.171, f32[6,1,1,1,768]{0,4,1,2,3:T(8,128)S(1)} %copy.31, f32[]{:T(128)} %constant.125.clone.1), kind=kCustom, calls=%fused_computation.810 | custom fusion | flops 4608 | bytes 417820 | tf_op jit(solution)/shard_map/scatter-add | solution.py:151
  35.0 4.6 %collective-permute-start.6 = (f32[7,1,2,2,128]{4,3,2,1,0:T(2,128)S(1)}, f32[7,1,2,2,128]{4,3,2,1,0:T(2,128)S(1)}, u32[]{:S(2)}, u32[]{:S(2)}) collective-permute-start(f32[7,1,2,2,128]{4,3,2,1,0:T(2,128)S(1)} %get-tuple-element.967), channel_id=1, source_target_pairs={{0,16},{16,32},{32,48},{48,64},{64,80},{80,96},{96,112},{112,128},... | collective-permute-start | bytes 43016 | tf_op jit(solution)/shard_map/ppermute | solution.py:33
  44.1 3.0 collective-permute-start.8
  48.5 3.2 collective-permute-done.9
  51.9 5.1 %collective-permute-start.11 = (f32[7,4,4,1,128]{4,3,2,1,0:T(1,128)S(1)}, f32[7,4,4,1,128]{4,3,2,1,0:T(1,128)S(1)}, u32[]{:S(2)}, u32[]{:S(2)}) collective-permute-start(f32[7,4,4,1,128]{4,3,2,1,0:T(1,128)S(1)} %get-tuple-element.699), channel_id=1, source_target_pairs={{1,0},{2,1},{3,2},{5,4},{6,5},{7,6},{9,8},{10,9},{11,10},{13,12},{... | collective-permute-start | bytes 172040 | tf_op jit(solution)/shard_map/ppermute | solution.py:36
  57.0 4.9 %collective-permute-start.10 = (f32[7,4,4,1,128]{4,3,2,1,0:T(1,128)S(1)}, f32[7,4,4,1,128]{4,3,2,1,0:T(1,128)S(1)}, u32[]{:S(2)}, u32[]{:S(2)}) collective-permute-start(f32[7,4,4,1,128]{4,3,2,1,0:T(1,128)S(1)} %get-tuple-element.700), channel_id=1, source_target_pairs={{0,1},{1,2},{2,3},{4,5},{5,6},{6,7},{8,9},{9,10},{10,11},{12,13},{... | collective-permute-start | bytes 172040 | tf_op jit(solution)/shard_map/ppermute | solution.py:33
  75.3 3.9 collective-permute-start.12
  80.5 3.0 collective-permute-done.13
  83.5 3.2 collective-permute-start.14
  91.7 8.7 %collective-permute-start.16 = (f32[1,4,4,1,128]{4,3,2,1,0:T(1,128)S(1)}, f32[1,4,4,1,128]{4,3,2,1,0:T(1,128)S(1)}, u32[]{:S(2)}, u32[]{:S(2)}) collective-permute-start(f32[1,4,4,1,128]{4,3,2,1,0:T(1,128)S(1)} %get-tuple-element.999), channel_id=1, source_target_pairs={{0,1},{1,2},{2,3},{4,5},{5,6},{6,7},{8,9},{9,10},{10,11},{12,13},{... | collective-permute-start | bytes 24584 | tf_op jit(solution)/shard_map/ppermute | solution.py:33
  149.6 3.8 collective-permute-done.19
  154.7 4.3 %collective-permute-start.20 = (f32[3,4,1,2,128]{4,3,2,1,0:T(2,128)S(1)}, f32[3,4,1,2,128]{4,3,2,1,0:T(2,128)S(1)}, u32[]{:S(2)}, u32[]{:S(2)}) collective-permute-start(f32[3,4,1,2,128]{4,3,2,1,0:T(2,128)S(1)} %get-tuple-element.976), channel_id=1, source_target_pairs={{0,4},{4,8},{8,12},{1,5},{5,9},{9,13},{2,6},{6,10},{10,14},{3,7},{... | collective-permute-start | bytes 36872 | tf_op jit(solution)/shard_map/ppermute | solution.py:33
  164.6 6.7 %collective-permute-start.22 = (f32[3,4,4,1,128]{4,3,2,1,0:T(1,128)S(1)}, f32[3,4,4,1,128]{4,3,2,1,0:T(1,128)S(1)}, u32[]{:S(2)}, u32[]{:S(2)}) collective-permute-start(f32[3,4,4,1,128]{4,3,2,1,0:T(1,128)S(1)} %get-tuple-element.862), channel_id=1, source_target_pairs={{0,1},{1,2},{2,3},{4,5},{5,6},{6,7},{8,9},{9,10},{10,11},{12,13},{... | collective-permute-start | bytes 73736 | tf_op jit(solution)/shard_map/ppermute | solution.py:33
  178.9 3.3 multiply_reduce_fusion.349
  217.6 3.8 collective-permute-start.24
  222.7 3.0 collective-permute-done.25
  225.7 3.6 collective-permute-start.26
  230.7 3.0 collective-permute-done.27
  235.7 5.8 %collective-permute-start.28 = (f32[1,4,4,1,128]{4,3,2,1,0:T(1,128)S(1)}, f32[1,4,4,1,128]{4,3,2,1,0:T(1,128)S(1)}, u32[]{:S(2)}, u32[]{:S(2)}) collective-permute-start(f32[1,4,4,1,128]{4,3,2,1,0:T(1,128)S(1)} %get-tuple-element.996), channel_id=1, source_target_pairs={{0,1},{1,2},{2,3},{4,5},{5,6},{6,7},{8,9},{9,10},{10,11},{12,13},{... | collective-permute-start | bytes 24584 | tf_op jit(solution)/shard_map/ppermute | solution.py:33
  242.4 3.1 multiply_reduce_fusion.175
  248.4 2.9 multiply_reduce_fusion.164
  251.3 2.9 multiply_reduce_fusion.167
  257.1 2.9 multiply_reduce_fusion.179
  265.8 2.9 multiply_reduce_fusion.176
  268.9 4.4 %collective-permute-start.30 = (f32[3,1,2,2,128]{4,3,2,1,0:T(2,128)S(1)}, f32[3,1,2,2,128]{4,3,2,1,0:T(2,128)S(1)}, u32[]{:S(2)}, u32[]{:S(2)}) collective-permute-start(f32[3,1,2,2,128]{4,3,2,1,0:T(2,128)S(1)} %get-tuple-element.1013), channel_id=1, source_target_pairs={{0,16},{16,32},{32,48},{48,64},{64,80},{80,96},{96,112},{112,128},... | collective-permute-start | bytes 18440 | tf_op jit(solution)/shard_map/ppermute | solution.py:33
  274.7 4.0 collective-permute-done.31
  285.1 8.3 %collective-permute-start.34 = (f32[3,4,4,1,128]{4,3,2,1,0:T(1,128)S(1)}, f32[3,4,4,1,128]{4,3,2,1,0:T(1,128)S(1)}, u32[]{:S(2)}, u32[]{:S(2)}) collective-permute-start(f32[3,4,4,1,128]{4,3,2,1,0:T(1,128)S(1)} %get-tuple-element.857), channel_id=1, source_target_pairs={{0,1},{1,2},{2,3},{4,5},{5,6},{6,7},{8,9},{9,10},{10,11},{12,13},{... | collective-permute-start | bytes 73736 | tf_op jit(solution)/shard_map/ppermute | solution.py:33
  327.4 15.5 %psum.35 = f32[2]{0:T(128)S(1)} all-reduce(f32[2]{0:T(128)S(1)} %pad_maximum_fusion.47), channel_id=1, replica_groups=mesh['gx_0'=8,'gx_1'=2,'gy'=4,'gz_0'=2,'gz_1'=2] {'gx_0'}, use_global_device_ids=true, to_apply=%region_467.468 | all-reduce | flops 2 | bytes 16 | tf_op jit(solution)/shard_map/psum | solution.py:43
  342.9 3.8 psum.36
  351.6 6.8 %psum.37 = f32[2]{0:T(128)S(1)} all-reduce(f32[2]{0:T(128)S(1)} %psum.36), channel_id=1, replica_groups=mesh['gx_0'=8,'gx_1'=2,'gy'=4,'gz_0'=2,'gz_1'=2] {'gy'}, use_global_device_ids=true, to_apply=%region_469.470 | all-reduce | flops 2 | bytes 16 | tf_op jit(solution)/shard_map/psum | solution.py:43
  358.6 5.3 %psum.38 = f32[2]{0:T(128)S(1)} all-reduce(f32[2]{0:T(128)S(1)} %psum.37), channel_id=1, replica_groups=mesh['gx_0'=8,'gx_1'=2,'gy'=4,'gz_0'=2,'gz_1'=2] {'gz_0'}, use_global_device_ids=true, to_apply=%region_470.471 | all-reduce | flops 2 | bytes 16 | tf_op jit(solution)/shard_map/psum | solution.py:43
  364.0 11.4 %psum.39 = f32[2]{0:T(128)} all-reduce(f32[2]{0:T(128)S(1)} %psum.38), channel_id=1, replica_groups=mesh['gx_0'=8,'gx_1'=2,'gy'=4,'gz_0'=2,'gz_1'=2] {'gz_1'}, use_global_device_ids=true, to_apply=%region_471.472 | all-reduce | flops 2 | bytes 16 | tf_op jit(solution)/shard_map/psum | solution.py:43
  379.6 3.0 collective-permute-done.39
  382.7 3.7 collective-permute-start.41
  386.4 5.1 %collective-permute-start.40 = (f32[1,4,4,1,128]{4,3,2,1,0:T(1,128)S(1)}, f32[1,4,4,1,128]{4,3,2,1,0:T(1,128)S(1)}, u32[]{:S(2)}, u32[]{:S(2)}) collective-permute-start(f32[1,4,4,1,128]{4,3,2,1,0:T(1,128)S(1)} %get-tuple-element.992), channel_id=1, source_target_pairs={{0,1},{1,2},{2,3},{4,5},{5,6},{6,7},{8,9},{9,10},{10,11},{12,13},{... | collective-permute-start | bytes 24584 | tf_op jit(solution)/shard_map/ppermute | solution.py:33
  392.3 2.9 multiply_reduce_fusion.67
  398.1 2.9 multiply_reduce_fusion.74
  401.0 2.9 multiply_reduce_fusion.71
  403.9 2.9 multiply_reduce_fusion.68
  406.8 2.9 multiply_reduce_fusion.62
  409.7 2.9 multiply_reduce_fusion.59
  412.6 2.9 multiply_reduce_fusion.79
  415.5 2.9 multiply_reduce_fusion.56
  (298 shorter events, 203.7 us)
Async XLA Ops:
  1.9 0.7 copy-start.5
  2.0 0.7 copy-start.4
  2.7 22.0 %collective-permute-start.5 = (f32[7,1,1,1,128]{4,3,2,1,0:T(1,128)S(1)}, f32[7,1,1,1,128]{4,3,2,1,0:T(1,128)S(1)}, u32[]{:S(2)}, u32[]{:S(2)}) collective-permute-start(f32[7,1,1,1,128]{4,3,2,1,0:T(1,128)S(1)} %get-tuple-element.569), channel_id=1, source_target_pairs={{1,0},{2,1},{3,2},{5,4},{6,5},{7,6},{9,8},{10,9},{11,10},{13,12},{... | collective-permute-start | bytes 10760 | tf_op jit(solution)/shard_map/ppermute | solution.py:25
  7.8 11.5 %copy-start.2 = (f32[3,2,2,2,128]{4,3,2,1,0:T(2,128)S(1)}, f32[3,2,2,2,128]{4,3,2,1,0:T(2,128)}, u32[]{:S(2)}) copy-start(f32[3,2,2,2,128]{4,3,2,1,0:T(2,128)} %param.11) | copy-start | bytes 36868
  7.8 11.5 %copy-start.3 = (f32[3,2,2,2,128]{4,3,2,1,0:T(2,128)S(1)}, f32[3,2,2,2,128]{4,3,2,1,0:T(2,128)}, u32[]{:S(2)}) copy-start(f32[3,2,2,2,128]{4,3,2,1,0:T(2,128)} %param.10) | copy-start | bytes 36868
  7.8 16.8 %collective-permute-start.4 = (f32[7,1,1,1,128]{4,3,2,1,0:T(1,128)S(1)}, f32[7,1,1,1,128]{4,3,2,1,0:T(1,128)S(1)}, u32[]{:S(2)}, u32[]{:S(2)}) collective-permute-start(f32[7,1,1,1,128]{4,3,2,1,0:T(1,128)S(1)} %get-tuple-element.1059), channel_id=1, source_target_pairs={{0,1},{1,2},{2,3},{4,5},{5,6},{6,7},{8,9},{9,10},{10,11},{12,13},{... | collective-permute-start | bytes 10760 | tf_op jit(solution)/shard_map/ppermute | solution.py:25
  10.8 8.3 %copy-start = (s32[2,2,2]{2,1,0:T(2,128)S(1)}, s32[2,2,2]{2,1,0:T(2,128)}, u32[]{:S(2)}) copy-start(s32[2,2,2]{2,1,0:T(2,128)} %param.13) | copy-start | bytes 100
  10.8 13.7 %collective-permute-start.3 = (f32[7,1,1,1,128]{4,3,2,1,0:T(1,128)S(1)}, f32[7,1,1,1,128]{4,3,2,1,0:T(1,128)S(1)}, u32[]{:S(2)}, u32[]{:S(2)}) collective-permute-start(f32[7,1,1,1,128]{4,3,2,1,0:T(1,128)S(1)} %get-tuple-element.1060), channel_id=1, source_target_pairs={{4,0},{8,4},{12,8},{5,1},{9,5},{13,9},{6,2},{10,6},{14,10},{7,3},{... | collective-permute-start | bytes 10760 | tf_op jit(solution)/shard_map/ppermute | solution.py:25
  12.1 12.4 %collective-permute-start.2 = (f32[7,1,1,1,128]{4,3,2,1,0:T(1,128)S(1)}, f32[7,1,1,1,128]{4,3,2,1,0:T(1,128)S(1)}, u32[]{:S(2)}, u32[]{:S(2)}) collective-permute-start(f32[7,1,1,1,128]{4,3,2,1,0:T(1,128)S(1)} %get-tuple-element.1061), channel_id=1, source_target_pairs={{0,4},{4,8},{8,12},{1,5},{5,9},{9,13},{2,6},{6,10},{10,14},{3,7},{... | collective-permute-start | bytes 10760 | tf_op jit(solution)/shard_map/ppermute | solution.py:25
  16.1 3.7 collective-permute-start
  19.8 4.7 %collective-permute-start.1 = (f32[7,1,1,1,128]{4,3,2,1,0:T(1,128)S(1)}, f32[7,1,1,1,128]{4,3,2,1,0:T(1,128)S(1)}, u32[]{:S(2)}, u32[]{:S(2)}) collective-permute-start(f32[7,1,1,1,128]{4,3,2,1,0:T(1,128)S(1)} %get-tuple-element.1062), channel_id=1, source_target_pairs={{16,0},{32,16},{48,32},{64,48},{80,64},{96,80},{112,96},{128,112},... | collective-permute-start | bytes 10760 | tf_op jit(solution)/shard_map/ppermute | solution.py:25
  35.0 7.5 %collective-permute-start.6 = (f32[7,1,2,2,128]{4,3,2,1,0:T(2,128)S(1)}, f32[7,1,2,2,128]{4,3,2,1,0:T(2,128)S(1)}, u32[]{:S(2)}, u32[]{:S(2)}) collective-permute-start(f32[7,1,2,2,128]{4,3,2,1,0:T(2,128)S(1)} %get-tuple-element.967), channel_id=1, source_target_pairs={{0,16},{16,32},{32,48},{48,64},{64,80},{80,96},{96,112},{112,128},... | collective-permute-start | bytes 43016 | tf_op jit(solution)/shard_map/ppermute | solution.py:33
  39.6 4.5 %collective-permute-start.7 = (f32[7,1,2,2,128]{4,3,2,1,0:T(2,128)S(1)}, f32[7,1,2,2,128]{4,3,2,1,0:T(2,128)S(1)}, u32[]{:S(2)}, u32[]{:S(2)}) collective-permute-start(f32[7,1,2,2,128]{4,3,2,1,0:T(2,128)S(1)} %get-tuple-element.968), channel_id=1, source_target_pairs={{16,0},{32,16},{48,32},{64,48},{80,64},{96,80},{112,96},{128,112},... | collective-permute-start | bytes 43016 | tf_op jit(solution)/shard_map/ppermute | solution.py:36
  44.1 4.4 %collective-permute-start.8 = (f32[7,4,1,2,128]{4,3,2,1,0:T(2,128)S(1)}, f32[7,4,1,2,128]{4,3,2,1,0:T(2,128)S(1)}, u32[]{:S(2)}, u32[]{:S(2)}) collective-permute-start(f32[7,4,1,2,128]{4,3,2,1,0:T(2,128)S(1)} %get-tuple-element.853), channel_id=1, source_target_pairs={{0,4},{4,8},{8,12},{1,5},{5,9},{9,13},{2,6},{6,10},{10,14},{3,7},{... | collective-permute-start | bytes 86024 | tf_op jit(solution)/shard_map/ppermute | solution.py:33
  47.2 4.6 %collective-permute-start.9 = (f32[7,4,1,2,128]{4,3,2,1,0:T(2,128)S(1)}, f32[7,4,1,2,128]{4,3,2,1,0:T(2,128)S(1)}, u32[]{:S(2)}, u32[]{:S(2)}) collective-permute-start(f32[7,4,1,2,128]{4,3,2,1,0:T(2,128)S(1)} %get-tuple-element.854), channel_id=1, source_target_pairs={{4,0},{8,4},{12,8},{5,1},{9,5},{13,9},{6,2},{10,6},{14,10},{7,3},{... | collective-permute-start | bytes 86024 | tf_op jit(solution)/shard_map/ppermute | solution.py:36
  51.9 10.1 %collective-permute-start.11 = (f32[7,4,4,1,128]{4,3,2,1,0:T(1,128)S(1)}, f32[7,4,4,1,128]{4,3,2,1,0:T(1,128)S(1)}, u32[]{:S(2)}, u32[]{:S(2)}) collective-permute-start(f32[7,4,4,1,128]{4,3,2,1,0:T(1,128)S(1)} %get-tuple-element.699), channel_id=1, source_target_pairs={{1,0},{2,1},{3,2},{5,4},{6,5},{7,6},{9,8},{10,9},{11,10},{13,12},{... | collective-permute-start | bytes 172040 | tf_op jit(solution)/shard_map/ppermute | solution.py:36
  57.0 5.7 %collective-permute-start.10 = (f32[7,4,4,1,128]{4,3,2,1,0:T(1,128)S(1)}, f32[7,4,4,1,128]{4,3,2,1,0:T(1,128)S(1)}, u32[]{:S(2)}, u32[]{:S(2)}) collective-permute-start(f32[7,4,4,1,128]{4,3,2,1,0:T(1,128)S(1)} %get-tuple-element.700), channel_id=1, source_target_pairs={{0,1},{1,2},{2,3},{4,5},{5,6},{6,7},{8,9},{9,10},{10,11},{12,13},{... | collective-permute-start | bytes 172040 | tf_op jit(solution)/shard_map/ppermute | solution.py:33
  74.5 0.7 copy-start.1
  75.3 5.2 %collective-permute-start.12 = (f32[1,1,2,2,128]{4,3,2,1,0:T(2,128)S(1)}, f32[1,1,2,2,128]{4,3,2,1,0:T(2,128)S(1)}, u32[]{:S(2)}, u32[]{:S(2)}) collective-permute-start(f32[1,1,2,2,128]{4,3,2,1,0:T(2,128)S(1)} %get-tuple-element.1057), channel_id=1, source_target_pairs={{0,16},{16,32},{32,48},{48,64},{64,80},{80,96},{96,112},{112,128},... | collective-permute-start | bytes 6152 | tf_op jit(solution)/shard_map/ppermute | solution.py:33
  79.2 4.3 %collective-permute-start.13 = (f32[1,1,2,2,128]{4,3,2,1,0:T(2,128)S(1)}, f32[1,1,2,2,128]{4,3,2,1,0:T(2,128)S(1)}, u32[]{:S(2)}, u32[]{:S(2)}) collective-permute-start(f32[1,1,2,2,128]{4,3,2,1,0:T(2,128)S(1)} %get-tuple-element.1058), channel_id=1, source_target_pairs={{16,0},{32,16},{48,32},{64,48},{80,64},{96,80},{112,96},{128,112},... | collective-permute-start | bytes 6152 | tf_op jit(solution)/shard_map/ppermute | solution.py:36
  83.5 8.1 %collective-permute-start.14 = (f32[1,4,1,2,128]{4,3,2,1,0:T(2,128)S(1)}, f32[1,4,1,2,128]{4,3,2,1,0:T(2,128)S(1)}, u32[]{:S(2)}, u32[]{:S(2)}) collective-permute-start(f32[1,4,1,2,128]{4,3,2,1,0:T(2,128)S(1)} %get-tuple-element.1045), channel_id=1, source_target_pairs={{0,4},{4,8},{8,12},{1,5},{5,9},{9,13},{2,6},{6,10},{10,14},{3,7},{... | collective-permute-start | bytes 12296 | tf_op jit(solution)/shard_map/ppermute | solution.py:33
  86.8 4.9 %collective-permute-start.15 = (f32[1,4,1,2,128]{4,3,2,1,0:T(2,128)S(1)}, f32[1,4,1,2,128]{4,3,2,1,0:T(2,128)S(1)}, u32[]{:S(2)}, u32[]{:S(2)}) collective-permute-start(f32[1,4,1,2,128]{4,3,2,1,0:T(2,128)S(1)} %get-tuple-element.1046), channel_id=1, source_target_pairs={{4,0},{8,4},{12,8},{5,1},{9,5},{13,9},{6,2},{10,6},{14,10},{7,3},{... | collective-permute-start | bytes 12296 | tf_op jit(solution)/shard_map/ppermute | solution.py:36
  91.7 21.5 %collective-permute-start.16 = (f32[1,4,4,1,128]{4,3,2,1,0:T(1,128)S(1)}, f32[1,4,4,1,128]{4,3,2,1,0:T(1,128)S(1)}, u32[]{:S(2)}, u32[]{:S(2)}) collective-permute-start(f32[1,4,4,1,128]{4,3,2,1,0:T(1,128)S(1)} %get-tuple-element.999), channel_id=1, source_target_pairs={{0,1},{1,2},{2,3},{4,5},{5,6},{6,7},{8,9},{9,10},{10,11},{12,13},{... | collective-permute-start | bytes 24584 | tf_op jit(solution)/shard_map/ppermute | solution.py:33
  100.4 12.8 %collective-permute-start.17 = (f32[1,4,4,1,128]{4,3,2,1,0:T(1,128)S(1)}, f32[1,4,4,1,128]{4,3,2,1,0:T(1,128)S(1)}, u32[]{:S(2)}, u32[]{:S(2)}) collective-permute-start(f32[1,4,4,1,128]{4,3,2,1,0:T(1,128)S(1)} %get-tuple-element.1000), channel_id=1, source_target_pairs={{1,0},{2,1},{3,2},{5,4},{6,5},{7,6},{9,8},{10,9},{11,10},{13,12},{... | collective-permute-start | bytes 24584 | tf_op jit(solution)/shard_map/ppermute | solution.py:36
  145.7 3.9 collective-permute-start.18
  148.3 5.1 %collective-permute-start.19 = (f32[3,1,2,2,128]{4,3,2,1,0:T(2,128)S(1)}, f32[3,1,2,2,128]{4,3,2,1,0:T(2,128)S(1)}, u32[]{:S(2)}, u32[]{:S(2)}) collective-permute-start(f32[3,1,2,2,128]{4,3,2,1,0:T(2,128)S(1)} %get-tuple-element.1028), channel_id=1, source_target_pairs={{16,0},{32,16},{48,32},{64,48},{80,64},{96,80},{112,96},{128,112},... | collective-permute-start | bytes 18440 | tf_op jit(solution)/shard_map/ppermute | solution.py:36
  153.4 9.2 %collective-permute-start.21 = (f32[3,4,1,2,128]{4,3,2,1,0:T(2,128)S(1)}, f32[3,4,1,2,128]{4,3,2,1,0:T(2,128)S(1)}, u32[]{:S(2)}, u32[]{:S(2)}) collective-permute-start(f32[3,4,1,2,128]{4,3,2,1,0:T(2,128)S(1)} %get-tuple-element.975), channel_id=1, source_target_pairs={{4,0},{8,4},{12,8},{5,1},{9,5},{13,9},{6,2},{10,6},{14,10},{7,3},{... | collective-permute-start | bytes 36872 | tf_op jit(solution)/shard_map/ppermute | solution.py:36
  154.7 7.9 %collective-permute-start.20 = (f32[3,4,1,2,128]{4,3,2,1,0:T(2,128)S(1)}, f32[3,4,1,2,128]{4,3,2,1,0:T(2,128)S(1)}, u32[]{:S(2)}, u32[]{:S(2)}) collective-permute-start(f32[3,4,1,2,128]{4,3,2,1,0:T(2,128)S(1)} %get-tuple-element.976), channel_id=1, source_target_pairs={{0,4},{4,8},{8,12},{1,5},{5,9},{9,13},{2,6},{6,10},{10,14},{3,7},{... | collective-permute-start | bytes 36872 | tf_op jit(solution)/shard_map/ppermute | solution.py:33
  162.7 21.3 %collective-permute-start.23 = (f32[3,4,4,1,128]{4,3,2,1,0:T(1,128)S(1)}, f32[3,4,4,1,128]{4,3,2,1,0:T(1,128)S(1)}, u32[]{:S(2)}, u32[]{:S(2)}) collective-permute-start(f32[3,4,4,1,128]{4,3,2,1,0:T(1,128)S(1)} %get-tuple-element.861), channel_id=1, source_target_pairs={{1,0},{2,1},{3,2},{5,4},{6,5},{7,6},{9,8},{10,9},{11,10},{13,12},{... | collective-permute-start | bytes 73736 | tf_op jit(solution)/shard_map/ppermute | solution.py:36
  164.6 19.4 %collective-permute-start.22 = (f32[3,4,4,1,128]{4,3,2,1,0:T(1,128)S(1)}, f32[3,4,4,1,128]{4,3,2,1,0:T(1,128)S(1)}, u32[]{:S(2)}, u32[]{:S(2)}) collective-permute-start(f32[3,4,4,1,128]{4,3,2,1,0:T(1,128)S(1)} %get-tuple-element.862), channel_id=1, source_target_pairs={{0,1},{1,2},{2,3},{4,5},{5,6},{6,7},{8,9},{9,10},{10,11},{12,13},{... | collective-permute-start | bytes 73736 | tf_op jit(solution)/shard_map/ppermute | solution.py:33
  217.6 5.1 %collective-permute-start.24 = (f32[1,1,2,2,128]{4,3,2,1,0:T(2,128)S(1)}, f32[1,1,2,2,128]{4,3,2,1,0:T(2,128)S(1)}, u32[]{:S(2)}, u32[]{:S(2)}) collective-permute-start(f32[1,1,2,2,128]{4,3,2,1,0:T(2,128)S(1)} %get-tuple-element.1053), channel_id=1, source_target_pairs={{0,16},{16,32},{32,48},{48,64},{64,80},{80,96},{96,112},{112,128},... | collective-permute-start | bytes 6152 | tf_op jit(solution)/shard_map/ppermute | solution.py:33
  221.4 4.4 %collective-permute-start.25 = (f32[1,1,2,2,128]{4,3,2,1,0:T(2,128)S(1)}, f32[1,1,2,2,128]{4,3,2,1,0:T(2,128)S(1)}, u32[]{:S(2)}, u32[]{:S(2)}) collective-permute-start(f32[1,1,2,2,128]{4,3,2,1,0:T(2,128)S(1)} %get-tuple-element.1054), channel_id=1, source_target_pairs={{16,0},{32,16},{48,32},{64,48},{80,64},{96,80},{112,96},{128,112},... | collective-permute-start | bytes 6152 | tf_op jit(solution)/shard_map/ppermute | solution.py:36
  225.7 5.0 %collective-permute-start.26 = (f32[1,4,1,2,128]{4,3,2,1,0:T(2,128)S(1)}, f32[1,4,1,2,128]{4,3,2,1,0:T(2,128)S(1)}, u32[]{:S(2)}, u32[]{:S(2)}) collective-permute-start(f32[1,4,1,2,128]{4,3,2,1,0:T(2,128)S(1)} %get-tuple-element.1041), channel_id=1, source_target_pairs={{0,4},{4,8},{8,12},{1,5},{5,9},{9,13},{2,6},{6,10},{10,14},{3,7},{... | collective-permute-start | bytes 12296 | tf_op jit(solution)/shard_map/ppermute | solution.py:33
  229.4 4.4 %collective-permute-start.27 = (f32[1,4,1,2,128]{4,3,2,1,0:T(2,128)S(1)}, f32[1,4,1,2,128]{4,3,2,1,0:T(2,128)S(1)}, u32[]{:S(2)}, u32[]{:S(2)}) collective-permute-start(f32[1,4,1,2,128]{4,3,2,1,0:T(2,128)S(1)} %get-tuple-element.1042), channel_id=1, source_target_pairs={{4,0},{8,4},{12,8},{5,1},{9,5},{13,9},{6,2},{10,6},{14,10},{7,3},{... | collective-permute-start | bytes 12296 | tf_op jit(solution)/shard_map/ppermute | solution.py:36
  233.8 7.8 %collective-permute-start.29 = (f32[1,4,4,1,128]{4,3,2,1,0:T(1,128)S(1)}, f32[1,4,4,1,128]{4,3,2,1,0:T(1,128)S(1)}, u32[]{:S(2)}, u32[]{:S(2)}) collective-permute-start(f32[1,4,4,1,128]{4,3,2,1,0:T(1,128)S(1)} %get-tuple-element.995), channel_id=1, source_target_pairs={{1,0},{2,1},{3,2},{5,4},{6,5},{7,6},{9,8},{10,9},{11,10},{13,12},{... | collective-permute-start | bytes 24584 | tf_op jit(solution)/shard_map/ppermute | solution.py:36
  235.7 6.6 %collective-permute-start.28 = (f32[1,4,4,1,128]{4,3,2,1,0:T(1,128)S(1)}, f32[1,4,4,1,128]{4,3,2,1,0:T(1,128)S(1)}, u32[]{:S(2)}, u32[]{:S(2)}) collective-permute-start(f32[1,4,4,1,128]{4,3,2,1,0:T(1,128)S(1)} %get-tuple-element.996), channel_id=1, source_target_pairs={{0,1},{1,2},{2,3},{4,5},{5,6},{6,7},{8,9},{9,10},{10,11},{12,13},{... | collective-permute-start | bytes 24584 | tf_op jit(solution)/shard_map/ppermute | solution.py:33
  268.9 5.8 %collective-permute-start.30 = (f32[3,1,2,2,128]{4,3,2,1,0:T(2,128)S(1)}, f32[3,1,2,2,128]{4,3,2,1,0:T(2,128)S(1)}, u32[]{:S(2)}, u32[]{:S(2)}) collective-permute-start(f32[3,1,2,2,128]{4,3,2,1,0:T(2,128)S(1)} %get-tuple-element.1013), channel_id=1, source_target_pairs={{0,16},{16,32},{32,48},{48,64},{64,80},{80,96},{96,112},{112,128},... | collective-permute-start | bytes 18440 | tf_op jit(solution)/shard_map/ppermute | solution.py:33
  273.4 5.3 %collective-permute-start.31 = (f32[3,1,2,2,128]{4,3,2,1,0:T(2,128)S(1)}, f32[3,1,2,2,128]{4,3,2,1,0:T(2,128)S(1)}, u32[]{:S(2)}, u32[]{:S(2)}) collective-permute-start(f32[3,1,2,2,128]{4,3,2,1,0:T(2,128)S(1)} %get-tuple-element.1014), channel_id=1, source_target_pairs={{16,0},{32,16},{48,32},{64,48},{80,64},{96,80},{112,96},{128,112},... | collective-permute-start | bytes 18440 | tf_op jit(solution)/shard_map/ppermute | solution.py:36
  278.6 5.7 %collective-permute-start.32 = (f32[3,4,1,2,128]{4,3,2,1,0:T(2,128)S(1)}, f32[3,4,1,2,128]{4,3,2,1,0:T(2,128)S(1)}, u32[]{:S(2)}, u32[]{:S(2)}) collective-permute-start(f32[3,4,1,2,128]{4,3,2,1,0:T(2,128)S(1)} %get-tuple-element.971), channel_id=1, source_target_pairs={{0,4},{4,8},{8,12},{1,5},{5,9},{9,13},{2,6},{6,10},{10,14},{3,7},{... | collective-permute-start | bytes 36872 | tf_op jit(solution)/shard_map/ppermute | solution.py:33
  280.6 4.4 %collective-permute-start.33 = (f32[3,4,1,2,128]{4,3,2,1,0:T(2,128)S(1)}, f32[3,4,1,2,128]{4,3,2,1,0:T(2,128)S(1)}, u32[]{:S(2)}, u32[]{:S(2)}) collective-permute-start(f32[3,4,1,2,128]{4,3,2,1,0:T(2,128)S(1)} %get-tuple-element.972), channel_id=1, source_target_pairs={{4,0},{8,4},{12,8},{5,1},{9,5},{13,9},{6,2},{10,6},{14,10},{7,3},{... | collective-permute-start | bytes 36872 | tf_op jit(solution)/shard_map/ppermute | solution.py:36
  285.1 18.2 %collective-permute-start.34 = (f32[3,4,4,1,128]{4,3,2,1,0:T(1,128)S(1)}, f32[3,4,4,1,128]{4,3,2,1,0:T(1,128)S(1)}, u32[]{:S(2)}, u32[]{:S(2)}) collective-permute-start(f32[3,4,4,1,128]{4,3,2,1,0:T(1,128)S(1)} %get-tuple-element.857), channel_id=1, source_target_pairs={{0,1},{1,2},{2,3},{4,5},{5,6},{6,7},{8,9},{9,10},{10,11},{12,13},{... | collective-permute-start | bytes 73736 | tf_op jit(solution)/shard_map/ppermute | solution.py:33
  293.4 9.9 %collective-permute-start.35 = (f32[3,4,4,1,128]{4,3,2,1,0:T(1,128)S(1)}, f32[3,4,4,1,128]{4,3,2,1,0:T(1,128)S(1)}, u32[]{:S(2)}, u32[]{:S(2)}) collective-permute-start(f32[3,4,4,1,128]{4,3,2,1,0:T(1,128)S(1)} %get-tuple-element.858), channel_id=1, source_target_pairs={{1,0},{2,1},{3,2},{5,4},{6,5},{7,6},{9,8},{10,9},{11,10},{13,12},{... | collective-permute-start | bytes 73736 | tf_op jit(solution)/shard_map/ppermute | solution.py:36
  347.3 28.1 %collective-permute-start.36 = (f32[1,1,2,2,128]{4,3,2,1,0:T(2,128)S(1)}, f32[1,1,2,2,128]{4,3,2,1,0:T(2,128)S(1)}, u32[]{:S(2)}, u32[]{:S(2)}) collective-permute-start(f32[1,1,2,2,128]{4,3,2,1,0:T(2,128)S(1)} %get-tuple-element.1049), channel_id=1, source_target_pairs={{0,16},{16,32},{32,48},{48,64},{64,80},{80,96},{96,112},{112,128},... | collective-permute-start | bytes 6152 | tf_op jit(solution)/shard_map/ppermute | solution.py:33
  350.2 25.2 %collective-permute-start.37 = (f32[1,1,2,2,128]{4,3,2,1,0:T(2,128)S(1)}, f32[1,1,2,2,128]{4,3,2,1,0:T(2,128)S(1)}, u32[]{:S(2)}, u32[]{:S(2)}) collective-permute-start(f32[1,1,2,2,128]{4,3,2,1,0:T(2,128)S(1)} %get-tuple-element.1050), channel_id=1, source_target_pairs={{16,0},{32,16},{48,32},{64,48},{80,64},{96,80},{112,96},{128,112},... | collective-permute-start | bytes 6152 | tf_op jit(solution)/shard_map/ppermute | solution.py:36
  375.4 4.2 collective-permute-start.38
  378.3 4.4 %collective-permute-start.39 = (f32[1,4,1,2,128]{4,3,2,1,0:T(2,128)S(1)}, f32[1,4,1,2,128]{4,3,2,1,0:T(2,128)S(1)}, u32[]{:S(2)}, u32[]{:S(2)}) collective-permute-start(f32[1,4,1,2,128]{4,3,2,1,0:T(2,128)S(1)} %get-tuple-element.1038), channel_id=1, source_target_pairs={{4,0},{8,4},{12,8},{5,1},{9,5},{13,9},{6,2},{10,6},{14,10},{7,3},{... | collective-permute-start | bytes 12296 | tf_op jit(solution)/shard_map/ppermute | solution.py:36
  382.7 8.8 %collective-permute-start.41 = (f32[1,4,4,1,128]{4,3,2,1,0:T(1,128)S(1)}, f32[1,4,4,1,128]{4,3,2,1,0:T(1,128)S(1)}, u32[]{:S(2)}, u32[]{:S(2)}) collective-permute-start(f32[1,4,4,1,128]{4,3,2,1,0:T(1,128)S(1)} %get-tuple-element.991), channel_id=1, source_target_pairs={{1,0},{2,1},{3,2},{5,4},{6,5},{7,6},{9,8},{10,9},{11,10},{13,12},{... | collective-permute-start | bytes 24584 | tf_op jit(solution)/shard_map/ppermute | solution.py:36
  386.4 5.8 %collective-permute-start.40 = (f32[1,4,4,1,128]{4,3,2,1,0:T(1,128)S(1)}, f32[1,4,4,1,128]{4,3,2,1,0:T(1,128)S(1)}, u32[]{:S(2)}, u32[]{:S(2)}) collective-permute-start(f32[1,4,4,1,128]{4,3,2,1,0:T(1,128)S(1)} %get-tuple-element.992), channel_id=1, source_target_pairs={{0,1},{1,2},{2,3},{4,5},{5,6},{6,7},{8,9},{9,10},{10,11},{12,13},{... | collective-permute-start | bytes 24584 | tf_op jit(solution)/shard_map/ppermute | solution.py:33
  (3 other events, 2.0 us)
where the time goes:
time: 427 us; the launch traced here: 420 us
  other arithmetic  205 us (48%)
  starting transfers between devices  130 us (30%)
  blocking collectives  42.7 us (10%)
  waiting for transfers between devices  31.1 us (7%)
  local copies, waits for them, and re-layouts  6.64 us (2%)
  between operations  4.65 us (1%)
    reduce_sum x44, other arithmetic, accel_pass(): totals = [totals[k] + jnp.sum(factor * grads[k], -1) for k in range(3)]  98.7 us
    ppermute x18, starting transfers between devices, with_halo(): lax.ppermute(lax.slice_in_dim(block, block.shape[dim] - width, None, axis...  80.5 us
    reduce_sum x51, other arithmetic, apply_pass(): total = total + jnp.sum(masses * closing, -1)  78.3 us
    psum x5, blocking collectives, one_axis_at_a_time(): x = lax.psum(x, axis)  42.7 us
    ppermute x18, starting transfers between devices, with_halo(): lax.ppermute(lax.slice_in_dim(block, 0, width, axis=dim), axis, backward)  32.1 us
    ppermute x18, waiting for transfers between devices, with_halo(): lax.ppermute(lax.slice_in_dim(block, 0, width, axis=dim), axis, backward)  25.4 us
    ppermute x6, starting transfers between devices, passed_along(): return lax.ppermute(x, axis, pairs)  17.6 us
    reduce_sum x7, other arithmetic, setup_pass(): density = density + jnp.sum(masses * kernel, -1)  11.4 us
  transfers between devices with their start and end apart: 42, of which 14 were waited for; matrix products, arithmetic and copies ran while one was open for 10% of the time, Pallas kernels for 0%

commit v1 on v0

v1 whole, which is shorter than its diff:
```python
import math

import jax
import jax.numpy as jnp
from jax import lax
from jax.experimental import pallas as pl
from jax.experimental.pallas import tpu as pltpu
from jax.sharding import PartitionSpec as P

ITERS = 2
PLANE = ("gy", "gz")
F32 = jnp.float32
BF16 = jnp.bfloat16

kernel_var = 0.25
time_step = 2.0
particle_mass = 1.0 / 45.0
rest_density = 1.0
relaxation = 0.5
floor_value = 0.1
gravity = 0.1

KAPPA = math.log2(math.e) / kernel_var
YSCALE = math.sqrt(2.0 * KAPPA)
GRAD = 2.0 / kernel_var
ABSENT = 30000.0
PADDED = ((-1, 1), (0, 0), (0, 1), (1, 0))
VMEM = pl.BlockSpec(memory_space=pltpu.VMEM)
SMEM = pl.BlockSpec(memory_space=pltpu.SMEM)


def rows_iota(shape):
    return lax.broadcasted_iota(jnp.int32, shape, 0)


def split3(x):
    h = x.astype(BF16).astype(F32)
    m = (x - h).astype(BF16).astype(F32)
    return h, m, x - h - m


def stacked(x):
    h, m, l = split3(x)
    return jnp.concatenate([h, m, l, jnp.zeros_like(x)], 0).astype(BF16)


def unstacked(acc):
    return acc[0:8] + acc[8:16] + acc[16:24]


def dot(a, b):
    return jnp.dot(a, b, preferred_element_type=F32)


def plane_source(idx, dy, dz):
    gy = idx[1] + dy
    gz = idx[2] + dz
    ok = (gy >= 0) & (gy < idx[3]) & (gz >= 0) & (gz < idx[4])
    return jnp.where(ok, gy * idx[4] + gz, 0), ok


def pack_kernel(cnt, pos, vel, heading, cell, send, one):
    lane = lax.broadcasted_iota(jnp.int32, (1, 128), 1)
    code = jnp.where(lane < cnt[0, 0, 0], heading[0, 0] * 8 + cell[0, 0] + 1, 0).astype(F32)
    one[0:1, :] = code
    for f in range(3):
        one[1 + f : 2 + f, :] = pos[f, 0, 0]
        one[4 + f : 5 + f, :] = vel[f, 0, 0]
    one[7:8, :] = jnp.zeros((1, 128), F32)
    tile = one[...]
    for p in range(send.shape[0]):
        send[p] = tile


def insert_kernel(idx, cnt, recv, xlo, xhi, pos, vel, send, base):
    row = rows_iota((8, 128))
    lane = lax.broadcasted_iota(jnp.int32, (8, 128), 1)
    cargos, marks = [], []
    for d in range(6):
        if d < 2:
            tile, ok = (xlo, xhi)[d][...], True
        else:
            step = -1 if d % 2 == 0 else 1
            src, ok = plane_source(idx, step if d < 4 else 0, step if d >= 4 else 0)
            tile = recv[src]
        mark = tile[0:1] == (row + (d * 8 + 1)).astype(F32)
        if ok is not True:
            mark = mark & ok
        cargos.append(stacked(tile))
        marks.append(jnp.where(mark, 1.0, 0.0))
    marked = jnp.concatenate(marks, 0).astype(BF16)
    r128 = rows_iota((128, 128))
    c128 = lax.broadcasted_iota(jnp.int32, (128, 128), 1)
    before = dot(marked, jnp.where(r128 < c128, 1.0, 0.0).astype(BF16))
    total = dot(marked, jnp.ones((128, 128), BF16))
    filled = jnp.zeros((8, 128), jnp.int32)
    for c in range(8):
        filled = jnp.where(row == c, cnt[c // 4, c // 2 % 2, c % 2], filled)
    grown = filled.astype(F32)
    targets = []
    for d in range(6):
        targets.append(jnp.where(marks[d] > 0, before[d * 8 : d * 8 + 8] + grown, -1.0))
        grown = grown + total[d * 8 : d * 8 + 8]
    slot = r128.astype(F32)
    lanef = lane.astype(F32)
    for c in range(8):
        acc = jnp.zeros((32, 128), F32)
        for d in range(6):
            hot = jnp.where(slot == targets[d][c : c + 1], 1.0, 0.0).astype(BF16)
            acc = acc + lax.dot_general(
                cargos[d], hot, (((1,), (1,)), ((), ())), preferred_element_type=F32
            )
        for f in range(3):
            base[c, 1 + f : 2 + f, :] = pos[f, c // 4, c // 2 % 2, c % 2 : c % 2 + 1, :]
            base[c, 4 + f : 5 + f, :] = vel[f, c // 4, c // 2 % 2, c % 2 : c % 2 + 1, :]
        base[c, 0:1, :] = jnp.zeros((1, 128), F32)
        base[c, 7:8, :] = jnp.zeros((1, 128), F32)
        tile = jnp.where(lane < cnt[c // 4, c // 2 % 2, c % 2], base[c], unstacked(acc))
        occ = lanef < grown[c : c + 1]
        tile = jnp.where(row == 0, 1.0, jnp.where(row == 7, 0.0, tile))
        tile = jnp.where(occ, tile, 0.0)
        for p in range(send.shape[0]):
            send[p, c] = tile


def gather_kernel(idx, recv, low, high):
    for yp, (dy, y) in enumerate(PADDED):
        for zp, (dz, z) in enumerate(PADDED):
            src, ok = plane_source(idx, dy, dz)
            q = yp * 4 + zp
            for x, out in enumerate((low, high)):
                c = x * 4 + y * 2 + z
                if len(recv.shape) == 3:
                    out[q : q + 1, :] = jnp.where(ok, recv[src, c : c + 1, :], 0.0)
                else:
                    out[q] = jnp.where(ok, recv[src, c], 0.0)


def gather_last_kernel(idx, recv, send, low, high):
    gather_kernel(idx, recv, low, high)
    totals = recv[0, 8:16, :]
    for p in range(1, recv.shape[0]):
        totals = totals + recv[p, 8:16, :]
    a0, a1 = low[...], high[...]
    for p in range(send.shape[0]):
        send[p, 0:16, :] = jnp.where(p > idx[0], a1, a0)
        send[p, 16:24, :] = totals


def setup_kernel(idx, cnt, p0, p1, p2, p3, pprev, whi, wlo, xr, own, aux, press, send, tiles, at, bi, ft, srow):
    row = rows_iota((8, 128))
    axis_row = (row >= 1) & (row <= 3)
    for x, ref in enumerate((p0, p1, p2, p3)):
        tiles[x * 16 : x * 16 + 16] = ref[...]
    ones_rows = jnp.where((row >= 3) & (row < 6), 1.0, 0.0)
    minus_rows = jnp.where(row < 3, -1.0, 0.0)
    zeros8 = jnp.zeros((8, 128), F32)

    def column(xy, carry):
        xs = (xy // 4 - 2).astype(F32)
        ys = (xy % 4 - 2).astype(F32)
        for z in range(4):
            tile = tiles[xy * 4 + z]
            occ = tile[0:1]
            shift = jnp.where(row == 1, xs, jnp.where(row == 2, ys, jnp.where(row == 3, z - 2.0, 0.0)))
            st = (tile + shift) * occ
            tiles[xy * 4 + z] = st
            xr[xy * 4 + z] = jnp.where(row < 4, st, 0.0)
            vel = pltpu.roll(st, 5, 0)
            vx = jnp.sum(jnp.where(axis_row, st * vel, 0.0), 0, keepdims=True)
            ft[xy, :, z * 128 : z * 128 + 128] = stacked(jnp.where(row == 7, vx, st))
            y = jnp.where(axis_row, st * YSCALE, 0.0)
            q = 0.5 * jnp.sum(y * y, 0, keepdims=True)
            h, m, l = split3(y)
            qj = jnp.where(occ > 0, q, ABSENT)
            jh, jm, jl = split3(qj)
            qcol = jnp.where(row == 0, jh, jnp.where(row == 1, jm, jnp.where(row == 2, jl, ones_rows)))
            side = jnp.concatenate([h, h, m, m, h, l, qcol, zeros8], 0)
            at[xy, z * 128 : z * 128 + 128, :] = side.T.astype(BF16)
            ih, im, il = split3(q)
            qrow = jnp.where(row == 3, -ih, jnp.where(row == 4, -im, jnp.where(row == 5, -il, minus_rows)))
            bi[xy * 4 + z] = jnp.concatenate([h, m, h, m, l, h, qrow, zeros8], 0).astype(BF16)
        return carry

    lax.fori_loop(0, 16, column, 0)

    def centre(cxy, carry):
        cx, cy = cxy // 2, cxy % 2
        for cz in range(2):
            c = cxy * 2 + cz
            q = ((cx + 1) * 4 + cy + 1) * 4 + cz + 1
            b = bi[q]
            acc = jnp.zeros((32, 128), F32)
            gs = jnp.zeros((8, 128), F32)
            for ab in range(9):
                xy = (cx + ab // 3) * 4 + cy + ab % 3
                e = dot(at[xy, cz * 128 : cz * 128 + 384, :], b)
                w = jnp.exp2(e)
                hi = w.astype(BF16)
                lo = (w - hi.astype(F32)).astype(BF16)
                whi[cxy, cz, ab] = hi
                wlo[cxy, cz, ab] = lo
                f = ft[xy, :, cz * 128 : cz * 128 + 384]
                acc = acc + dot(f, hi) + dot(f, lo)
                gs = gs + jnp.sum((w * w * e).reshape(48, 8, 128), 0)
            r = unstacked(acc)
            st = tiles[q]
            occ = st[0:1] > 0
            s0 = r[0:1]
            g = jnp.where(axis_row, st * s0 - r, 0.0)
            own[c] = g
            density = particle_mass * s0
            pair = pltpu.roll(st, 5, 0) * g - st * pltpu.roll(r, 5, 0)
            divergence = (-GRAD * particle_mass) * (
                jnp.sum(jnp.where(axis_row, pair, 0.0), 0, keepdims=True) + r[7:8]
            )
            grad_norm = (GRAD * particle_mass) ** 2 * jnp.sum(g * g, 0, keepdims=True)
            grad_square = (-GRAD * GRAD * particle_mass / KAPPA) * jnp.sum(gs, 0, keepdims=True)
            safe = jnp.where(occ, density, 1.0)
            safe2 = safe * safe
            source = jnp.where(occ, rest_density - (density + time_step * divergence), 0.0)
            weight = jnp.where(occ, particle_mass, 0.0)
            diagonal = jnp.maximum(
                time_step * time_step * (grad_norm + weight * grad_square) / safe2, floor_value
            )
            lane = lax.broadcasted_iota(jnp.int32, (1, 128), 1)
            pressure = jnp.where(lane < cnt[cx, cy, cz], pprev[cx, cy, cz : cz + 1, :], 0.0)
            aux[c, 0:1, :] = safe2
            aux[c, 1:2, :] = source
            aux[c, 2:3, :] = diagonal
            press[pl.ds(c, 1), :] = pressure
            srow[pl.ds(c, 1), :] = jnp.where(occ, pressure / safe2, 0.0)
        return carry

    lax.fori_loop(0, 4, centre, 0)
    tile = srow[...]
    for p in range(send.shape[0]):
        send[p] = tile


def pass_over(whi, wlo, ft, finish):
    def centre(cxy, carry):
        cx, cy = cxy // 2, cxy % 2
        for cz in range(2):
            acc = jnp.zeros((32, 128), F32)
            for ab in range(9):
                f = ft[(cx + ab // 3) * 4 + cy + ab % 3, :, cz * 128 : cz * 128 + 384]
                acc = acc + dot(f, whi[cxy, cz, ab]) + dot(f, wlo[cxy, cz, ab])
            finish(cx, cy, cz, ((cx + 1) * 4 + cy + 1) * 4 + cz + 1, unstacked(acc))
        return carry

    lax.fori_loop(0, 4, centre, 0)


def scaled_features(planes, xr, ft, srows):
    for x, ref in enumerate(planes):
        srows[x * 16 : x * 16 + 16, :] = ref[...]

    def column(xy, carry):
        for z in range(4):
            q = xy * 4 + z
            ft[xy, :, z * 128 : z * 128 + 128] = stacked(srows[pl.ds(q, 1), :] * xr[q])
        return carry

    lax.fori_loop(0, 16, column, 0)


def accel_of(q, c, r, srows, xr, own):
    return (GRAD * particle_mass) * (srows[pl.ds(q, 1), :] * own[c] + xr[q] * r[0:1] - r)


def accel_kernel(p0, p1, p2, p3, xr, own, whi, wlo, send, ft, srows):
    scaled_features((p0, p1, p2, p3), xr, ft, srows)

    def finish(cx, cy, cz, q, r):
        c = (cx * 2 + cy) * 2 + cz
        a = accel_of(q, c, r, srows, xr, own)[0:4]
        for p in range(send.shape[0]):
            send[p, c] = a

    pass_over(whi, wlo, ft, finish)


def apply_kernel(p0, p1, p2, p3, xr, own, whi, wlo, aux, press, errs, pnew, enew, send, ft, tiles, *, at_iter, last):
    row = rows_iota((8, 128))
    axis_row = (row >= 1) & (row <= 3)
    zeros4 = jnp.zeros((4, 128), F32)

    for x, ref in enumerate((p0, p1, p2, p3)):
        tiles[x * 16 : x * 16 + 16] = ref[...]

    def column(xy, carry):
        for z in range(4):
            q = xy * 4 + z
            a = jnp.concatenate([tiles[q], zeros4], 0)
            ax = jnp.sum(jnp.where(axis_row, a * xr[q], 0.0), 0, keepdims=True)
            ft[xy, :, z * 128 : z * 128 + 128] = stacked(jnp.where(row == 0, ax, a))
        return carry

    lax.fori_loop(0, 16, column, 0)
    enew[...] = errs[...]

    def finish(cx, cy, cz, q, r):
        c = (cx * 2 + cy) * 2 + cz
        a = jnp.concatenate([tiles[q], zeros4], 0)
        x = xr[q]
        inner = jnp.sum(jnp.where(axis_row, a * own[c] - x * r, 0.0), 0, keepdims=True) + r[0:1]
        applied = (-time_step * time_step * GRAD * particle_mass) * inner
        occ = x[0:1] > 0
        safe2, source, diagonal = (aux[c, k : k + 1, :] for k in range(3))
        residual = jnp.where(occ, source - applied, 0.0)
        enew[at_iter : at_iter + 1, :] = enew[at_iter : at_iter + 1, :] + jnp.abs(residual)
        p = press[pl.ds(c, 1), :]
        p = jnp.where(occ, jnp.maximum(p + relaxation * (applied - source) / diagonal, 0.0), 0.0)
        scaled = jnp.where(occ, p / safe2, 0.0)
        if last:
            pnew[cx, cy, cz : cz + 1, :] = p
        else:
            pnew[pl.ds(c, 1), :] = p
        send[0, pl.ds(c, 1), :] = scaled

    pass_over(whi, wlo, ft, finish)
    if last:
        send[0, 8:16, :] = enew[...]
    tile = send[0]
    for p in range(1, send.shape[0]):
        send[p] = tile


def final_kernel(idx, recv, p1, p2, state, xr, own, whi, wlo, vout, eout, ft, srows, *, slots):
    gx, nx = idx[0], recv.shape[0]
    totals = recv[0, 16:24, :]
    for p in range(1, nx):
        totals = totals + recv[p, 16:24, :]
    for it in range(ITERS):
        eout[it] = jnp.sum(totals[it : it + 1, :]) / slots
    low = jnp.where(gx > 0, recv[jnp.maximum(gx - 1, 0), 0:16, :], 0.0)
    high = jnp.where(gx < nx - 1, recv[jnp.minimum(gx + 1, nx - 1), 0:16, :], 0.0)
    scaled_features((low, p1, p2, high), xr, ft, srows)
    row = rows_iota((8, 128))

    def finish(cx, cy, cz, q, r):
        c = (cx * 2 + cy) * 2 + cz
        a = accel_of(q, c, r, srows, xr, own)
        st = state[0, c]
        pulled = a - jnp.where(row == 3, gravity, 0.0)
        v = pltpu.roll(st, 5, 0) + time_step * pulled
        v = jnp.where(st[0:1] > 0, v, 0.0)
        for f in range(3):
            vout[f, cx, cy, cz : cz + 1, :] = v[1 + f : 2 + f]

    pass_over(whi, wlo, ft, finish)


def call(body, outs, specs, scratch=(), limit=24 << 20):
    params = pltpu.CompilerParams(vmem_limit_bytes=limit)
    return pl.pallas_call(
        body,
        out_shape=outs,
        in_specs=specs,
        out_specs=jax.tree.map(lambda o: SMEM if o.shape == (ITERS,) else VMEM, outs),
        scratch_shapes=list(scratch),
        compiler_params=params,
    )


def sds(*shape, dtype=F32):
    return jax.ShapeDtypeStruct(shape, dtype)


def on_device(positions, velocities, pressure_prev, counts, out_positions, out_velocities, out_dir, out_cell, out_count):
    nx, ny, nz = lax.axis_size("gx"), lax.axis_size("gy"), lax.axis_size("gz")
    plane = ny * nz
    idx = jnp.stack([lax.axis_index("gx"), lax.axis_index("gy"), lax.axis_index("gz"), ny, nz]).astype(jnp.int32)
    forward = [(i, i + 1) for i in range(nx - 1)]
    backward = [(b, a) for a, b in forward]

    def spread(send):
        return lax.all_to_all(send, PLANE, 0, 0)

    def beside(a0, a1):
        return lax.ppermute(a1, "gx", forward), lax.ppermute(a0, "gx", backward)

    def planes(send, shape):
        a0, a1 = call(gather_kernel, (sds(16, *shape), sds(16, *shape)), [SMEM, VMEM])(idx, spread(send))
        low, high = beside(a0, a1)
        return low, a0, a1, high

    send, one = call(pack_kernel, (sds(plane, 8, 128), sds(8, 128)), [SMEM] + [VMEM] * 4)(
        out_count, out_positions, out_velocities, out_dir, out_cell
    )
    xlo, xhi = beside(one, one)
    send = call(
        insert_kernel, sds(plane, 8, 8, 128), [SMEM, SMEM] + [VMEM] * 5, [pltpu.VMEM((8, 8, 128), F32)]
    )(idx, counts, spread(send), xlo, xhi, positions, velocities)
    state = send
    near = planes(send, (8, 128))
    wshape = sds(4, 2, 9, 384, 128, dtype=BF16)
    ft = pltpu.VMEM((16, 32, 512), BF16)
    whi, wlo, xr, own, aux, press, send = call(
        setup_kernel,
        (wshape, wshape, sds(64, 8, 128), sds(8, 8, 128), sds(8, 8, 128), sds(8, 128), sds(plane, 8, 128)),
        [SMEM, SMEM] + [VMEM] * 5,
        [pltpu.VMEM((64, 8, 128), F32), pltpu.VMEM((16, 512, 64), BF16), pltpu.VMEM((64, 64, 128), BF16), ft, pltpu.VMEM((8, 128), F32)],
    )(idx, counts, *near, pressure_prev)
    errs = jnp.zeros((8, 128), F32)
    for it in range(ITERS):
        last = it == ITERS - 1
        near = planes(send, (128,))
        send = call(accel_kernel, sds(plane, 8, 4, 128), [VMEM] * 8, [ft, pltpu.VMEM((64, 128), F32)])(
            *near, xr, own, whi, wlo
        )
        near = planes(send, (4, 128))

        def body(*refs, it=it, last=last):
            apply_kernel(*refs, at_iter=it, last=last)

        press, errs, send = call(
            body,
            (sds(2, 2, 2, 128) if last else sds(8, 128), sds(8, 128), sds(plane, 16 if last else 8, 128)),
            [VMEM] * 11,
            [ft, pltpu.VMEM((64, 4, 128), F32)],
        )(*near, xr, own, whi, wlo, aux, press, errs)
    send, a0, a1 = call(gather_last_kernel, (sds(nx, 24, 128), sds(16, 128), sds(16, 128)), [SMEM, VMEM])(
        idx, spread(send)
    )
    recv = lax.all_to_all(send, "gx", 0, 0)
    slots = nx * plane * 8 * 128

    def body(*refs):
        final_kernel(*refs, slots=slots)

    velocity_new, density_error = call(
        body, (sds(3, 2, 2, 2, 128), sds(ITERS)), [SMEM] + [VMEM] * 8, [ft, pltpu.VMEM((64, 128), F32)]
    )(idx, recv, a0, a1, state, xr, own, whi, wlo)
    return press, velocity_new, density_error


def solution(mesh):
    cells = P("gx", "gy", "gz", None)
    vectors = P(None, "gx", "gy", "gz", None)
    ints = P("gx", "gy", "gz")
    return jax.shard_map(
        on_device,
        mesh=mesh,
        in_specs=(vectors, vectors, cells, ints, vectors, vectors, cells, cells, ints),
        out_specs=(cells, vectors, P()),
        check_vma=False,
    )
```

time: 427 us -> 209 us (0.49); the launches traced: 420 us -> 209 us
  other arithmetic: 205 us -> 0.08 us
  starting transfers between devices: 130 us -> 38 us
  blocking collectives: 42.7 us -> 96.6 us
  Pallas kernels: 0 us -> 42 us
  waiting for transfers between devices: 31.1 us -> 24.8 us
    reduce_sum x105 -> x0, other arithmetic: 192 us -> none  [the longest x44 98.7 us: accel_pass(): totals = [totals[k] + jnp.sum(factor * grads[k], -1) for k in range(3)]]
    ppermute x42 -> x12, starting transfers between devices: 130 us -> 29.7 us  [beside(): return (lax.ppermute(a1, 'gx', forward), lax.ppermute(a0, 'gx', backward))]
    all_to_all x0 -> x7, blocking collectives: none -> 96.6 us  [the longest x6 78.2 us: spread(): return lax.all_to_all(send, PLANE, 0, 0)]
    psum x5 -> x0, blocking collectives: 42.7 us -> none  [one_axis_at_a_time(): x = lax.psum(x, axis)]
    pallas_call x0 -> x14, Pallas kernels: none -> 42 us  [the longest x1 17.6 us: on_device(): call(setup_kernel, (wshape, wshape, sds(64, 8, 128), sds(8, 8, 128), sds(...]
    ppermute x42 -> x12, waiting for transfers between devices: 31.1 us -> 17.5 us  [beside(): return (lax.ppermute(a1, 'gx', forward), lax.ppermute(a0, 'gx', backward))]
    all_to_all x0 -> x1, starting transfers between devices: none -> 8.35 us  [spread(): return lax.all_to_all(send, PLANE, 0, 0)]
    all_to_all x0 -> x1, waiting for transfers between devices: none -> 7.28 us  [spread(): return lax.all_to_all(send, PLANE, 0, 0)]
  transfers between devices with their start and end apart: 42 -> 13, of which waited for: 14 -> 6; matrix products, arithmetic and copies ran while one was open for 10% -> 0% of each run, Pallas kernels for 0% -> 0%
where the time goes in v1:
time: 209 us
  blocking collectives  96.6 us (46%)
  Pallas kernels  42 us (20%)
  starting transfers between devices  38 us (18%)
  waiting for transfers between devices  24.8 us (12%)
  local copies, waits for them, and re-layouts  5.45 us (3%)
    all_to_all x6, blocking collectives, spread(): return lax.all_to_all(send, PLANE, 0, 0)  78.2 us
    ppermute x12, starting transfers between devices, beside(): return (lax.ppermute(a1, 'gx', forward), lax.ppermute(a0, 'gx', backward))  29.7 us
    all_to_all x1, blocking collectives, on_device(): recv = lax.all_to_all(send, 'gx', 0, 0)  18.4 us
    pallas_call x1, Pallas kernels, on_device(): call(setup_kernel, (wshape, wshape, sds(64, 8, 128), sds(8, 8, 128), sds(...  17.6 us
    ppermute x12, waiting for transfers between devices, beside(): return (lax.ppermute(a1, 'gx', forward), lax.ppermute(a0, 'gx', backward))  17.5 us
    all_to_all x1, starting transfers between devices, spread(): return lax.all_to_all(send, PLANE, 0, 0)  8.35 us
    pallas_call x2, Pallas kernels, on_device(): call(body, (sds(2, 2, 2, 128) if last else sds(8, 128), sds(8, 128), sds(...  7.49 us
    all_to_all x1, waiting for transfers between devices, spread(): return lax.all_to_all(send, PLANE, 0, 0)  7.28 us
  transfers between devices with their start and end apart: 13, of which 6 were waited for; matrix products, arithmetic and copies ran while one was open for 0% of the time, Pallas kernels for 0%

profile of v1, /device:TPU:1, one launch (start us, length us, event | category | flops | bytes accessed | tf_op | source)
XLA Modules:
  0.0 208.5 jit_solution(9695236451441272816)
XLA Ops:
  1.3 0.7 copy-done.4
  2.0 0.7 copy-done.5
  2.6 0.7 copy-done.6
  3.3 0.7 copy-done.7
  4.0 0.7 shard_map.112
  4.6 1.3 collective-permute-start.1
  5.9 4.6 %collective-permute-start = (f32[8,128]{1,0:T(8,128)S(1)}, f32[8,128]{1,0:T(8,128)S(1)}, u32[]{:S(2)}, u32[]{:S(2)}) collective-permute-start(f32[8,128]{1,0:T(8,128)S(1)} %get-tuple-element.33), channel_id=1, source_target_pairs={{0,16},{16,32},{32,48},{48,64},{64,80},{80,96},{96,112},{112,128},... | collective-permute-start | bytes 12296 | tf_op jit(solution)/shard_map/ppermute | solution.py:382
  10.5 8.3 %all-to-all-start = ((f32[16,8,128]{2,1,0:T(8,128)}), f32[16,8,128]{2,1,0:T(8,128)S(1)}, u32[]{:S(2)}, u32[]{:S(2)}) async-start(f32[16,8,128]{2,1,0:T(8,128)} %get-tuple-element.32), calls=%async_computation | async-start | bytes 131072 | tf_op jit(solution)/shard_map/all_to_all | solution.py:379
  19.0 7.3 %all-to-all-done.recv = f32[16,8,128]{2,1,0:T(8,128)S(1)} async-done(((f32[16,8,128]{2,1,0:T(8,128)}), f32[16,8,128]{2,1,0:T(8,128)S(1)}, u32[]{:S(2)}, u32[]{:S(2)}) %all-to-all-start) | async-done | bytes 65568 | tf_op jit(solution)/shard_map/all_to_all | solution.py:379
  26.3 0.7 copy-done
  27.0 0.7 copy-done.1
  27.7 0.7 copy-done.2
  28.4 1.7 shard_map.113.refs_4_
  30.0 14.1 %all_to_all.40.recv = f32[16,8,8,128]{3,2,1,0:T(8,128)S(1)} all-to-all(f32[16,8,8,128]{3,2,1,0:T(8,128)S(1)} %shard_map.113.refs_4_), channel_id=1, replica_groups=mesh['gx'=16,'gy'=4,'gz'=4] {'gy','gz'}, dimensions={0} | all-to-all | bytes 1048576 | tf_op jit(solution)/shard_map/all_to_all | solution.py:379
  44.1 0.6 shard_map.114
  44.7 3.2 %collective-permute-start.2 = (f32[16,8,128]{2,1,0:T(8,128)S(1)}, f32[16,8,128]{2,1,0:T(8,128)S(1)}, u32[]{:S(2)}, u32[]{:S(2)}) collective-permute-start(f32[16,8,128]{2,1,0:T(8,128)S(1)} %get-tuple-element.34.p2), channel_id=1, source_target_pairs={{0,16},{16,32},{32,48},{48,64},{64,80},{80,96},{96,112},{112,128},... | collective-permute-start | bytes 196616 | tf_op jit(solution)/shard_map/ppermute | solution.py:382
  47.9 1.3 collective-permute-start.3
  49.2 3.8 %collective-permute-done.3.p3 = f32[16,8,128]{2,1,0:T(8,128)S(1)} collective-permute-done((f32[16,8,128]{2,1,0:T(8,128)S(1)}, f32[16,8,128]{2,1,0:T(8,128)S(1)}, u32[]{:S(2)}, u32[]{:S(2)}) %collective-permute-start.3) | collective-permute-done | bytes 65568 | tf_op jit(solution)/shard_map/ppermute | solution.py:382
  53.0 0.7 copy-done.3
  53.7 17.6 %shard_map.115 = (bf16[4,2,9,384,128]{4,3,2,1,0:T(8,128)(2,1)S(1)}, bf16[4,2,9,384,128]{4,3,2,1,0:T(8,128)(2,1)S(1)}, f32[64,8,128]{2,1,0:T(8,128)S(1)}, f32[8,8...) custom-call(s32[5]{0:T(128)S(1)} %pad_add_fusion.idx.refs_0_, ...), custom_call_target="tpu_custom_call" | custom-call | tf_op jit(solution)/shard_map/pallas_call | solution.py:400
  71.3 12.8 %all_to_all.41.recv = f32[16,8,128]{2,1,0:T(8,128)S(1)} all-to-all(f32[16,8,128]{2,1,0:T(8,128)S(1)} %get-tuple-element.36), channel_id=1, replica_groups=mesh['gx'=16,'gy'=4,'gz'=4] {'gy','gz'}, dimensions={0} | all-to-all | bytes 131072 | tf_op jit(solution)/shard_map/all_to_all | solution.py:379
  84.1 0.6 shard_map.116
  84.7 4.0 %collective-permute-start.4 = (f32[16,128]{1,0:T(8,128)S(1)}, f32[16,128]{1,0:T(8,128)S(1)}, u32[]{:S(2)}, u32[]{:S(2)}) collective-permute-start(f32[16,128]{1,0:T(8,128)S(1)} %get-tuple-element.37.p2), channel_id=1, source_target_pairs={{0,16},{16,32},{32,48},{48,64},{64,80},{80,96},{96,112},{112,128},... | collective-permute-start | bytes 24584 | tf_op jit(solution)/shard_map/ppermute | solution.py:382
  88.7 1.3 collective-permute-start.5
  90.0 3.1 %collective-permute-done.5.p3 = f32[16,128]{1,0:T(8,128)S(1)} collective-permute-done((f32[16,128]{1,0:T(8,128)S(1)}, f32[16,128]{1,0:T(8,128)S(1)}, u32[]{:S(2)}, u32[]{:S(2)}) %collective-permute-start.5) | collective-permute-done | bytes 8224 | tf_op jit(solution)/shard_map/ppermute | solution.py:382
  93.1 3.3 %shard_map.117 = f32[16,8,4,128]{3,2,1,0:T(4,128)S(1)} custom-call(f32[16,128]{1,0:T(8,128)S(1)} %collective-permute-done.4.p0, f32[16,128]{1,0:T(8,128)S(1)} %get-tuple-element.38.p1, f32[16,128]{1,0:T(8,128)S(1)} %get-tuple-element.37.p2, f32[16,128]{1,0:T(8,128)S(1)} %collective-permute-done.5.p3, f32[64,8,128]{2,1,0:T(8,128)S(1)} %get-tuple-element.39.xr.refs_4_.refs_5_, ...), custom_call_target="tpu_custom_call" | custom-call | tf_op jit(solution)/shard_map/pallas_call | solution.py:410
  96.4 13.7 %all_to_all.42.recv = f32[16,8,4,128]{3,2,1,0:T(4,128)S(1)} all-to-all(f32[16,8,4,128]{3,2,1,0:T(4,128)S(1)} %shard_map.117), channel_id=1, replica_groups=mesh['gx'=16,'gy'=4,'gz'=4] {'gy','gz'}, dimensions={0} | all-to-all | bytes 524288 | tf_op jit(solution)/shard_map/all_to_all | solution.py:379
  110.1 0.6 shard_map.118
  110.6 3.0 %collective-permute-start.6 = (f32[16,4,128]{2,1,0:T(4,128)S(1)}, f32[16,4,128]{2,1,0:T(4,128)S(1)}, u32[]{:S(2)}, u32[]{:S(2)}) collective-permute-start(f32[16,4,128]{2,1,0:T(4,128)S(1)} %get-tuple-element.43.refs_2_), channel_id=1, source_target_pairs={{0,16},{16,32},{32,48},{48,64},{64,80},{80,96},{96,112},{112,128},... | collective-permute-start | bytes 98312 | tf_op jit(solution)/shard_map/ppermute | solution.py:382
  113.7 1.3 collective-permute-start.7
  115.0 3.6 %collective-permute-done.7.refs_3_ = f32[16,4,128]{2,1,0:T(4,128)S(1)} collective-permute-done((f32[16,4,128]{2,1,0:T(4,128)S(1)}, f32[16,4,128]{2,1,0:T(4,128)S(1)}, u32[]{:S(2)}, u32[]{:S(2)}) %collective-permute-start.7) | collective-permute-done | bytes 32800 | tf_op jit(solution)/shard_map/ppermute | solution.py:382
  118.6 3.4 %shard_map.119 = (f32[8,128]{1,0:T(8,128)S(1)}, f32[8,128]{1,0:T(8,128)S(1)}, f32[16,8,128]{2,1,0:T(8,128)S(1)}) custom-call(f32[16,4,128]{2,1,0:T(4,128)S(1)} %collective-permute-done.6.refs_0_, f32[16,4,128]{2,1,0:T(4,128)S(1)} %get-tuple-element.44.refs_1_, f32[16,4,128]{2,1,0:T(4,128)S(1)} %get-tuple-element.43.refs_2_, ...), custom_call_target="tpu_custom_call" | custom-call | tf_op jit(solution)/shard_map/pallas_call | solution.py:418
  122.0 12.1 %all_to_all.43.recv = f32[16,8,128]{2,1,0:T(8,128)S(1)} all-to-all(f32[16,8,128]{2,1,0:T(8,128)S(1)} %get-tuple-element.47), channel_id=1, replica_groups=mesh['gx'=16,'gy'=4,'gz'=4] {'gy','gz'}, dimensions={0} | all-to-all | bytes 131072 | tf_op jit(solution)/shard_map/all_to_all | solution.py:379
  134.1 0.6 shard_map.120
  134.7 3.8 %collective-permute-start.8 = (f32[16,128]{1,0:T(8,128)S(1)}, f32[16,128]{1,0:T(8,128)S(1)}, u32[]{:S(2)}, u32[]{:S(2)}) collective-permute-start(f32[16,128]{1,0:T(8,128)S(1)} %get-tuple-element.48.p2), channel_id=1, source_target_pairs={{0,16},{16,32},{32,48},{48,64},{64,80},{80,96},{96,112},{112,128},... | collective-permute-start | bytes 24584 | tf_op jit(solution)/shard_map/ppermute | solution.py:382
  138.5 1.3 collective-permute-start.9
  139.9 3.1 %collective-permute-done.9.p3 = f32[16,128]{1,0:T(8,128)S(1)} collective-permute-done((f32[16,128]{1,0:T(8,128)S(1)}, f32[16,128]{1,0:T(8,128)S(1)}, u32[]{:S(2)}, u32[]{:S(2)}) %collective-permute-start.9) | collective-permute-done | bytes 8224 | tf_op jit(solution)/shard_map/ppermute | solution.py:382
  142.9 3.3 %shard_map.121 = f32[16,8,4,128]{3,2,1,0:T(4,128)S(1)} custom-call(f32[16,128]{1,0:T(8,128)S(1)} %collective-permute-done.8.p0, f32[16,128]{1,0:T(8,128)S(1)} %get-tuple-element.49.p1, f32[16,128]{1,0:T(8,128)S(1)} %get-tuple-element.48.p2, f32[16,128]{1,0:T(8,128)S(1)} %collective-permute-done.9.p3, f32[64,8,128]{2,1,0:T(8,128)S(1)} %get-tuple-element.39.xr.refs_4_.refs_5_, ...), custom_call_target="tpu_custom_call" | custom-call | tf_op jit(solution)/shard_map/pallas_call | solution.py:410
  146.2 13.7 %all_to_all.44.recv = f32[16,8,4,128]{3,2,1,0:T(4,128)S(1)} all-to-all(f32[16,8,4,128]{3,2,1,0:T(4,128)S(1)} %shard_map.121), channel_id=1, replica_groups=mesh['gx'=16,'gy'=4,'gz'=4] {'gy','gz'}, dimensions={0} | all-to-all | bytes 524288 | tf_op jit(solution)/shard_map/all_to_all | solution.py:379
  159.9 0.6 shard_map.122
  160.5 3.2 %collective-permute-start.10 = (f32[16,4,128]{2,1,0:T(4,128)S(1)}, f32[16,4,128]{2,1,0:T(4,128)S(1)}, u32[]{:S(2)}, u32[]{:S(2)}) collective-permute-start(f32[16,4,128]{2,1,0:T(4,128)S(1)} %get-tuple-element.50.refs_2_), channel_id=1, source_target_pairs={{0,16},{16,32},{32,48},{48,64},{64,80},{80,96},{96,112},{112,128},... | collective-permute-start | bytes 98312 | tf_op jit(solution)/shard_map/ppermute | solution.py:382
  163.7 1.3 collective-permute-start.11
  165.0 4.0 %collective-permute-done.11.refs_3_ = f32[16,4,128]{2,1,0:T(4,128)S(1)} collective-permute-done((f32[16,4,128]{2,1,0:T(4,128)S(1)}, f32[16,4,128]{2,1,0:T(4,128)S(1)}, u32[]{:S(2)}, u32[]{:S(2)}) %collective-permute-start.11) | collective-permute-done | bytes 32800 | tf_op jit(solution)/shard_map/ppermute | solution.py:382
  169.0 4.0 %shard_map.123 = (f32[2,2,2,128]{3,2,1,0:T(2,128)}, f32[8,128]{1,0:T(8,128)}, f32[16,16,128]{2,1,0:T(8,128)S(1)}) custom-call(f32[16,4,128]{2,1,0:T(4,128)S(1)} %collective-permute-done.10.refs_0_, f32[16,4,128]{2,1,0:T(4,128)S(1)} %get-tuple-element.51.refs_1_, f32[16,4,128]{2,1,0:T(4,128)S(1)} %get-tuple-element.50.refs_2_, ...), custom_call_target="tpu_custom_call" | custom-call | tf_op jit(solution)/shard_map/pallas_call | solution.py:418
  173.0 11.9 %all_to_all.45.recv = f32[16,16,128]{2,1,0:T(8,128)S(1)} all-to-all(f32[16,16,128]{2,1,0:T(8,128)S(1)} %get-tuple-element.55), channel_id=1, replica_groups=mesh['gx'=16,'gy'=4,'gz'=4] {'gy','gz'}, dimensions={0} | all-to-all | bytes 262144 | tf_op jit(solution)/shard_map/all_to_all | solution.py:379
  185.0 0.6 shard_map.124
  185.6 18.4 %all_to_all.46.refs_1_ = f32[16,24,128]{2,1,0:T(8,128)S(1)} all-to-all(f32[16,24,128]{2,1,0:T(8,128)S(1)} %get-tuple-element.56), channel_id=1, replica_groups=mesh['gx'=16,'gy'=4,'gz'=4] {'gx'}, dimensions={0} | all-to-all | bytes 393216 | tf_op jit(solution)/shard_map/all_to_all | solution.py:427
  204.0 4.5 %shard_map.125 = (f32[3,2,2,2,128]{4,3,2,1,0:T(2,128)}, f32[2]{0:T(128)}) custom-call(s32[5]{0:T(128)S(1)} %pad_add_fusion.idx.refs_0_, f32[16,24,128]{2,1,0:T(8,128)S(1)} %all_to_all.46.refs_1_, f32[16,128]{1,0:T(8,128)S(1)} %get-tuple-element.57.refs_2_, f32[16,128]{1,0:T(8,128)S(1)} %get-tuple-element.58.refs_3_, ...), custom_call_target="tpu_custom_call" | custom-call | tf_op jit(solution)/shard_map/pallas_call | solution.py:433
  (18 shorter events, 0.1 us)
Async XLA Ops:
  1.3 0.7 copy-start.4
  2.0 0.7 copy-start.5
  2.6 0.7 copy-start.6
  3.3 0.7 copy-start.7
  4.6 14.4 %collective-permute-start.1 = (f32[8,128]{1,0:T(8,128)S(1)}, f32[8,128]{1,0:T(8,128)S(1)}, u32[]{:S(2)}, u32[]{:S(2)}) collective-permute-start(f32[8,128]{1,0:T(8,128)S(1)} %get-tuple-element.33), channel_id=1, source_target_pairs={{16,0},{32,16},{48,32},{64,48},{80,64},{96,80},{112,96},{128,112},... | collective-permute-start | bytes 12296 | tf_op jit(solution)/shard_map/ppermute | solution.py:382
  5.9 13.1 %collective-permute-start = (f32[8,128]{1,0:T(8,128)S(1)}, f32[8,128]{1,0:T(8,128)S(1)}, u32[]{:S(2)}, u32[]{:S(2)}) collective-permute-start(f32[8,128]{1,0:T(8,128)S(1)} %get-tuple-element.33), channel_id=1, source_target_pairs={{0,16},{16,32},{32,48},{48,64},{64,80},{80,96},{96,112},{112,128},... | collective-permute-start | bytes 12296 | tf_op jit(solution)/shard_map/ppermute | solution.py:382
  10.5 15.7 %all-to-all-start = ((f32[16,8,128]{2,1,0:T(8,128)}), f32[16,8,128]{2,1,0:T(8,128)S(1)}, u32[]{:S(2)}, u32[]{:S(2)}) async-start(f32[16,8,128]{2,1,0:T(8,128)} %get-tuple-element.32), calls=%async_computation | async-start | bytes 131072 | tf_op jit(solution)/shard_map/all_to_all | solution.py:379
  26.3 0.7 copy-start
  27.0 0.7 copy-start.1
  27.7 0.7 copy-start.2
  44.7 4.5 %collective-permute-start.2 = (f32[16,8,128]{2,1,0:T(8,128)S(1)}, f32[16,8,128]{2,1,0:T(8,128)S(1)}, u32[]{:S(2)}, u32[]{:S(2)}) collective-permute-start(f32[16,8,128]{2,1,0:T(8,128)S(1)} %get-tuple-element.34.p2), channel_id=1, source_target_pairs={{0,16},{16,32},{32,48},{48,64},{64,80},{80,96},{96,112},{112,128},... | collective-permute-start | bytes 196616 | tf_op jit(solution)/shard_map/ppermute | solution.py:382
  47.9 5.1 %collective-permute-start.3 = (f32[16,8,128]{2,1,0:T(8,128)S(1)}, f32[16,8,128]{2,1,0:T(8,128)S(1)}, u32[]{:S(2)}, u32[]{:S(2)}) collective-permute-start(f32[16,8,128]{2,1,0:T(8,128)S(1)} %get-tuple-element.35.p1), channel_id=1, source_target_pairs={{16,0},{32,16},{48,32},{64,48},{80,64},{96,80},{112,96},{128,112},... | collective-permute-start | bytes 196616 | tf_op jit(solution)/shard_map/ppermute | solution.py:382
  53.0 0.7 copy-start.3
  84.7 5.3 %collective-permute-start.4 = (f32[16,128]{1,0:T(8,128)S(1)}, f32[16,128]{1,0:T(8,128)S(1)}, u32[]{:S(2)}, u32[]{:S(2)}) collective-permute-start(f32[16,128]{1,0:T(8,128)S(1)} %get-tuple-element.37.p2), channel_id=1, source_target_pairs={{0,16},{16,32},{32,48},{48,64},{64,80},{80,96},{96,112},{112,128},... | collective-permute-start | bytes 24584 | tf_op jit(solution)/shard_map/ppermute | solution.py:382
  88.7 4.4 %collective-permute-start.5 = (f32[16,128]{1,0:T(8,128)S(1)}, f32[16,128]{1,0:T(8,128)S(1)}, u32[]{:S(2)}, u32[]{:S(2)}) collective-permute-start(f32[16,128]{1,0:T(8,128)S(1)} %get-tuple-element.38.p1), channel_id=1, source_target_pairs={{16,0},{32,16},{48,32},{64,48},{80,64},{96,80},{112,96},{128,112},... | collective-permute-start | bytes 24584 | tf_op jit(solution)/shard_map/ppermute | solution.py:382
  110.6 4.3 %collective-permute-start.6 = (f32[16,4,128]{2,1,0:T(4,128)S(1)}, f32[16,4,128]{2,1,0:T(4,128)S(1)}, u32[]{:S(2)}, u32[]{:S(2)}) collective-permute-start(f32[16,4,128]{2,1,0:T(4,128)S(1)} %get-tuple-element.43.refs_2_), channel_id=1, source_target_pairs={{0,16},{16,32},{32,48},{48,64},{64,80},{80,96},{96,112},{112,128},... | collective-permute-start | bytes 98312 | tf_op jit(solution)/shard_map/ppermute | solution.py:382
  113.7 4.9 %collective-permute-start.7 = (f32[16,4,128]{2,1,0:T(4,128)S(1)}, f32[16,4,128]{2,1,0:T(4,128)S(1)}, u32[]{:S(2)}, u32[]{:S(2)}) collective-permute-start(f32[16,4,128]{2,1,0:T(4,128)S(1)} %get-tuple-element.44.refs_1_), channel_id=1, source_target_pairs={{16,0},{32,16},{48,32},{64,48},{80,64},{96,80},{112,96},{128,112},... | collective-permute-start | bytes 98312 | tf_op jit(solution)/shard_map/ppermute | solution.py:382
  134.7 5.2 %collective-permute-start.8 = (f32[16,128]{1,0:T(8,128)S(1)}, f32[16,128]{1,0:T(8,128)S(1)}, u32[]{:S(2)}, u32[]{:S(2)}) collective-permute-start(f32[16,128]{1,0:T(8,128)S(1)} %get-tuple-element.48.p2), channel_id=1, source_target_pairs={{0,16},{16,32},{32,48},{48,64},{64,80},{80,96},{96,112},{112,128},... | collective-permute-start | bytes 24584 | tf_op jit(solution)/shard_map/ppermute | solution.py:382
  138.5 4.4 %collective-permute-start.9 = (f32[16,128]{1,0:T(8,128)S(1)}, f32[16,128]{1,0:T(8,128)S(1)}, u32[]{:S(2)}, u32[]{:S(2)}) collective-permute-start(f32[16,128]{1,0:T(8,128)S(1)} %get-tuple-element.49.p1), channel_id=1, source_target_pairs={{16,0},{32,16},{48,32},{64,48},{80,64},{96,80},{112,96},{128,112},... | collective-permute-start | bytes 24584 | tf_op jit(solution)/shard_map/ppermute | solution.py:382
  160.5 4.5 %collective-permute-start.10 = (f32[16,4,128]{2,1,0:T(4,128)S(1)}, f32[16,4,128]{2,1,0:T(4,128)S(1)}, u32[]{:S(2)}, u32[]{:S(2)}) collective-permute-start(f32[16,4,128]{2,1,0:T(4,128)S(1)} %get-tuple-element.50.refs_2_), channel_id=1, source_target_pairs={{0,16},{16,32},{32,48},{48,64},{64,80},{80,96},{96,112},{112,128},... | collective-permute-start | bytes 98312 | tf_op jit(solution)/shard_map/ppermute | solution.py:382
  163.7 5.3 %collective-permute-start.11 = (f32[16,4,128]{2,1,0:T(4,128)S(1)}, f32[16,4,128]{2,1,0:T(4,128)S(1)}, u32[]{:S(2)}, u32[]{:S(2)}) collective-permute-start(f32[16,4,128]{2,1,0:T(4,128)S(1)} %get-tuple-element.51.refs_1_), channel_id=1, source_target_pairs={{16,0},{32,16},{48,32},{64,48},{80,64},{96,80},{112,96},{128,112},... | collective-permute-start | bytes 98312 | tf_op jit(solution)/shard_map/ppermute | solution.py:382

commit v2 on v1

v2 whole, which is shorter than its diff:
```python
import math

import jax
import jax.numpy as jnp
from jax import lax
from jax.experimental import pallas as pl
from jax.experimental.pallas import tpu as pltpu
from jax.sharding import Mesh
from jax.sharding import PartitionSpec as P

ITERS = 2
GROUP = ("gx1", "gy", "gz")
F32 = jnp.float32
BF16 = jnp.bfloat16

kernel_var = 0.25
time_step = 2.0
particle_mass = 1.0 / 45.0
rest_density = 1.0
relaxation = 0.5
floor_value = 0.1
gravity = 0.1

KAPPA = math.log2(math.e) / kernel_var
YSCALE = math.sqrt(2.0 * KAPPA)
GRAD = 2.0 / kernel_var
ABSENT = 30000.0
PADDED = ((-1, 1), (0, 0), (0, 1), (1, 0))
VMEM = pl.BlockSpec(memory_space=pltpu.VMEM)
SMEM = pl.BlockSpec(memory_space=pltpu.SMEM)


def rows_iota(shape):
    return lax.broadcasted_iota(jnp.int32, shape, 0)


def split3(x):
    h = x.astype(BF16).astype(F32)
    m = (x - h).astype(BF16).astype(F32)
    return h, m, x - h - m


def stacked(x):
    h, m, l = split3(x)
    return jnp.concatenate([h, m, l, jnp.zeros_like(x)], 0).astype(BF16)


def unstacked(acc):
    return acc[0:8] + acc[8:16] + acc[16:24]


def dot(a, b):
    return jnp.dot(a, b, preferred_element_type=F32)


def plane_source(dy, dz):
    ny, nz = lax.axis_size("gy"), lax.axis_size("gz")
    y, z = lax.axis_index("gy"), lax.axis_index("gz")
    ok = (y + dy >= 0) & (y + dy < ny) & (z + dz >= 0) & (z + dz < nz)
    return jnp.where(ok, (y + dy) * nz + z + dz, y * nz + z), ok


def plane_start(other):
    g = lax.axis_index("gx1")
    return (1 - g if other else g) * (lax.axis_size("gy") * lax.axis_size("gz"))


def outer_x(x):
    g = lax.axis_index("gx1")
    return g if x == 0 else 1 - g


def pack_kernel(count, pos, vel, heading, cell, send, one):
    lane = lax.broadcasted_iota(jnp.int32, (1, 128), 1)
    code = jnp.where(lane < count[0, 0, 0], heading[0, 0] * 8 + cell[0, 0] + 1, 0).astype(F32)
    one[0:1, :] = code
    for f in range(3):
        one[1 + f : 2 + f, :] = pos[f, 0, 0]
        one[4 + f : 5 + f, :] = vel[f, 0, 0]
    one[7:8, :] = jnp.zeros((1, 128), F32)
    tile = one[...]
    for p in range(send.shape[0]):
        send[p] = tile


def prepare_kernel(pos, vel, pprev, counts, base, before, filled):
    lane2 = lax.broadcasted_iota(jnp.int32, (1, 2), 1)
    for c in range(8):
        x, y, z = outer_x(c // 4), c // 2 % 2, c % 2
        base[c, 0:1, :] = jnp.zeros((1, 128), F32)
        base[c, 7:8, :] = jnp.zeros((1, 128), F32)
        for f in range(3):
            base[c, 1 + f : 2 + f, :] = pos[f, x, y, z : z + 1, :]
            base[c, 4 + f : 5 + f, :] = vel[f, x, y, z : z + 1, :]
        before[c : c + 1, :] = pprev[x, y, z : z + 1, :]
        pair = counts[x, y : y + 1, :].astype(F32)
        count = jnp.sum(jnp.where(lane2 == z, pair, 0.0), 1, keepdims=True)
        filled[c : c + 1, :] = jnp.broadcast_to(count, (1, 128))


def fill_chunks(send, cell_of, rows):
    def put(p, cells):
        for k, c in enumerate(cells):
            if rows:
                send[p, k] = cell_of(c)
            else:
                send[p, k : k + 1, :] = cell_of(c)

    for p in range(send.shape[0]):
        put(p, range(4, 8))
    here = plane_start(False)
    for dy in (-1, 0, 1):
        for dz in (-1, 0, 1):
            if dy or dz:
                src, _ = plane_source(dy, dz)
                face = max(dz if dz else dy, 0)
                cells = [x * 4 + (k * 2 + face if dz else face * 2 + k) for x in range(2) for k in range(2)]
                put(here + src, cells)


def gather_kernel(recv, mine, l1, l2, near, far=None):
    here, there = plane_start(False), plane_start(True)
    whole = len(mine.shape) == 3

    def read(ref, p, k):
        return ref[p, k] if whole else ref[p, k : k + 1, :]

    for yp, (dy, y) in enumerate(PADDED):
        for zp, (dz, z) in enumerate(PADDED):
            src, ok = plane_source(dy, dz)
            q = yp * 4 + zp
            outs = [(near, jnp.where(ok, read(recv, there + src, y * 2 + z), 0.0))]
            if far is not None:
                outs.append((far, jnp.where(ok, read(recv, there + src, 4 + y * 2 + z), 0.0)))
            for x, out in enumerate((l1, l2)):
                if dy == 0 and dz == 0:
                    c = x * 4 + y * 2 + z
                    value = mine[c] if whole else mine[c : c + 1, :]
                else:
                    value = jnp.where(ok, read(recv, here + src, x * 2 + (y if dz else z)), 0.0)
                outs.append((out, value))
            for out, value in outs:
                if whole:
                    out[q] = value
                else:
                    out[q : q + 1, :] = value


def gather_last_kernel(recv, mine, send, l1, l2, near, far):
    gather_kernel(recv, mine, l1, l2, near, far)
    totals = recv[0, 8:16, :]
    for p in range(1, recv.shape[0]):
        totals = totals + recv[p, 8:16, :]
    layer = far[...]
    for p in range(send.shape[0]):
        send[p, 0:16, :] = layer
        send[p, 16:24, :] = totals


def insert_kernel(recv, beyond, base, counts, send, state):
    row = rows_iota((8, 128))
    lanef = lax.broadcasted_iota(jnp.int32, (8, 128), 1).astype(F32)
    here, there = plane_start(False), plane_start(True)
    g = lax.axis_index("gx1")
    cell = row + 4 * g - jnp.where(row >= 4, 8 * g, 0)
    cargos, marks = [], []
    for d in range(6):
        step = -1 if d % 2 == 0 else 1
        if d < 2:
            src, ok = plane_source(0, 0)
            tile = jnp.where(g == d, beyond[...], recv[there + src])
        else:
            src, ok = plane_source(step if d < 4 else 0, step if d >= 4 else 0)
            tile = recv[here + src]
        mark = (tile[0:1] == (cell + (d * 8 + 1)).astype(F32)) & ok
        cargos.append(stacked(tile))
        marks.append(jnp.where(mark, 1.0, 0.0))
    marked = jnp.concatenate(marks, 0).astype(BF16)
    r128 = rows_iota((128, 128))
    c128 = lax.broadcasted_iota(jnp.int32, (128, 128), 1)
    earlier = dot(marked, jnp.where(r128 < c128, 1.0, 0.0).astype(BF16))
    total = dot(marked, jnp.ones((128, 128), BF16))
    filled = counts[...]
    grown = filled
    targets = []
    for d in range(6):
        targets.append(jnp.where(marks[d] > 0, earlier[d * 8 : d * 8 + 8] + grown, -1.0))
        grown = grown + total[d * 8 : d * 8 + 8]
    slot = r128.astype(F32)
    for c in range(8):
        acc = jnp.zeros((32, 128), F32)
        for d in range(6):
            hot = jnp.where(slot == targets[d][c : c + 1], 1.0, 0.0).astype(BF16)
            acc = acc + lax.dot_general(
                cargos[d], hot, (((1,), (1,)), ((), ())), preferred_element_type=F32
            )
        tile = jnp.where(lanef < filled[c : c + 1], base[c], unstacked(acc))
        occ = lanef < grown[c : c + 1]
        tile = jnp.where(row == 0, 1.0, jnp.where(row == 7, 0.0, tile))
        state[c] = jnp.where(occ, tile, 0.0)
    fill_chunks(send, lambda c: state[c], True)


def column_features(xy, z, tile, xs, ys, xr, at, ft):
    row = rows_iota((8, 128))
    axis_row = (row >= 1) & (row <= 3)
    occ = tile[0:1]
    shift = jnp.where(row == 1, xs, jnp.where(row == 2, ys, jnp.where(row == 3, z - 2.0, 0.0)))
    st = (tile + shift) * occ
    xr[xy * 4 + z] = jnp.where(row < 4, st, 0.0)
    vx = jnp.sum(jnp.where(axis_row, st * pltpu.roll(st, 5, 0), 0.0), 0, keepdims=True)
    ft[xy, :, z * 128 : z * 128 + 128] = stacked(jnp.where(row == 7, vx, st))
    y = jnp.where(axis_row, st * YSCALE, 0.0)
    h, m, l = split3(y)
    qh, qm, ql = split3(jnp.where(occ > 0, 0.5 * jnp.sum(y * y, 0, keepdims=True), ABSENT))
    ones_rows = jnp.where((row >= 3) & (row < 6), 1.0, 0.0)
    qcol = jnp.where(row == 0, qh, jnp.where(row == 1, qm, jnp.where(row == 2, ql, ones_rows)))
    side = jnp.concatenate([h, h, m, m, h, l, qcol, jnp.zeros((8, 128), F32)], 0)
    at[xy, z * 128 : z * 128 + 128, :] = side.T.astype(BF16)
    return st


def centre_side(st):
    row = rows_iota((8, 128))
    y = jnp.where((row >= 1) & (row <= 3), st * YSCALE, 0.0)
    h, m, l = split3(y)
    qh, qm, ql = split3(0.5 * jnp.sum(y * y, 0, keepdims=True))
    minus_rows = jnp.where(row < 3, -1.0, 0.0)
    qrow = jnp.where(row == 3, -qh, jnp.where(row == 4, -qm, jnp.where(row == 5, -ql, minus_rows)))
    return jnp.concatenate([h, m, h, m, l, h, qrow, jnp.zeros((8, 128), F32)], 0).astype(BF16)


def weigh(side, b, put):
    inner = dot(side(128, 384), b)
    pieces = (
        (0, 0, dot(side(0, 128), b[:, 0:128])),
        (0, 128, inner[:, 0:128]),
        (1, 0, inner[:, 128:256]),
        (1, 256, dot(side(384, 512), b[:, 128:256])),
    )
    sums = [jnp.zeros((8, 128), F32), jnp.zeros((8, 128), F32)]
    for cz, k, e in pieces:
        w = jnp.exp2(e)
        hi = w.astype(BF16)
        put(cz, k, k + e.shape[0], hi, (w - hi.astype(F32)).astype(BF16))
        sums[cz] = sums[cz] + jnp.sum((w * w * e).reshape(e.shape[0] // 8, 8, 128), 0)
    return sums


def main_columns(cx):
    if cx == 0:
        return [(k, k // 3, k % 3) for k in range(6)]
    return [(6 + k, k // 3, k % 3) for k in range(9)]


def setup_main_kernel(l1, l2, near, whi, wlo, xr, own, bside, part, gpart, at, bi, ft):
    g = lax.axis_index("gx1")
    for x, ref in enumerate((l1, l2, near)):
        xs = jnp.where(g == 0, x - 1.0, -1.0 * x)

        def column(y, carry, x=x, ref=ref, xs=xs):
            for z in range(4):
                column_features(x * 4 + y, z, ref[y * 4 + z], xs, (y - 2).astype(F32), xr, at, ft)
            return carry

        lax.fori_loop(0, 4, column, 0)
    row = rows_iota((8, 128))
    for c in range(8):
        cx, cy, cz = c // 4, c // 2 % 2, c % 2
        tile = (l1, l2)[cx][(cy + 1) * 4 + cz + 1]
        xs = jnp.where(g == 0, cx - 1.0, -1.0 * cx)
        shift = jnp.where(row == 1, xs, jnp.where(row == 2, cy - 1.0, jnp.where(row == 3, cz - 1.0, 0.0)))
        st = (tile + shift) * tile[0:1]
        own[c] = st
        bi[c // 2, :, cz * 128 : cz * 128 + 128] = centre_side(st)
    bside[...] = bi[0:2]

    def weights(cy, carry):
        for cx in range(2):
            b = bi[cx * 2 + cy]
            sums = [jnp.zeros((8, 128), F32), jnp.zeros((8, 128), F32)]
            for k, x, y in main_columns(cx):
                xy = x * 4 + cy + y

                def put(cz, lo, hi, a, b, k=k):
                    whi[cy, cz, k, lo:hi, :] = a
                    wlo[cy, cz, k, lo:hi, :] = b

                more = weigh(lambda lo, hi, xy=xy: at[xy, lo:hi, :], b, put)
                sums = [p + q for p, q in zip(sums, more)]
            for cz in range(2):
                gpart[(cx * 2 + cy) * 2 + cz] = sums[cz]
        return carry

    lax.fori_loop(0, 2, weights, 0)
    main_pass(whi, wlo, ft, part)


def main_pass(whi, wlo, ft, part):
    def centre(cy, carry):
        for cx in range(2):
            for cz in range(2):
                acc = jnp.zeros((32, 128), F32)
                for k, x, y in main_columns(cx):
                    f = ft[x * 4 + cy + y, :, cz * 128 : cz * 128 + 384]
                    acc = acc + dot(f, whi[cy, cz, k]) + dot(f, wlo[cy, cz, k])
                part[(cx * 2 + cy) * 2 + cz] = unstacked(acc)
        return carry

    lax.fori_loop(0, 2, centre, 0)


def beyond_pass(whi, wlo, ft, part, finish):
    for c in range(8):
        cx, cy, cz = c // 4, c // 2 % 2, c % 2
        r = part[c]
        if cx == 0:
            acc = jnp.zeros((32, 128), F32)
            for y in range(3):
                f = ft[cy + y, :, cz * 128 : cz * 128 + 384]
                acc = acc + dot(f, whi[cy, cz, y]) + dot(f, wlo[cy, cz, y])
            r = r + unstacked(acc)
        finish(c, r)


def setup_beyond_kernel(beyond, own, bside, part, gpart, counts, pprev, whi, wlo, xr, grad, aux, press, send, srow, at, ft, gsq):
    g = lax.axis_index("gx1")
    row = rows_iota((8, 128))
    axis_row = (row >= 1) & (row <= 3)
    xs = jnp.where(g == 0, -2.0, 1.0)
    for y in range(4):
        for z in range(4):
            column_features(y, z, beyond[y * 4 + z], xs, y - 2.0, xr, at, ft)
    gsq[...] = gpart[...]
    for cy in range(2):
        for y in range(3):

            def put(cz, lo, hi, a, b, cy=cy, y=y):
                whi[cy, cz, y, lo:hi, :] = a
                wlo[cy, cz, y, lo:hi, :] = b

            more = weigh(lambda lo, hi, xy=cy + y: at[xy, lo:hi, :], bside[cy], put)
            for cz in range(2):
                gsq[cy * 2 + cz] = gsq[cy * 2 + cz] + more[cz]

    def finish(c, r):
        st = own[c]
        occ = st[0:1] > 0
        s0 = r[0:1]
        gr = jnp.where(axis_row, st * s0 - r, 0.0)
        grad[c] = gr
        density = particle_mass * s0
        pair = pltpu.roll(st, 5, 0) * gr - st * pltpu.roll(r, 5, 0)
        divergence = (-GRAD * particle_mass) * (
            jnp.sum(jnp.where(axis_row, pair, 0.0), 0, keepdims=True) + r[7:8]
        )
        grad_norm = (GRAD * particle_mass) ** 2 * jnp.sum(gr * gr, 0, keepdims=True)
        grad_square = (-GRAD * GRAD * particle_mass / KAPPA) * jnp.sum(gsq[c], 0, keepdims=True)
        safe = jnp.where(occ, density, 1.0)
        safe2 = safe * safe
        source = jnp.where(occ, rest_density - (density + time_step * divergence), 0.0)
        weight = jnp.where(occ, particle_mass, 0.0)
        diagonal = jnp.maximum(
            time_step * time_step * (grad_norm + weight * grad_square) / safe2, floor_value
        )
        lane = lax.broadcasted_iota(jnp.int32, (1, 128), 1).astype(F32)
        pressure = jnp.where(lane < counts[c : c + 1, :], pprev[c : c + 1, :], 0.0)
        aux[c, 0:1, :] = safe2
        aux[c, 1:2, :] = source
        aux[c, 2:3, :] = diagonal
        press[c : c + 1, :] = pressure
        srow[c : c + 1, :] = jnp.where(occ, pressure / safe2, 0.0)

    beyond_pass(whi, wlo, ft, part, finish)
    fill_chunks(send, lambda c: srow[c : c + 1, :], False)


def scaled_features(layer, base, xr, ft):
    for y in range(4):
        for z in range(4):
            q = y * 4 + z
            ft[base // 4 + y, :, z * 128 : z * 128 + 128] = stacked(layer[q : q + 1, :] * xr[base + q])


def accel_features(layer, base, xr, ft):
    row = rows_iota((8, 128))
    axis_row = (row >= 1) & (row <= 3)
    zeros4 = jnp.zeros((4, 128), F32)
    for y in range(4):
        for z in range(4):
            q = y * 4 + z
            a = jnp.concatenate([layer[q], zeros4], 0)
            ax = jnp.sum(jnp.where(axis_row, a * xr[base + q], 0.0), 0, keepdims=True)
            ft[base // 4 + y, :, z * 128 : z * 128 + 128] = stacked(jnp.where(row == 0, ax, a))


def main_kernel(l1, l2, near, xr, whi, wlo, part, ft, *, features):
    for x, layer in enumerate((l1, l2, near)):
        features(layer, x * 16, xr, ft)
    main_pass(whi, wlo, ft, part)


def own_row(c):
    return (c // 2 % 2 + 1) * 4 + c % 2 + 1


def accel_of(c, r, l1, l2, xr, grad):
    q = own_row(c)
    s = (l1, l2)[c // 4][q : q + 1, :]
    return (GRAD * particle_mass) * (s * grad[c] + xr[c // 4 * 16 + q] * r[0:1] - r)


def accel_kernel(beyond, xrb, whi, wlo, part, l1, l2, xr, grad, send, mine, ft):
    scaled_features(beyond, 0, xrb, ft)

    def finish(c, r):
        mine[c] = accel_of(c, r, l1, l2, xr, grad)[0:4]

    beyond_pass(whi, wlo, ft, part, finish)
    fill_chunks(send, lambda c: mine[c], True)


def apply_kernel(beyond, xrb, whi, wlo, part, l1, l2, xr, grad, aux, press, errs, pnew, enew, send, mine, ft, *, at_iter, last):
    row = rows_iota((8, 128))
    axis_row = (row >= 1) & (row <= 3)
    zeros4 = jnp.zeros((4, 128), F32)
    accel_features(beyond, 0, xrb, ft)
    enew[...] = jnp.zeros((8, 128), F32) if errs is None else errs[...]

    def finish(c, r):
        q = own_row(c)
        a = jnp.concatenate([(l1, l2)[c // 4][q], zeros4], 0)
        x = xr[c // 4 * 16 + q]
        inner = jnp.sum(jnp.where(axis_row, a * grad[c] - x * r, 0.0), 0, keepdims=True) + r[0:1]
        applied = (-time_step * time_step * GRAD * particle_mass) * inner
        occ = x[0:1] > 0
        safe2, source, diagonal = (aux[c, k : k + 1, :] for k in range(3))
        residual = jnp.where(occ, source - applied, 0.0)
        enew[at_iter : at_iter + 1, :] = enew[at_iter : at_iter + 1, :] + jnp.abs(residual)
        p = press[c : c + 1, :]
        p = jnp.where(occ, jnp.maximum(p + relaxation * (applied - source) / diagonal, 0.0), 0.0)
        if last:
            pnew[outer_x(c // 4), c // 2 % 2, c % 2 : c % 2 + 1, :] = p
        else:
            pnew[c : c + 1, :] = p
        mine[c : c + 1, :] = jnp.where(occ, p / safe2, 0.0)

    beyond_pass(whi, wlo, ft, part, finish)
    fill_chunks(send, lambda c: mine[c : c + 1, :], False)
    if last:
        first, totals = mine[0:4, :], enew[...]
        for p in range(send.shape[0]):
            send[p, 4:8, :] = first
            send[p, 8:16, :] = totals


def final_kernel(recv, xrb, whi, wlo, part, l1, l2, xr, grad, state, vout, eout, beyond, ft, *, slots):
    n = recv.shape[0]
    totals = recv[0, 16:24, :]
    for p in range(1, n):
        totals = totals + recv[p, 16:24, :]
    for it in range(ITERS):
        eout[it] = jnp.sum(totals[it : it + 1, :]) / slots
    src = lax.axis_index("gx0") + 2 * lax.axis_index("gx1") - 1
    ok = (src >= 0) & (src < n)
    beyond[...] = jnp.where(ok, recv[jnp.where(ok, src, 0), 0:16, :], 0.0)
    scaled_features(beyond, 0, xrb, ft)
    row = rows_iota((8, 128))

    def finish(c, r):
        a = accel_of(c, r, l1, l2, xr, grad)
        st = state[c]
        pulled = a - jnp.where(row == 3, gravity, 0.0)
        v = pltpu.roll(st, 5, 0) + time_step * pulled
        v = jnp.where(st[0:1] > 0, v, 0.0)
        for f in range(3):
            vout[f, outer_x(c // 4), c // 2 % 2, c % 2 : c % 2 + 1, :] = v[1 + f : 2 + f]

    beyond_pass(whi, wlo, ft, part, finish)


def call(body, outs, operands, scratch=(), limit=12 << 20, flops=0, first=None, **static):
    def named(*refs):
        body(*refs, **static)

    specs = [VMEM] * len(operands)
    if first is not None:
        specs[0] = first
    return pl.pallas_call(
        named,
        out_shape=outs,
        in_specs=specs,
        out_specs=jax.tree.map(lambda o: SMEM if o.shape == (ITERS,) else VMEM, outs),
        scratch_shapes=list(scratch),
        compiler_params=pltpu.CompilerParams(vmem_limit_bytes=limit),
        cost_estimate=pl.CostEstimate(flops=flops, transcendentals=0, bytes_accessed=0) if flops else None,
    )(*operands)


def sds(*shape, dtype=F32):
    return jax.ShapeDtypeStruct(shape, dtype)


def on_device(positions, velocities, pressure_prev, counts, out_positions, out_velocities, out_dir, out_cell, out_count):
    pairs, plane = lax.axis_size("gx0"), lax.axis_size("gy") * lax.axis_size("gz")
    group = 2 * plane
    across = [(2 * j + 1, 2 * j + 2) for j in range(pairs - 1)]
    across = across + [(b, a) for a, b in across]
    busy = 4 * 10**9

    def spread(send):
        return lax.all_to_all(send, GROUP, 0, 0)

    def from_beyond(layer):
        return lax.ppermute(layer, ("gx0", "gx1"), across)

    def layers(send, mine, shape):
        return call(gather_kernel, (sds(16, *shape),) * 3, (spread(send), mine))

    def features(columns):
        return pltpu.VMEM((columns, 32, 512), BF16)

    tiles, rows = sds(8, 8, 128), sds(8, 128)
    send, one = call(
        pack_kernel,
        (sds(group, 8, 128), rows),
        (out_count, out_positions, out_velocities, out_dir, out_cell),
        limit=60 * 1024 * 1024,
        first=SMEM,
    )
    base, before, filled = call(
        prepare_kernel, (tiles, rows, rows), (positions, velocities, pressure_prev, counts), flops=busy // 4
    )
    send, state = call(insert_kernel, (sds(group, 4, 8, 128), tiles), (spread(send), from_beyond(one), base, filled))
    l1, l2, near = layers(send, state, (8, 128))
    beyond = from_beyond(l1)
    wmain, wside = sds(2, 2, 15, 384, 128, dtype=BF16), sds(2, 2, 3, 384, 128, dtype=BF16)
    whi, wlo, xr, own, bside, part, gpart = call(
        setup_main_kernel,
        (wmain, wmain, sds(48, 8, 128), tiles, sds(2, 64, 256, dtype=BF16), tiles, tiles),
        (l1, l2, near),
        [pltpu.VMEM((12, 512, 64), BF16), pltpu.VMEM((4, 64, 256), BF16), features(12)],
        flops=3 * busy,
    )
    bhi, blo, xrb, grad, aux, press, send, mine = call(
        setup_beyond_kernel,
        (wside, wside, sds(16, 8, 128), tiles, tiles, rows, sds(group, 4, 128), rows),
        (beyond, own, bside, part, gpart, filled, before),
        [pltpu.VMEM((4, 512, 64), BF16), features(4), pltpu.VMEM((8, 8, 128), F32)],
    )
    errs = None
    for it in range(ITERS):
        last = it == ITERS - 1
        l1, l2, near = layers(send, mine, (128,))
        beyond = from_beyond(l1)
        (part,) = call(
            main_kernel, (tiles,), (l1, l2, near, xr, whi, wlo), [features(12)], flops=busy, features=scaled_features
        )
        send, mine = call(
            accel_kernel,
            (sds(group, 4, 4, 128), sds(8, 4, 128)),
            (beyond, xrb, bhi, blo, part, l1, l2, xr, grad),
            [features(4)],
        )
        l1, l2, near = layers(send, mine, (4, 128))
        beyond = from_beyond(l1)
        (part,) = call(
            main_kernel, (tiles,), (l1, l2, near, xr, whi, wlo), [features(12)], flops=busy, features=accel_features
        )

        def body(*refs, it=it, last=last):
            refs = refs if it else (*refs[:11], None, *refs[11:])
            apply_kernel(*refs, at_iter=it, last=last)

        operands = (beyond, xrb, bhi, blo, part, l1, l2, xr, grad, aux, press) + (() if it == 0 else (errs,))
        press, errs, send, mine = call(
            body,
            (sds(2, 2, 2, 128) if last else rows, rows, sds(group, 16 if last else 4, 128), rows),
            operands,
            [features(4)],
        )
    send, l1, l2, near, _ = call(
        gather_last_kernel, (sds(pairs, 24, 128),) + (sds(16, 128),) * 4, (spread(send), mine)
    )
    recv = lax.all_to_all(send, "gx0", 0, 0)
    (part,) = call(
        main_kernel, (tiles,), (l1, l2, near, xr, whi, wlo), [features(12)], flops=busy, features=scaled_features
    )
    velocity_new, density_error = call(
        final_kernel,
        (sds(3, 2, 2, 2, 128), sds(ITERS)),
        (recv, xrb, bhi, blo, part, l1, l2, xr, grad, state),
        [pltpu.VMEM((16, 128), F32), features(4)],
        slots=pairs * group * 8 * 128,
    )
    return press, velocity_new, density_error


def solution(mesh):
    nx, ny, nz = (mesh.shape[a] for a in ("gx", "gy", "gz"))
    paired = Mesh(mesh.devices.reshape(nx // 2, 2, ny, nz), ("gx0", "gx1", "gy", "gz"))
    gx = ("gx0", "gx1")
    cells = P(gx, "gy", "gz", None)
    vectors = P(None, gx, "gy", "gz", None)
    ints = P(gx, "gy", "gz")
    return jax.shard_map(
        on_device,
        mesh=paired,
        in_specs=(vectors, vectors, cells, ints, vectors, vectors, cells, cells, ints),
        out_specs=(cells, vectors, P()),
        check_vma=False,
    )
```

time: 209 us -> 163 us (0.78)
  waiting for transfers between devices: 24.8 us -> 3.98 us
  starting transfers between devices: 38 us -> 21.7 us
  Pallas kernels: 42 us -> 28.2 us
  local copies, waits for them, and re-layouts: 5.45 us -> 8.13 us
    ppermute x12 -> x6, starting transfers between devices: 29.7 us -> 4.16 us  [from_beyond(): return lax.ppermute(layer, ('gx0', 'gx1'), across)]
    ppermute x12 -> x6, waiting for transfers between devices: 17.5 us -> 0.02 us  [from_beyond(): return lax.ppermute(layer, ('gx0', 'gx1'), across)]
    pallas_call x14 -> x21, Pallas kernels: 42 us -> 28.2 us  [call(): pl.pallas_call(named, out_shape=outs, in_specs=specs, out_specs=jax.tree....]
    all_to_all x1 -> x2, starting transfers between devices: 8.35 us -> 17.5 us  [the longest x1 8.94 us: on_device(): recv = lax.all_to_all(send, 'gx0', 0, 0)]
    all_to_all x1 -> x2, waiting for transfers between devices: 7.28 us -> 3.97 us  [the longest x1 3.96 us: spread(): return lax.all_to_all(send, GROUP, 0, 0)]
    unnamed x16, local copies, waits for them, and re-layouts: 5.44 us -> 8.13 us
    all_to_all x7 -> x6, blocking collectives: 96.6 us -> 98.5 us  [spread(): return lax.all_to_all(send, GROUP, 0, 0)]
  transfers between devices with their start and end apart: 13 -> 8, of which waited for: 6 -> 1; matrix products, arithmetic and copies ran while one was open for 0% -> 0% of each run, Pallas kernels for 0% -> 12%
where the time goes in v2:
time: 163 us; the launch traced here: 162 us
  blocking collectives  98.5 us (60%)
  Pallas kernels  28.2 us (17%)
  starting transfers between devices  21.7 us (13%)
  local copies, waits for them, and re-layouts  8.13 us (5%)
  waiting for transfers between devices  3.98 us (2%)
  between operations  1.71 us (1%)
    all_to_all x6, blocking collectives, spread(): return lax.all_to_all(send, GROUP, 0, 0)  98.5 us
    pallas_call x21, Pallas kernels, call(): pl.pallas_call(named, out_shape=outs, in_specs=specs, out_specs=jax.tree....  28.2 us
    all_to_all x1, starting transfers between devices, on_device(): recv = lax.all_to_all(send, 'gx0', 0, 0)  8.94 us
    all_to_all x1, starting transfers between devices, spread(): return lax.all_to_all(send, GROUP, 0, 0)  8.58 us
    unnamed x16, local copies, waits for them, and re-layouts  8.13 us
    ppermute x6, starting transfers between devices, from_beyond(): return lax.ppermute(layer, ('gx0', 'gx1'), across)  4.16 us
    all_to_all x1, waiting for transfers between devices, spread(): return lax.all_to_all(send, GROUP, 0, 0)  3.96 us
  transfers between devices with their start and end apart: 8, of which 1 were waited for; matrix products, arithmetic and copies ran while one was open for 0% of the time, Pallas kernels for 12%

profile of v2, /device:TPU:1, one launch (start us, length us, event | category | flops | bytes accessed | tf_op | source)
XLA Modules:
  0.0 162.3 jit_solution(2864128333362461560)
XLA Ops:
  1.3 1.4 shard_map.112
  2.7 8.6 %all-to-all-start = ((f32[32,8,128]{2,1,0:T(8,128)}), f32[32,8,128]{2,1,0:T(8,128)S(1)}, u32[]{:S(2)}, u32[]{:S(2)}) async-start(f32[32,8,128]{2,1,0:T(8,128)} %get-tuple-element.57), calls=%async_computation | async-start | bytes 262144 | tf_op jit(solution)/shard_map/all_to_all | solution.py:512
  11.2 0.7 collective-permute-start
  11.9 0.0 copy-start
  11.9 0.7 copy-done
  12.6 0.7 copy-done.1
  13.3 0.7 copy-done.2
  14.0 0.7 copy-done.3
  14.7 0.1 shard_map.113
  14.8 0.0 collective-permute-done.refs_1_
  14.8 4.0 %all-to-all-done.refs_0_ = f32[32,8,128]{2,1,0:T(8,128)S(1)} async-done(((f32[32,8,128]{2,1,0:T(8,128)}), f32[32,8,128]{2,1,0:T(8,128)S(1)}, u32[]{:S(2)}, u32[]{:S(2)}) %all-to-all-start) | async-done | bytes 131104 | tf_op jit(solution)/shard_map/all_to_all | solution.py:512
  18.8 1.1 shard_map.114
  19.9 17.9 %all_to_all.40.refs_0_ = f32[32,4,8,128]{3,2,1,0:T(8,128)S(1)} all-to-all(f32[32,4,8,128]{3,2,1,0:T(8,128)S(1)} %get-tuple-element.61), channel_id=1, replica_groups=mesh['gx0'=8,'gx1'=2,'gy'=4,'gz'=4] {'gx1','gy','gz'}, dimensions={0} | all-to-all | bytes 1048576 | tf_op jit(solution)/shard_map/all_to_all | solution.py:512
  37.8 0.7 collective-permute-start.1
  38.5 7.5 %shard_map.116 = (bf16[2,2,15,384,128]{4,3,2,1,0:T(8,128)(2,1)S(1)}, bf16[2,2,15,384,128]{4,3,2,1,0:T(8,128)(2,1)S(1)}, f32[48,8,128]{2,1,0:T(8,128)S(1)}, f32[8...) custom-call(f32[16,8,128]{2,1,0:T(8,128)S(1)} %get-tuple-element.63., ...), custom_call_target="tpu_custom_call" | custom-call | flops 12000000000 | tf_op jit(solution)/shard_map/pallas_call | solution.py:489
  46.0 0.0 copy-start.4
  46.0 0.0 collective-permute-done.1.refs_0_
  46.0 1.4 shard_map.117
  47.4 14.7 %all_to_all.41.refs_0_ = f32[32,4,128]{2,1,0:T(4,128)S(1)} all-to-all(f32[32,4,128]{2,1,0:T(4,128)S(1)} %get-tuple-element.71), channel_id=1, replica_groups=mesh['gx0'=8,'gx1'=2,'gy'=4,'gz'=4] {'gx1','gy','gz'}, dimensions={0} | all-to-all | bytes 131072 | tf_op jit(solution)/shard_map/all_to_all | solution.py:512
  62.1 0.7 collective-permute-start.2
  62.7 2.3 %shard_map.119.refs_4_ = f32[8,8,128]{2,1,0:T(8,128)S(1)} custom-call(f32[16,128]{1,0:T(8,128)S(1)} %get-tuple-element.73.refs_0_.refs_5_, f32[16,128]{1,0:T(8,128)S(1)} %get-tuple-element.77.refs_1_.refs_6_, f32[16,128]{1,0:T(8,128)S(1)} %get-tuple-element.78.refs_2_, f32[48,8,128]{2,1,0:T(8,128)S(1)} %get-tuple-element.79.refs_3_.refs_7_, ...), custom_call_target="tpu_custom_call" | custom-call | flops 4000000000 | tf_op jit(solution)/shard_map/pallas_call | solution.py:489
  65.1 0.0 collective-permute-done.2.refs_0_
  65.1 0.6 shard_map.120
  65.7 15.9 %all_to_all.42.refs_0_ = f32[32,4,4,128]{3,2,1,0:T(4,128)S(1)} all-to-all(f32[32,4,4,128]{3,2,1,0:T(4,128)S(1)} %get-tuple-element.83), channel_id=1, replica_groups=mesh['gx0'=8,'gx1'=2,'gy'=4,'gz'=4] {'gx1','gy','gz'}, dimensions={0} | all-to-all | bytes 524288 | tf_op jit(solution)/shard_map/all_to_all | solution.py:512
  81.6 0.7 collective-permute-start.3
  82.2 2.4 %shard_map.122.refs_4_ = f32[8,8,128]{2,1,0:T(8,128)S(1)} custom-call(f32[16,4,128]{2,1,0:T(4,128)S(1)} %get-tuple-element.85.refs_0_.refs_5_, f32[16,4,128]{2,1,0:T(4,128)S(1)} %get-tuple-element.86.refs_1_.refs_6_, f32[16,4,128]{2,1,0:T(4,128)S(1)} %get-tuple-element.87.refs_2_, f32[48,8,128]{2,1,0:T(8,128)S(1)} %get-tuple-element.79.refs_3_.refs_7_, ...), custom_call_target="tpu_custom_call" | custom-call | flops 4000000000 | tf_op jit(solution)/shard_map/pallas_call | solution.py:489
  84.7 0.0 collective-permute-done.3.refs_0_
  84.7 0.6 shard_map.123
  85.3 15.9 %all_to_all.43.refs_0_ = f32[32,4,128]{2,1,0:T(4,128)S(1)} all-to-all(f32[32,4,128]{2,1,0:T(4,128)S(1)} %get-tuple-element.90), channel_id=1, replica_groups=mesh['gx0'=8,'gx1'=2,'gy'=4,'gz'=4] {'gx1','gy','gz'}, dimensions={0} | all-to-all | bytes 131072 | tf_op jit(solution)/shard_map/all_to_all | solution.py:512
  101.2 0.8 collective-permute-start.4
  102.1 2.3 %shard_map.125.refs_4_ = f32[8,8,128]{2,1,0:T(8,128)S(1)} custom-call(f32[16,128]{1,0:T(8,128)S(1)} %get-tuple-element.92.refs_0_.refs_5_, f32[16,128]{1,0:T(8,128)S(1)} %get-tuple-element.93.refs_1_.refs_6_, f32[16,128]{1,0:T(8,128)S(1)} %get-tuple-element.94.refs_2_, f32[48,8,128]{2,1,0:T(8,128)S(1)} %get-tuple-element.79.refs_3_.refs_7_, ...), custom_call_target="tpu_custom_call" | custom-call | flops 4000000000 | tf_op jit(solution)/shard_map/pallas_call | solution.py:489
  104.4 0.0 collective-permute-done.4.refs_0_
  104.4 0.6 shard_map.126
  105.0 16.9 %all_to_all.44.refs_0_ = f32[32,4,4,128]{3,2,1,0:T(4,128)S(1)} all-to-all(f32[32,4,4,128]{3,2,1,0:T(4,128)S(1)} %get-tuple-element.95), channel_id=1, replica_groups=mesh['gx0'=8,'gx1'=2,'gy'=4,'gz'=4] {'gx1','gy','gz'}, dimensions={0} | all-to-all | bytes 524288 | tf_op jit(solution)/shard_map/all_to_all | solution.py:512
  122.0 0.7 collective-permute-start.5
  122.6 0.0 copy-done.4
  122.7 0.0 copy-done.6
  122.7 2.4 %shard_map.128.refs_4_ = f32[8,8,128]{2,1,0:T(8,128)S(1)} custom-call(f32[16,4,128]{2,1,0:T(4,128)S(1)} %get-tuple-element.97.refs_0_.refs_5_, f32[16,4,128]{2,1,0:T(4,128)S(1)} %get-tuple-element.98.refs_1_.refs_6_, f32[16,4,128]{2,1,0:T(4,128)S(1)} %get-tuple-element.99.refs_2_, f32[48,8,128]{2,1,0:T(8,128)S(1)} %get-tuple-element.79.refs_3_.refs_7_, ...), custom_call_target="tpu_custom_call" | custom-call | flops 4000000000 | tf_op jit(solution)/shard_map/pallas_call | solution.py:489
  125.1 0.0 collective-permute-done.5.refs_0_
  125.1 1.2 shard_map.129
  126.3 17.3 %all_to_all.45.refs_0_ = f32[32,16,128]{2,1,0:T(8,128)S(1)} all-to-all(f32[32,16,128]{2,1,0:T(8,128)S(1)} %get-tuple-element.103), channel_id=1, replica_groups=mesh['gx0'=8,'gx1'=2,'gy'=4,'gz'=4] {'gx1','gy','gz'}, dimensions={0} | all-to-all | bytes 524288 | tf_op jit(solution)/shard_map/all_to_all | solution.py:512
  143.6 0.7 shard_map.130
  144.3 8.9 %all-to-all-start.7 = ((f32[8,24,128]{2,1,0:T(8,128)}), f32[8,24,128]{2,1,0:T(8,128)S(1)}, u32[]{:S(2)}, u32[]{:S(2)}) async-start(f32[8,24,128]{2,1,0:T(8,128)} %get-tuple-element.105), calls=%async_computation.7 | async-start | bytes 196608 | tf_op jit(solution)/shard_map/all_to_all | solution.py:585
  153.2 2.7 %copy-done.5 = bf16[2,2,15,384,128]{4,3,2,1,0:T(8,128)(2,1)S(1)} copy-done((bf16[2,2,15,384,128]{4,3,2,1,0:T(8,128)(2,1)S(1)}, bf16[2,2,15,384,128]{4,3,2,1,0:T(8,128)(2,1)}, u32[]{:S(2)}) %copy-start.5) | copy-done | bytes 5898264
  155.9 2.7 %copy-done.7 = bf16[2,2,15,384,128]{4,3,2,1,0:T(8,128)(2,1)S(1)} copy-done((bf16[2,2,15,384,128]{4,3,2,1,0:T(8,128)(2,1)S(1)}, bf16[2,2,15,384,128]{4,3,2,1,0:T(8,128)(2,1)}, u32[]{:S(2)}) %copy-start.7) | copy-done | bytes 5898264
  158.6 2.3 %shard_map.131.refs_4_ = f32[8,8,128]{2,1,0:T(8,128)S(1)} custom-call(f32[16,128]{1,0:T(8,128)S(1)} %get-tuple-element.106.refs_0_.refs_5_, f32[16,128]{1,0:T(8,128)S(1)} %get-tuple-element.107.refs_1_.refs_6_, f32[16,128]{1,0:T(8,128)S(1)} %get-tuple-element.108.refs_2_, f32[48,8,128]{2,1,0:T(8,128)S(1)} %get-tuple-element.79.refs_3_.refs_7_, ...), custom_call_target="tpu_custom_call" | custom-call | flops 4000000000 | tf_op jit(solution)/shard_map/pallas_call | solution.py:489
  160.9 0.0 all-to-all-done.7.refs_0_
  160.9 1.2 shard_map.132
  (11 shorter events, 0.2 us)
Async XLA Ops:
  2.7 16.1 %all-to-all-start = ((f32[32,8,128]{2,1,0:T(8,128)}), f32[32,8,128]{2,1,0:T(8,128)S(1)}, u32[]{:S(2)}, u32[]{:S(2)}) async-start(f32[32,8,128]{2,1,0:T(8,128)} %get-tuple-element.57), calls=%async_computation | async-start | bytes 262144 | tf_op jit(solution)/shard_map/all_to_all | solution.py:512
  11.2 3.6 %collective-permute-start = (f32[8,128]{1,0:T(8,128)}, f32[8,128]{1,0:T(8,128)S(1)}, u32[]{:S(2)}, u32[]{:S(2)}) collective-permute-start(f32[8,128]{1,0:T(8,128)} %get-tuple-element.58), channel_id=1, source_target_pairs={{16,32},{48,64},{80,96},{112,128},{144,160},{176,192},{208,224},{3... | collective-permute-start | bytes 12296 | tf_op jit(solution)/shard_map/ppermute | solution.py:515
  11.9 0.7 copy-start
  12.6 0.7 copy-start.1
  13.3 0.7 copy-start.2
  14.0 0.7 copy-start.3
  37.8 8.2 %collective-permute-start.1 = (f32[16,8,128]{2,1,0:T(8,128)S(1)}, f32[16,8,128]{2,1,0:T(8,128)S(1)}, u32[]{:S(2)}, u32[]{:S(2)}) collective-permute-start(f32[16,8,128]{2,1,0:T(8,128)S(1)} %get-tuple-element.63.refs_0_), channel_id=1, source_target_pairs={{16,32},{48,64},{80,96},{112,128},{144,160},{176,192},{208,224},{3... | collective-permute-start | bytes 196616 | tf_op jit(solution)/shard_map/ppermute | solution.py:515
  46.0 76.7 %copy-start.4 = (bf16[2,2,15,384,128]{4,3,2,1,0:T(8,128)(2,1)}, bf16[2,2,15,384,128]{4,3,2,1,0:T(8,128)(2,1)S(1)}, u32[]{:S(2)}) copy-start(bf16[2,2,15,384,128]{4,3,2,1,0:T(8,128)(2,1)S(1)} %get-tuple-element.80.refs_4_) | copy-start | bytes 17694724
  46.0 76.7 %copy-start.6 = (bf16[2,2,15,384,128]{4,3,2,1,0:T(8,128)(2,1)}, bf16[2,2,15,384,128]{4,3,2,1,0:T(8,128)(2,1)S(1)}, u32[]{:S(2)}) copy-start(bf16[2,2,15,384,128]{4,3,2,1,0:T(8,128)(2,1)S(1)} %get-tuple-element.81.refs_5_) | copy-start | bytes 17694724
  62.1 3.0 %collective-permute-start.2 = (f32[16,128]{1,0:T(8,128)S(1)}, f32[16,128]{1,0:T(8,128)S(1)}, u32[]{:S(2)}, u32[]{:S(2)}) collective-permute-start(f32[16,128]{1,0:T(8,128)S(1)} %get-tuple-element.73.refs_0_.refs_5_), channel_id=1, source_target_pairs={{16,32},{48,64},{80,96},{112,128},{144,160},{176,192},{208,224},{3... | collective-permute-start | bytes 24584 | tf_op jit(solution)/shard_map/ppermute | solution.py:515
  81.6 3.1 %collective-permute-start.3 = (f32[16,4,128]{2,1,0:T(4,128)S(1)}, f32[16,4,128]{2,1,0:T(4,128)S(1)}, u32[]{:S(2)}, u32[]{:S(2)}) collective-permute-start(f32[16,4,128]{2,1,0:T(4,128)S(1)} %get-tuple-element.85.refs_0_.refs_5_), channel_id=1, source_target_pairs={{16,32},{48,64},{80,96},{112,128},{144,160},{176,192},{208,224},{3... | collective-permute-start | bytes 98312 | tf_op jit(solution)/shard_map/ppermute | solution.py:515
  101.2 3.2 %collective-permute-start.4 = (f32[16,128]{1,0:T(8,128)S(1)}, f32[16,128]{1,0:T(8,128)S(1)}, u32[]{:S(2)}, u32[]{:S(2)}) collective-permute-start(f32[16,128]{1,0:T(8,128)S(1)} %get-tuple-element.92.refs_0_.refs_5_), channel_id=1, source_target_pairs={{16,32},{48,64},{80,96},{112,128},{144,160},{176,192},{208,224},{3... | collective-permute-start | bytes 24584 | tf_op jit(solution)/shard_map/ppermute | solution.py:515
  122.0 3.1 %collective-permute-start.5 = (f32[16,4,128]{2,1,0:T(4,128)S(1)}, f32[16,4,128]{2,1,0:T(4,128)S(1)}, u32[]{:S(2)}, u32[]{:S(2)}) collective-permute-start(f32[16,4,128]{2,1,0:T(4,128)S(1)} %get-tuple-element.97.refs_0_.refs_5_), channel_id=1, source_target_pairs={{16,32},{48,64},{80,96},{112,128},{144,160},{176,192},{208,224},{3... | collective-permute-start | bytes 98312 | tf_op jit(solution)/shard_map/ppermute | solution.py:515
  144.3 16.6 %all-to-all-start.7 = ((f32[8,24,128]{2,1,0:T(8,128)}), f32[8,24,128]{2,1,0:T(8,128)S(1)}, u32[]{:S(2)}, u32[]{:S(2)}) async-start(f32[8,24,128]{2,1,0:T(8,128)} %get-tuple-element.105), calls=%async_computation.7 | async-start | bytes 196608 | tf_op jit(solution)/shard_map/all_to_all | solution.py:585
  153.2 2.7 %copy-start.5 = (bf16[2,2,15,384,128]{4,3,2,1,0:T(8,128)(2,1)S(1)}, bf16[2,2,15,384,128]{4,3,2,1,0:T(8,128)(2,1)}, u32[]{:S(2)}) copy-start(bf16[2,2,15,384,128]{4,3,2,1,0:T(8,128)(2,1)} %copy-done.4) | copy-start | bytes 17694724
  155.9 2.7 %copy-start.7 = (bf16[2,2,15,384,128]{4,3,2,1,0:T(8,128)(2,1)S(1)}, bf16[2,2,15,384,128]{4,3,2,1,0:T(8,128)(2,1)}, u32[]{:S(2)}) copy-start(bf16[2,2,15,384,128]{4,3,2,1,0:T(8,128)(2,1)} %copy-done.6) | copy-start | bytes 17694724

commit v3 on v2

--- a/solution.py
+++ b/solution.py
@@ -238,12 +238,16 @@
         (1, 0, inner[:, 128:256]),
         (1, 256, dot(side(384, 512), b[:, 128:256])),
     )
-    sums = [jnp.zeros((8, 128), F32), jnp.zeros((8, 128), F32)]
+    sums = [[jnp.zeros((8, 128), F32)] * 2 for _ in range(2)]
     for cz, k, e in pieces:
         w = jnp.exp2(e)
         hi = w.astype(BF16)
         put(cz, k, k + e.shape[0], hi, (w - hi.astype(F32)).astype(BF16))
-        sums[cz] = sums[cz] + jnp.sum((w * w * e).reshape(e.shape[0] // 8, 8, 128), 0)
+        n = e.shape[0] // 8
+        sums[cz] = [
+            sums[cz][0] + jnp.sum(w.reshape(n, 8, 128), 0),
+            sums[cz][1] + jnp.sum((w * w * e).reshape(n, 8, 128), 0),
+        ]
     return sums
 
 
@@ -253,7 +257,7 @@
     return [(6 + k, k // 3, k % 3) for k in range(9)]
 
 
-def setup_main_kernel(l1, l2, near, whi, wlo, xr, own, bside, part, gpart, at, bi, ft):
+def setup_main_kernel(l1, l2, near, whi, wlo, xr, own, bside, ft, dpart, gpart, at, bi):
     g = lax.axis_index("gx1")
     for x, ref in enumerate((l1, l2, near)):
         xs = jnp.where(g == 0, x - 1.0, -1.0 * x)
@@ -278,7 +282,7 @@
     def weights(cy, carry):
         for cx in range(2):
             b = bi[cx * 2 + cy]
-            sums = [jnp.zeros((8, 128), F32), jnp.zeros((8, 128), F32)]
+            sums = [[jnp.zeros((8, 128), F32)] * 2 for _ in range(2)]
             for k, x, y in main_columns(cx):
                 xy = x * 4 + cy + y
 
@@ -287,51 +291,59 @@
                     wlo[cy, cz, k, lo:hi, :] = b
 
                 more = weigh(lambda lo, hi, xy=xy: at[xy, lo:hi, :], b, put)
-                sums = [p + q for p, q in zip(sums, more)]
+                sums = [[p + q for p, q in zip(a, b)] for a, b in zip(sums, more)]
             for cz in range(2):
-                gpart[(cx * 2 + cy) * 2 + cz] = sums[cz]
+                dpart[(cx * 2 + cy) * 2 + cz], gpart[(cx * 2 + cy) * 2 + cz] = sums[cz]
         return carry
 
     lax.fori_loop(0, 2, weights, 0)
-    main_pass(whi, wlo, ft, part)
-
-
-def main_pass(whi, wlo, ft, part):
+
+
+def unstacked_groups(acc):
+    return [unstacked(acc[k : k + 32]) for k in range(0, acc.shape[0], 32)]
+
+
+def slices(fts, column, cz):
+    parts = [ft[column, :, cz * 128 : cz * 128 + 384] for ft in fts]
+    return parts[0] if len(parts) == 1 else jnp.concatenate(parts, 0)
+
+
+def main_pass(whi, wlo, fts, part):
     def centre(cy, carry):
         for cx in range(2):
             for cz in range(2):
-                acc = jnp.zeros((32, 128), F32)
+                acc = jnp.zeros((32 * len(fts), 128), F32)
                 for k, x, y in main_columns(cx):
-                    f = ft[x * 4 + cy + y, :, cz * 128 : cz * 128 + 384]
+                    f = slices(fts, x * 4 + cy + y, cz)
                     acc = acc + dot(f, whi[cy, cz, k]) + dot(f, wlo[cy, cz, k])
-                part[(cx * 2 + cy) * 2 + cz] = unstacked(acc)
+                for g, r in enumerate(unstacked_groups(acc)):
+                    part[(cx * 2 + cy) * 2 + cz, g * 8 : g * 8 + 8, :] = r
         return carry
 
     lax.fori_loop(0, 2, centre, 0)
 
 
-def beyond_pass(whi, wlo, ft, part, finish):
+def beyond_pass(whi, wlo, fts, part, finish):
     for c in range(8):
         cx, cy, cz = c // 4, c // 2 % 2, c % 2
-        r = part[c]
+        r = [part[c, g * 8 : g * 8 + 8, :] for g in range(len(fts))]
         if cx == 0:
-            acc = jnp.zeros((32, 128), F32)
+            acc = jnp.zeros((32 * len(fts), 128), F32)
             for y in range(3):
-                f = ft[cy + y, :, cz * 128 : cz * 128 + 384]
+                f = slices(fts, cy + y, cz)
                 acc = acc + dot(f, whi[cy, cz, y]) + dot(f, wlo[cy, cz, y])
-            r = r + unstacked(acc)
-        finish(c, r)
-
-
-def setup_beyond_kernel(beyond, own, bside, part, gpart, counts, pprev, whi, wlo, xr, grad, aux, press, send, srow, at, ft, gsq):
+            r = [p + q for p, q in zip(r, unstacked_groups(acc))]
+        finish(c, *r)
+
+
+def setup_beyond_kernel(beyond, own, bside, dpart, gpart, counts, pprev, whi, wlo, xr, ft, gsq, safe2, press, send, srow, at, dsum):
     g = lax.axis_index("gx1")
-    row = rows_iota((8, 128))
-    axis_row = (row >= 1) & (row <= 3)
     xs = jnp.where(g == 0, -2.0, 1.0)
     for y in range(4):
         for z in range(4):
             column_features(y, z, beyond[y * 4 + z], xs, y - 2.0, xr, at, ft)
     gsq[...] = gpart[...]
+    dsum[...] = dpart[...]
     for cy in range(2):
         for y in range(3):
 
@@ -341,38 +353,39 @@
 
             more = weigh(lambda lo, hi, xy=cy + y: at[xy, lo:hi, :], bside[cy], put)
             for cz in range(2):
-                gsq[cy * 2 + cz] = gsq[cy * 2 + cz] + more[cz]
-
-    def finish(c, r):
-        st = own[c]
-        occ = st[0:1] > 0
-        s0 = r[0:1]
-        gr = jnp.where(axis_row, st * s0 - r, 0.0)
-        grad[c] = gr
-        density = particle_mass * s0
-        pair = pltpu.roll(st, 5, 0) * gr - st * pltpu.roll(r, 5, 0)
-        divergence = (-GRAD * particle_mass) * (
-            jnp.sum(jnp.where(axis_row, pair, 0.0), 0, keepdims=True) + r[7:8]
-        )
-        grad_norm = (GRAD * particle_mass) ** 2 * jnp.sum(gr * gr, 0, keepdims=True)
-        grad_square = (-GRAD * GRAD * particle_mass / KAPPA) * jnp.sum(gsq[c], 0, keepdims=True)
-        safe = jnp.where(occ, density, 1.0)
-        safe2 = safe * safe
-        source = jnp.where(occ, rest_density - (density + time_step * divergence), 0.0)
-        weight = jnp.where(occ, particle_mass, 0.0)
-        diagonal = jnp.maximum(
-            time_step * time_step * (grad_norm + weight * grad_square) / safe2, floor_value
-        )
-        lane = lax.broadcasted_iota(jnp.int32, (1, 128), 1).astype(F32)
+                c = cy * 2 + cz
+                dsum[c] = dsum[c] + more[cz][0]
+                gsq[c] = gsq[c] + more[cz][1]
+    lane = lax.broadcasted_iota(jnp.int32, (1, 128), 1).astype(F32)
+    for c in range(8):
+        occ = own[c, 0:1, :] > 0
+        safe = jnp.where(occ, particle_mass * jnp.sum(dsum[c], 0, keepdims=True), 1.0)
         pressure = jnp.where(lane < counts[c : c + 1, :], pprev[c : c + 1, :], 0.0)
-        aux[c, 0:1, :] = safe2
-        aux[c, 1:2, :] = source
-        aux[c, 2:3, :] = diagonal
+        safe2[c : c + 1, :] = safe * safe
         press[c : c + 1, :] = pressure
-        srow[c : c + 1, :] = jnp.where(occ, pressure / safe2, 0.0)
-
-    beyond_pass(whi, wlo, ft, part, finish)
+        srow[c : c + 1, :] = jnp.where(occ, pressure / (safe * safe), 0.0)
     fill_chunks(send, lambda c: srow[c : c + 1, :], False)
+
+
+def sources(st, r, gsq, safe2):
+    row = rows_iota((8, 128))
+    axis_row = (row >= 1) & (row <= 3)
+    occ = st[0:1] > 0
+    s0 = r[0:1]
+    gr = jnp.where(axis_row, st * s0 - r, 0.0)
+    density = particle_mass * s0
+    pair = pltpu.roll(st, 5, 0) * gr - st * pltpu.roll(r, 5, 0)
+    divergence = (-GRAD * particle_mass) * (
+        jnp.sum(jnp.where(axis_row, pair, 0.0), 0, keepdims=True) + r[7:8]
+    )
+    grad_norm = (GRAD * particle_mass) ** 2 * jnp.sum(gr * gr, 0, keepdims=True)
+    grad_square = (-GRAD * GRAD * particle_mass / KAPPA) * jnp.sum(gsq, 0, keepdims=True)
+    source = jnp.where(occ, rest_density - (density + time_step * divergence), 0.0)
+    weight = jnp.where(occ, particle_mass, 0.0)
+    diagonal = jnp.maximum(
+        time_step * time_step * (grad_norm + weight * grad_square) / safe2, floor_value
+    )
+    return gr, source, diagonal
 
 
 def scaled_features(layer, base, xr, ft):
@@ -397,7 +410,13 @@
 def main_kernel(l1, l2, near, xr, whi, wlo, part, ft, *, features):
     for x, layer in enumerate((l1, l2, near)):
         features(layer, x * 16, xr, ft)
-    main_pass(whi, wlo, ft, part)
+    main_pass(whi, wlo, (ft,), part)
+
+
+def first_main_kernel(l1, l2, near, xr, whi, wlo, fs, part, ft):
+    for x, layer in enumerate((l1, l2, near)):
+        scaled_features(layer, x * 16, xr, ft)
+    main_pass(whi, wlo, (fs, ft), part)
 
 
 def own_row(c):
@@ -407,16 +426,32 @@
 def accel_of(c, r, l1, l2, xr, grad):
     q = own_row(c)
     s = (l1, l2)[c // 4][q : q + 1, :]
-    return (GRAD * particle_mass) * (s * grad[c] + xr[c // 4 * 16 + q] * r[0:1] - r)
+    return (GRAD * particle_mass) * (s * grad + xr[c // 4 * 16 + q] * r[0:1] - r)
 
 
 def accel_kernel(beyond, xrb, whi, wlo, part, l1, l2, xr, grad, send, mine, ft):
     scaled_features(beyond, 0, xrb, ft)
 
     def finish(c, r):
-        mine[c] = accel_of(c, r, l1, l2, xr, grad)[0:4]
-
-    beyond_pass(whi, wlo, ft, part, finish)
+        mine[c] = accel_of(c, r, l1, l2, xr, grad[c])[0:4]
+
+    beyond_pass(whi, wlo, (ft,), part, finish)
+    fill_chunks(send, lambda c: mine[c], True)
+
+
+def first_accel_kernel(beyond, xrb, whi, wlo, fs, part, l1, l2, xr, own, gsq, safe2, send, mine, grad, aux, ft):
+    scaled_features(beyond, 0, xrb, ft)
+
+    def finish(c, rs, r):
+        squared = safe2[c : c + 1, :]
+        gr, source, diagonal = sources(own[c], rs, gsq[c], squared)
+        grad[c] = gr
+        aux[c, 0:1, :] = squared
+        aux[c, 1:2, :] = source
+        aux[c, 2:3, :] = diagonal
+        mine[c] = accel_of(c, r, l1, l2, xr, gr)[0:4]
+
+    beyond_pass(whi, wlo, (fs, ft), part, finish)
     fill_chunks(send, lambda c: mine[c], True)
 
 
@@ -445,7 +480,7 @@
             pnew[c : c + 1, :] = p
         mine[c : c + 1, :] = jnp.where(occ, p / safe2, 0.0)
 
-    beyond_pass(whi, wlo, ft, part, finish)
+    beyond_pass(whi, wlo, (ft,), part, finish)
     fill_chunks(send, lambda c: mine[c : c + 1, :], False)
     if last:
         first, totals = mine[0:4, :], enew[...]
@@ -468,7 +503,7 @@
     row = rows_iota((8, 128))
 
     def finish(c, r):
-        a = accel_of(c, r, l1, l2, xr, grad)
+        a = accel_of(c, r, l1, l2, xr, grad[c])
         st = state[c]
         pulled = a - jnp.where(row == 3, gravity, 0.0)
         v = pltpu.roll(st, 5, 0) + time_step * pulled
@@ -476,7 +511,7 @@
         for f in range(3):
             vout[f, outer_x(c // 4), c // 2 % 2, c % 2 : c % 2 + 1, :] = v[1 + f : 2 + f]
 
-    beyond_pass(whi, wlo, ft, part, finish)
+    beyond_pass(whi, wlo, (ft,), part, finish)
 
 
 def call(body, outs, operands, scratch=(), limit=12 << 20, flops=0, first=None, **static):
@@ -535,33 +570,43 @@
     l1, l2, near = layers(send, state, (8, 128))
     beyond = from_beyond(l1)
     wmain, wside = sds(2, 2, 15, 384, 128, dtype=BF16), sds(2, 2, 3, 384, 128, dtype=BF16)
-    whi, wlo, xr, own, bside, part, gpart = call(
+    fshape = sds(12, 32, 512, dtype=BF16)
+    whi, wlo, xr, own, bside, fs, dpart, gpart = call(
         setup_main_kernel,
-        (wmain, wmain, sds(48, 8, 128), tiles, sds(2, 64, 256, dtype=BF16), tiles, tiles),
+        (wmain, wmain, sds(48, 8, 128), tiles, sds(2, 64, 256, dtype=BF16), fshape, tiles, tiles),
         (l1, l2, near),
-        [pltpu.VMEM((12, 512, 64), BF16), pltpu.VMEM((4, 64, 256), BF16), features(12)],
+        [pltpu.VMEM((12, 512, 64), BF16), pltpu.VMEM((4, 64, 256), BF16)],
         flops=3 * busy,
     )
-    bhi, blo, xrb, grad, aux, press, send, mine = call(
+    bhi, blo, xrb, fsb, gsq, safe2, press, send, mine = call(
         setup_beyond_kernel,
-        (wside, wside, sds(16, 8, 128), tiles, tiles, rows, sds(group, 4, 128), rows),
-        (beyond, own, bside, part, gpart, filled, before),
-        [pltpu.VMEM((4, 512, 64), BF16), features(4), pltpu.VMEM((8, 8, 128), F32)],
+        (wside, wside, sds(16, 8, 128), sds(4, 32, 512, dtype=BF16), tiles, rows, rows, sds(group, 4, 128), rows),
+        (beyond, own, bside, dpart, gpart, filled, before),
+        [pltpu.VMEM((4, 512, 64), BF16), pltpu.VMEM((8, 8, 128), F32)],
     )
     errs = None
     for it in range(ITERS):
         last = it == ITERS - 1
         l1, l2, near = layers(send, mine, (128,))
         beyond = from_beyond(l1)
-        (part,) = call(
-            main_kernel, (tiles,), (l1, l2, near, xr, whi, wlo), [features(12)], flops=busy, features=scaled_features
-        )
-        send, mine = call(
-            accel_kernel,
-            (sds(group, 4, 4, 128), sds(8, 4, 128)),
-            (beyond, xrb, bhi, blo, part, l1, l2, xr, grad),
-            [features(4)],
-        )
+        accels = (sds(group, 4, 4, 128), sds(8, 4, 128))
+        if it == 0:
+            (part,) = call(
+                first_main_kernel, (sds(8, 16, 128),), (l1, l2, near, xr, whi, wlo, fs), [features(12)], flops=busy
+            )
+            send, mine, grad, aux = call(
+                first_accel_kernel,
+                (*accels, tiles, tiles),
+                (beyond, xrb, bhi, blo, fsb, part, l1, l2, xr, own, gsq, safe2),
+                [features(4)],
+            )
+        else:
+            (part,) = call(
+                main_kernel, (tiles,), (l1, l2, near, xr, whi, wlo), [features(12)], flops=busy, features=scaled_features
+            )
+            send, mine = call(
+                accel_kernel, accels, (beyond, xrb, bhi, blo, part, l1, l2, xr, grad), [features(4)]
+            )
         l1, l2, near = layers(send, mine, (4, 128))
         beyond = from_beyond(l1)
         (part,) = call(

time: 163 us -> 161 us (0.988)
  Pallas kernels: 28.2 us -> 26.2 us
    pallas_call x21, Pallas kernels: 28.2 us -> 26.2 us  [call(): pl.pallas_call(named, out_shape=outs, in_specs=specs, out_specs=jax.tree....]
  transfers between devices with their start and end apart: 8 -> 8, of which waited for: 1 -> 1; matrix products, arithmetic and copies ran while one was open for 0% -> 0% of each run, Pallas kernels for 12% -> 11%
where the time goes in v3:
time: 161 us; the launch traced here: 160 us
  blocking collectives  98.5 us (61%)
  Pallas kernels  26.2 us (16%)
  starting transfers between devices  21.7 us (13%)
  local copies, waits for them, and re-layouts  8.13 us (5%)
  waiting for transfers between devices  3.98 us (2%)
  between operations  1.71 us (1%)
    all_to_all x6, blocking collectives, spread(): return lax.all_to_all(send, GROUP, 0, 0)  98.5 us
    pallas_call x21, Pallas kernels, call(): pl.pallas_call(named, out_shape=outs, in_specs=specs, out_specs=jax.tree....  26.2 us
    all_to_all x1, starting transfers between devices, on_device(): recv = lax.all_to_all(send, 'gx0', 0, 0)  8.94 us
    all_to_all x1, starting transfers between devices, spread(): return lax.all_to_all(send, GROUP, 0, 0)  8.58 us
    unnamed x16, local copies, waits for them, and re-layouts  8.13 us
    ppermute x6, starting transfers between devices, from_beyond(): return lax.ppermute(layer, ('gx0', 'gx1'), across)  4.16 us
    all_to_all x1, waiting for transfers between devices, spread(): return lax.all_to_all(send, GROUP, 0, 0)  3.96 us
  transfers between devices with their start and end apart: 8, of which 1 were waited for; matrix products, arithmetic and copies ran while one was open for 0% of the time, Pallas kernels for 11%

profile of v3, /device:TPU:1, one launch (start us, length us, event | category | flops | bytes accessed | tf_op | source)
XLA Modules:
  0.0 160.1 jit_solution(16229124743975156344)
XLA Ops:
  1.3 1.4 shard_map.112
  2.7 8.6 %all-to-all-start = ((f32[32,8,128]{2,1,0:T(8,128)}), f32[32,8,128]{2,1,0:T(8,128)S(1)}, u32[]{:S(2)}, u32[]{:S(2)}) async-start(f32[32,8,128]{2,1,0:T(8,128)} %get-tuple-element.61), calls=%async_computation | async-start | bytes 262144 | tf_op jit(solution)/shard_map/all_to_all | solution.py:547
  11.2 0.7 collective-permute-start
  11.9 0.0 copy-start
  11.9 0.7 copy-done
  12.6 0.7 copy-done.1
  13.3 0.7 copy-done.2
  14.0 0.7 copy-done.3
  14.7 0.1 shard_map.113
  14.8 0.0 collective-permute-done.refs_1_
  14.8 4.0 %all-to-all-done.refs_0_ = f32[32,8,128]{2,1,0:T(8,128)S(1)} async-done(((f32[32,8,128]{2,1,0:T(8,128)}), f32[32,8,128]{2,1,0:T(8,128)S(1)}, u32[]{:S(2)}, u32[]{:S(2)}) %all-to-all-start) | async-done | bytes 131104 | tf_op jit(solution)/shard_map/all_to_all | solution.py:547
  18.8 1.1 shard_map.114
  19.9 17.9 %all_to_all.40.refs_0_ = f32[32,4,8,128]{3,2,1,0:T(8,128)S(1)} all-to-all(f32[32,4,8,128]{3,2,1,0:T(8,128)S(1)} %get-tuple-element.65), channel_id=1, replica_groups=mesh['gx0'=8,'gx1'=2,'gy'=4,'gz'=4] {'gx1','gy','gz'}, dimensions={0} | all-to-all | bytes 1048576 | tf_op jit(solution)/shard_map/all_to_all | solution.py:547
  37.8 0.7 collective-permute-start.1
  38.5 5.5 %shard_map.116 = (bf16[2,2,15,384,128]{4,3,2,1,0:T(8,128)(2,1)S(1)}, bf16[2,2,15,384,128]{4,3,2,1,0:T(8,128)(2,1)S(1)}, f32[48,8,128]{2,1,0:T(8,128)S(1)}, f32[8...) custom-call(f32[16,8,128]{2,1,0:T(8,128)S(1)} %get-tuple-element.67., ...), custom_call_target="tpu_custom_call" | custom-call | flops 12000000000 | tf_op jit(solution)/shard_map/pallas_call | solution.py:524
  44.0 0.0 copy-start.4
  44.1 0.0 collective-permute-done.1.refs_0_
  44.1 1.1 shard_map.117
  45.2 14.7 %all_to_all.41.refs_0_ = f32[32,4,128]{2,1,0:T(4,128)S(1)} all-to-all(f32[32,4,128]{2,1,0:T(4,128)S(1)} %get-tuple-element.75), channel_id=1, replica_groups=mesh['gx0'=8,'gx1'=2,'gy'=4,'gz'=4] {'gx1','gy','gz'}, dimensions={0} | all-to-all | bytes 131072 | tf_op jit(solution)/shard_map/all_to_all | solution.py:547
  59.9 0.7 collective-permute-start.2
  60.5 2.4 %shard_map.119.refs_5_ = f32[8,16,128]{2,1,0:T(8,128)S(1)} custom-call(f32[16,128]{1,0:T(8,128)S(1)} %get-tuple-element.77.refs_0_.refs_6_, f32[16,128]{1,0:T(8,128)S(1)} %get-tuple-element.82.refs_1_.refs_7_, f32[16,128]{1,0:T(8,128)S(1)} %get-tuple-element.83.refs_2_, f32[48,8,128]{2,1,0:T(8,128)S(1)} %get-tuple-element.84.refs_3_.refs_8_.refs_7_, ...), custom_call_target="tpu_custom_call" | custom-call | flops 4000000000 | tf_op jit(solution)/shard_map/pallas_call | solution.py:524
  63.0 0.0 collective-permute-done.2.refs_0_
  63.0 0.6 shard_map.120
  63.6 15.9 %all_to_all.42.refs_0_ = f32[32,4,4,128]{3,2,1,0:T(4,128)S(1)} all-to-all(f32[32,4,4,128]{3,2,1,0:T(4,128)S(1)} %get-tuple-element.90), channel_id=1, replica_groups=mesh['gx0'=8,'gx1'=2,'gy'=4,'gz'=4] {'gx1','gy','gz'}, dimensions={0} | all-to-all | bytes 524288 | tf_op jit(solution)/shard_map/all_to_all | solution.py:547
  79.5 0.7 collective-permute-start.3
  80.2 2.4 %shard_map.122.refs_4_ = f32[8,8,128]{2,1,0:T(8,128)S(1)} custom-call(f32[16,4,128]{2,1,0:T(4,128)S(1)} %get-tuple-element.92.refs_0_.refs_5_, f32[16,4,128]{2,1,0:T(4,128)S(1)} %get-tuple-element.93.refs_1_.refs_6_, f32[16,4,128]{2,1,0:T(4,128)S(1)} %get-tuple-element.94.refs_2_, f32[48,8,128]{2,1,0:T(8,128)S(1)} %get-tuple-element.84.refs_3_.refs_8_.refs_7_, ...), custom_call_target="tpu_custom_call" | custom-call | flops 4000000000 | tf_op jit(solution)/shard_map/pallas_call | solution.py:524
  82.6 0.0 collective-permute-done.3.refs_0_
  82.6 0.6 shard_map.123
  83.2 15.9 %all_to_all.43.refs_0_ = f32[32,4,128]{2,1,0:T(4,128)S(1)} all-to-all(f32[32,4,128]{2,1,0:T(4,128)S(1)} %get-tuple-element.98), channel_id=1, replica_groups=mesh['gx0'=8,'gx1'=2,'gy'=4,'gz'=4] {'gx1','gy','gz'}, dimensions={0} | all-to-all | bytes 131072 | tf_op jit(solution)/shard_map/all_to_all | solution.py:547
  99.1 0.8 collective-permute-start.4
  100.0 2.3 %shard_map.125.refs_4_ = f32[8,8,128]{2,1,0:T(8,128)S(1)} custom-call(f32[16,128]{1,0:T(8,128)S(1)} %get-tuple-element.100.refs_0_.refs_5_, f32[16,128]{1,0:T(8,128)S(1)} %get-tuple-element.101.refs_1_.refs_6_, f32[16,128]{1,0:T(8,128)S(1)} %get-tuple-element.102.refs_2_, f32[48,8,128]{2,1,0:T(8,128)S(1)} %get-tuple-element.84.refs_3_.refs_8_.refs_7_, ...), custom_call_target="tpu_custom_call" | custom-call | flops 4000000000 | tf_op jit(solution)/shard_map/pallas_call | solution.py:524
  102.3 0.0 collective-permute-done.4.refs_0_
  102.4 0.6 shard_map.126
  102.9 16.9 %all_to_all.44.refs_0_ = f32[32,4,4,128]{3,2,1,0:T(4,128)S(1)} all-to-all(f32[32,4,4,128]{3,2,1,0:T(4,128)S(1)} %get-tuple-element.103), channel_id=1, replica_groups=mesh['gx0'=8,'gx1'=2,'gy'=4,'gz'=4] {'gx1','gy','gz'}, dimensions={0} | all-to-all | bytes 524288 | tf_op jit(solution)/shard_map/all_to_all | solution.py:547
  119.9 0.7 collective-permute-start.5
  120.6 0.0 copy-done.4
  120.6 0.0 copy-done.6
  120.6 2.4 %shard_map.128.refs_4_ = f32[8,8,128]{2,1,0:T(8,128)S(1)} custom-call(f32[16,4,128]{2,1,0:T(4,128)S(1)} %get-tuple-element.105.refs_0_.refs_5_, f32[16,4,128]{2,1,0:T(4,128)S(1)} %get-tuple-element.106.refs_1_.refs_6_, f32[16,4,128]{2,1,0:T(4,128)S(1)} %get-tuple-element.107.refs_2_, f32[48,8,128]{2,1,0:T(8,128)S(1)} %get-tuple-element.84.refs_3_.refs_8_.refs_7_, ...), custom_call_target="tpu_custom_call" | custom-call | flops 4000000000 | tf_op jit(solution)/shard_map/pallas_call | solution.py:524
  123.0 0.0 collective-permute-done.5.refs_0_
  123.0 1.2 shard_map.129
  124.2 17.2 %all_to_all.45.refs_0_ = f32[32,16,128]{2,1,0:T(8,128)S(1)} all-to-all(f32[32,16,128]{2,1,0:T(8,128)S(1)} %get-tuple-element.111), channel_id=1, replica_groups=mesh['gx0'=8,'gx1'=2,'gy'=4,'gz'=4] {'gx1','gy','gz'}, dimensions={0} | all-to-all | bytes 524288 | tf_op jit(solution)/shard_map/all_to_all | solution.py:547
  141.5 0.7 shard_map.130
  142.1 8.9 %all-to-all-start.7 = ((f32[8,24,128]{2,1,0:T(8,128)}), f32[8,24,128]{2,1,0:T(8,128)S(1)}, u32[]{:S(2)}, u32[]{:S(2)}) async-start(f32[8,24,128]{2,1,0:T(8,128)} %get-tuple-element.113), calls=%async_computation.7 | async-start | bytes 196608 | tf_op jit(solution)/shard_map/all_to_all | solution.py:630
  151.1 2.7 %copy-done.5 = bf16[2,2,15,384,128]{4,3,2,1,0:T(8,128)(2,1)S(1)} copy-done((bf16[2,2,15,384,128]{4,3,2,1,0:T(8,128)(2,1)S(1)}, bf16[2,2,15,384,128]{4,3,2,1,0:T(8,128)(2,1)}, u32[]{:S(2)}) %copy-start.5) | copy-done | bytes 5898264
  153.8 2.7 %copy-done.7 = bf16[2,2,15,384,128]{4,3,2,1,0:T(8,128)(2,1)S(1)} copy-done((bf16[2,2,15,384,128]{4,3,2,1,0:T(8,128)(2,1)S(1)}, bf16[2,2,15,384,128]{4,3,2,1,0:T(8,128)(2,1)}, u32[]{:S(2)}) %copy-start.7) | copy-done | bytes 5898264
  156.4 2.3 %shard_map.131.refs_4_ = f32[8,8,128]{2,1,0:T(8,128)S(1)} custom-call(f32[16,128]{1,0:T(8,128)S(1)} %get-tuple-element.114.refs_0_.refs_5_, f32[16,128]{1,0:T(8,128)S(1)} %get-tuple-element.115.refs_1_.refs_6_, f32[16,128]{1,0:T(8,128)S(1)} %get-tuple-element.116.refs_2_, f32[48,8,128]{2,1,0:T(8,128)S(1)} %get-tuple-element.84.refs_3_.refs_8_.refs_7_, ...), custom_call_target="tpu_custom_call" | custom-call | flops 4000000000 | tf_op jit(solution)/shard_map/pallas_call | solution.py:524
  158.8 0.0 all-to-all-done.7.refs_0_
  158.8 1.2 shard_map.132
  (11 shorter events, 0.2 us)
Async XLA Ops:
  2.7 16.1 %all-to-all-start = ((f32[32,8,128]{2,1,0:T(8,128)}), f32[32,8,128]{2,1,0:T(8,128)S(1)}, u32[]{:S(2)}, u32[]{:S(2)}) async-start(f32[32,8,128]{2,1,0:T(8,128)} %get-tuple-element.61), calls=%async_computation | async-start | bytes 262144 | tf_op jit(solution)/shard_map/all_to_all | solution.py:547
  11.2 3.6 %collective-permute-start = (f32[8,128]{1,0:T(8,128)}, f32[8,128]{1,0:T(8,128)S(1)}, u32[]{:S(2)}, u32[]{:S(2)}) collective-permute-start(f32[8,128]{1,0:T(8,128)} %get-tuple-element.62), channel_id=1, source_target_pairs={{16,32},{48,64},{80,96},{112,128},{144,160},{176,192},{208,224},{3... | collective-permute-start | bytes 12296 | tf_op jit(solution)/shard_map/ppermute | solution.py:550
  11.9 0.7 copy-start
  12.6 0.7 copy-start.1
  13.3 0.7 copy-start.2
  14.0 0.7 copy-start.3
  37.8 6.3 %collective-permute-start.1 = (f32[16,8,128]{2,1,0:T(8,128)S(1)}, f32[16,8,128]{2,1,0:T(8,128)S(1)}, u32[]{:S(2)}, u32[]{:S(2)}) collective-permute-start(f32[16,8,128]{2,1,0:T(8,128)S(1)} %get-tuple-element.67.refs_0_), channel_id=1, source_target_pairs={{16,32},{48,64},{80,96},{112,128},{144,160},{176,192},{208,224},{3... | collective-permute-start | bytes 196616 | tf_op jit(solution)/shard_map/ppermute | solution.py:550
  44.0 76.5 %copy-start.4 = (bf16[2,2,15,384,128]{4,3,2,1,0:T(8,128)(2,1)}, bf16[2,2,15,384,128]{4,3,2,1,0:T(8,128)(2,1)S(1)}, u32[]{:S(2)}) copy-start(bf16[2,2,15,384,128]{4,3,2,1,0:T(8,128)(2,1)S(1)} %get-tuple-element.85.refs_4_) | copy-start | bytes 17694724
  44.0 76.5 %copy-start.6 = (bf16[2,2,15,384,128]{4,3,2,1,0:T(8,128)(2,1)}, bf16[2,2,15,384,128]{4,3,2,1,0:T(8,128)(2,1)S(1)}, u32[]{:S(2)}) copy-start(bf16[2,2,15,384,128]{4,3,2,1,0:T(8,128)(2,1)S(1)} %get-tuple-element.86.refs_5_) | copy-start | bytes 17694724
  59.9 3.1 %collective-permute-start.2 = (f32[16,128]{1,0:T(8,128)S(1)}, f32[16,128]{1,0:T(8,128)S(1)}, u32[]{:S(2)}, u32[]{:S(2)}) collective-permute-start(f32[16,128]{1,0:T(8,128)S(1)} %get-tuple-element.77.refs_0_.refs_6_), channel_id=1, source_target_pairs={{16,32},{48,64},{80,96},{112,128},{144,160},{176,192},{208,224},{3... | collective-permute-start | bytes 24584 | tf_op jit(solution)/shard_map/ppermute | solution.py:550
  79.5 3.1 %collective-permute-start.3 = (f32[16,4,128]{2,1,0:T(4,128)S(1)}, f32[16,4,128]{2,1,0:T(4,128)S(1)}, u32[]{:S(2)}, u32[]{:S(2)}) collective-permute-start(f32[16,4,128]{2,1,0:T(4,128)S(1)} %get-tuple-element.92.refs_0_.refs_5_), channel_id=1, source_target_pairs={{16,32},{48,64},{80,96},{112,128},{144,160},{176,192},{208,224},{3... | collective-permute-start | bytes 98312 | tf_op jit(solution)/shard_map/ppermute | solution.py:550
  99.1 3.2 %collective-permute-start.4 = (f32[16,128]{1,0:T(8,128)S(1)}, f32[16,128]{1,0:T(8,128)S(1)}, u32[]{:S(2)}, u32[]{:S(2)}) collective-permute-start(f32[16,128]{1,0:T(8,128)S(1)} %get-tuple-element.100.refs_0_.refs_5_), channel_id=1, source_target_pairs={{16,32},{48,64},{80,96},{112,128},{144,160},{176,192},{208,224},{3... | collective-permute-start | bytes 24584 | tf_op jit(solution)/shard_map/ppermute | solution.py:550
  119.9 3.1 %collective-permute-start.5 = (f32[16,4,128]{2,1,0:T(4,128)S(1)}, f32[16,4,128]{2,1,0:T(4,128)S(1)}, u32[]{:S(2)}, u32[]{:S(2)}) collective-permute-start(f32[16,4,128]{2,1,0:T(4,128)S(1)} %get-tuple-element.105.refs_0_.refs_5_), channel_id=1, source_target_pairs={{16,32},{48,64},{80,96},{112,128},{144,160},{176,192},{208,224},{3... | collective-permute-start | bytes 98312 | tf_op jit(solution)/shard_map/ppermute | solution.py:550
  142.1 16.6 %all-to-all-start.7 = ((f32[8,24,128]{2,1,0:T(8,128)}), f32[8,24,128]{2,1,0:T(8,128)S(1)}, u32[]{:S(2)}, u32[]{:S(2)}) async-start(f32[8,24,128]{2,1,0:T(8,128)} %get-tuple-element.113), calls=%async_computation.7 | async-start | bytes 196608 | tf_op jit(solution)/shard_map/all_to_all | solution.py:630
  151.1 2.7 %copy-start.5 = (bf16[2,2,15,384,128]{4,3,2,1,0:T(8,128)(2,1)S(1)}, bf16[2,2,15,384,128]{4,3,2,1,0:T(8,128)(2,1)}, u32[]{:S(2)}) copy-start(bf16[2,2,15,384,128]{4,3,2,1,0:T(8,128)(2,1)} %copy-done.4) | copy-start | bytes 17694724
  153.8 2.7 %copy-start.7 = (bf16[2,2,15,384,128]{4,3,2,1,0:T(8,128)(2,1)S(1)}, bf16[2,2,15,384,128]{4,3,2,1,0:T(8,128)(2,1)}, u32[]{:S(2)}) copy-start(bf16[2,2,15,384,128]{4,3,2,1,0:T(8,128)(2,1)} %copy-done.6) | copy-start | bytes 17694724

commit v4 on v3

--- a/solution.py
+++ b/solution.py
@@ -157,7 +157,7 @@
         send[p, 16:24, :] = totals
 
 
-def insert_kernel(recv, beyond, base, counts, send, state):
+def insert_kernel(recv, beyond, base, counts, send, state, places):
     row = rows_iota((8, 128))
     lanef = lax.broadcasted_iota(jnp.int32, (8, 128), 1).astype(F32)
     here, there = plane_start(False), plane_start(True)
@@ -197,19 +197,20 @@
         tile = jnp.where(lanef < filled[c : c + 1], base[c], unstacked(acc))
         occ = lanef < grown[c : c + 1]
         tile = jnp.where(row == 0, 1.0, jnp.where(row == 7, 0.0, tile))
-        state[c] = jnp.where(occ, tile, 0.0)
-    fill_chunks(send, lambda c: state[c], True)
-
-
-def column_features(xy, z, tile, xs, ys, xr, at, ft):
+        tile = jnp.where(occ, tile, 0.0)
+        state[c] = tile
+        places[c] = tile[0:4]
+    fill_chunks(send, lambda c: places[c], True)
+
+
+def column_features(xy, z, place, xs, ys, xr, at):
     row = rows_iota((8, 128))
     axis_row = (row >= 1) & (row <= 3)
+    tile = jnp.concatenate([place, jnp.zeros((4, 128), F32)], 0)
     occ = tile[0:1]
     shift = jnp.where(row == 1, xs, jnp.where(row == 2, ys, jnp.where(row == 3, z - 2.0, 0.0)))
     st = (tile + shift) * occ
-    xr[xy * 4 + z] = jnp.where(row < 4, st, 0.0)
-    vx = jnp.sum(jnp.where(axis_row, st * pltpu.roll(st, 5, 0), 0.0), 0, keepdims=True)
-    ft[xy, :, z * 128 : z * 128 + 128] = stacked(jnp.where(row == 7, vx, st))
+    xr[xy * 4 + z] = st
     y = jnp.where(axis_row, st * YSCALE, 0.0)
     h, m, l = split3(y)
     qh, qm, ql = split3(jnp.where(occ > 0, 0.5 * jnp.sum(y * y, 0, keepdims=True), ABSENT))
@@ -257,21 +258,21 @@
     return [(6 + k, k // 3, k % 3) for k in range(9)]
 
 
-def setup_main_kernel(l1, l2, near, whi, wlo, xr, own, bside, ft, dpart, gpart, at, bi):
+def setup_main_kernel(l1, l2, near, state, whi, wlo, xr, own, bside, dpart, gpart, at, bi):
     g = lax.axis_index("gx1")
     for x, ref in enumerate((l1, l2, near)):
         xs = jnp.where(g == 0, x - 1.0, -1.0 * x)
 
         def column(y, carry, x=x, ref=ref, xs=xs):
             for z in range(4):
-                column_features(x * 4 + y, z, ref[y * 4 + z], xs, (y - 2).astype(F32), xr, at, ft)
+                column_features(x * 4 + y, z, ref[y * 4 + z], xs, (y - 2).astype(F32), xr, at)
             return carry
 
         lax.fori_loop(0, 4, column, 0)
     row = rows_iota((8, 128))
     for c in range(8):
         cx, cy, cz = c // 4, c // 2 % 2, c % 2
-        tile = (l1, l2)[cx][(cy + 1) * 4 + cz + 1]
+        tile = state[c]
         xs = jnp.where(g == 0, cx - 1.0, -1.0 * cx)
         shift = jnp.where(row == 1, xs, jnp.where(row == 2, cy - 1.0, jnp.where(row == 3, cz - 1.0, 0.0)))
         st = (tile + shift) * tile[0:1]
@@ -336,12 +337,12 @@
         finish(c, *r)
 
 
-def setup_beyond_kernel(beyond, own, bside, dpart, gpart, counts, pprev, whi, wlo, xr, ft, gsq, safe2, press, send, srow, at, dsum):
+def setup_beyond_kernel(beyond, own, bside, dpart, gpart, counts, pprev, whi, wlo, xr, gsq, safe2, press, send, mine, at, dsum):
     g = lax.axis_index("gx1")
     xs = jnp.where(g == 0, -2.0, 1.0)
     for y in range(4):
         for z in range(4):
-            column_features(y, z, beyond[y * 4 + z], xs, y - 2.0, xr, at, ft)
+            column_features(y, z, beyond[y * 4 + z], xs, y - 2.0, xr, at)
     gsq[...] = gpart[...]
     dsum[...] = dpart[...]
     for cy in range(2):
@@ -363,8 +364,9 @@
         pressure = jnp.where(lane < counts[c : c + 1, :], pprev[c : c + 1, :], 0.0)
         safe2[c : c + 1, :] = safe * safe
         press[c : c + 1, :] = pressure
-        srow[c : c + 1, :] = jnp.where(occ, pressure / (safe * safe), 0.0)
-    fill_chunks(send, lambda c: srow[c : c + 1, :], False)
+        mine[c, 0:1, :] = jnp.where(occ, pressure / (safe * safe), 0.0)
+        mine[c, 1:4, :] = own[c, 4:7, :]
+    fill_chunks(send, lambda c: mine[c], True)
 
 
 def sources(st, r, gsq, safe2):
@@ -395,6 +397,19 @@
             ft[base // 4 + y, :, z * 128 : z * 128 + 128] = stacked(layer[q : q + 1, :] * xr[base + q])
 
 
+def first_features(layer, base, xr, fs, ft):
+    row = rows_iota((8, 128))
+    for y in range(4):
+        for z in range(4):
+            q = y * 4 + z
+            x = xr[base + q]
+            t = jnp.concatenate([layer[q], jnp.zeros((4, 128), F32)], 0)
+            vx = jnp.sum(jnp.where((row >= 1) & (row <= 3), x * t, 0.0), 0, keepdims=True)
+            v = jnp.where((row >= 4) & (row <= 6), pltpu.roll(t, 3, 0), 0.0)
+            fs[base // 4 + y, :, z * 128 : z * 128 + 128] = stacked(jnp.where(row == 7, vx, x + v))
+            ft[base // 4 + y, :, z * 128 : z * 128 + 128] = stacked(t[0:1] * x)
+
+
 def accel_features(layer, base, xr, ft):
     row = rows_iota((8, 128))
     axis_row = (row >= 1) & (row <= 3)
@@ -413,9 +428,9 @@
     main_pass(whi, wlo, (ft,), part)
 
 
-def first_main_kernel(l1, l2, near, xr, whi, wlo, fs, part, ft):
+def first_main_kernel(l1, l2, near, xr, whi, wlo, part, fs, ft):
     for x, layer in enumerate((l1, l2, near)):
-        scaled_features(layer, x * 16, xr, ft)
+        first_features(layer, x * 16, xr, fs, ft)
     main_pass(whi, wlo, (fs, ft), part)
 
 
@@ -425,7 +440,8 @@
 
 def accel_of(c, r, l1, l2, xr, grad):
     q = own_row(c)
-    s = (l1, l2)[c // 4][q : q + 1, :]
+    layer = (l1, l2)[c // 4]
+    s = layer[q : q + 1, :] if len(layer.shape) == 2 else layer[q, 0:1, :]
     return (GRAD * particle_mass) * (s * grad + xr[c // 4 * 16 + q] * r[0:1] - r)
 
 
@@ -439,8 +455,8 @@
     fill_chunks(send, lambda c: mine[c], True)
 
 
-def first_accel_kernel(beyond, xrb, whi, wlo, fs, part, l1, l2, xr, own, gsq, safe2, send, mine, grad, aux, ft):
-    scaled_features(beyond, 0, xrb, ft)
+def first_accel_kernel(beyond, xrb, whi, wlo, part, l1, l2, xr, own, gsq, safe2, send, mine, grad, aux, fs, ft):
+    first_features(beyond, 0, xrb, fs, ft)
 
     def finish(c, rs, r):
         squared = safe2[c : c + 1, :]
@@ -566,46 +582,47 @@
     base, before, filled = call(
         prepare_kernel, (tiles, rows, rows), (positions, velocities, pressure_prev, counts), flops=busy // 4
     )
-    send, state = call(insert_kernel, (sds(group, 4, 8, 128), tiles), (spread(send), from_beyond(one), base, filled))
-    l1, l2, near = layers(send, state, (8, 128))
+    chunks, cells = sds(group, 4, 4, 128), sds(8, 4, 128)
+    send, state, mine = call(
+        insert_kernel, (chunks, tiles, cells), (spread(send), from_beyond(one), base, filled)
+    )
+    l1, l2, near = layers(send, mine, (4, 128))
     beyond = from_beyond(l1)
     wmain, wside = sds(2, 2, 15, 384, 128, dtype=BF16), sds(2, 2, 3, 384, 128, dtype=BF16)
-    fshape = sds(12, 32, 512, dtype=BF16)
-    whi, wlo, xr, own, bside, fs, dpart, gpart = call(
+    whi, wlo, xr, own, bside, dpart, gpart = call(
         setup_main_kernel,
-        (wmain, wmain, sds(48, 8, 128), tiles, sds(2, 64, 256, dtype=BF16), fshape, tiles, tiles),
-        (l1, l2, near),
+        (wmain, wmain, sds(48, 8, 128), tiles, sds(2, 64, 256, dtype=BF16), tiles, tiles),
+        (l1, l2, near, state),
         [pltpu.VMEM((12, 512, 64), BF16), pltpu.VMEM((4, 64, 256), BF16)],
         flops=3 * busy,
     )
-    bhi, blo, xrb, fsb, gsq, safe2, press, send, mine = call(
+    bhi, blo, xrb, gsq, safe2, press, send, mine = call(
         setup_beyond_kernel,
-        (wside, wside, sds(16, 8, 128), sds(4, 32, 512, dtype=BF16), tiles, rows, rows, sds(group, 4, 128), rows),
+        (wside, wside, sds(16, 8, 128), tiles, rows, rows, chunks, cells),
         (beyond, own, bside, dpart, gpart, filled, before),
         [pltpu.VMEM((4, 512, 64), BF16), pltpu.VMEM((8, 8, 128), F32)],
     )
     errs = None
     for it in range(ITERS):
         last = it == ITERS - 1
-        l1, l2, near = layers(send, mine, (128,))
+        l1, l2, near = layers(send, mine, (128,) if it else (4, 128))
         beyond = from_beyond(l1)
-        accels = (sds(group, 4, 4, 128), sds(8, 4, 128))
         if it == 0:
             (part,) = call(
-                first_main_kernel, (sds(8, 16, 128),), (l1, l2, near, xr, whi, wlo, fs), [features(12)], flops=busy
+                first_main_kernel, (sds(8, 16, 128),), (l1, l2, near, xr, whi, wlo), [features(12)] * 2, flops=busy
             )
             send, mine, grad, aux = call(
                 first_accel_kernel,
-                (*accels, tiles, tiles),
-                (beyond, xrb, bhi, blo, fsb, part, l1, l2, xr, own, gsq, safe2),
-                [features(4)],
+                (chunks, cells, tiles, tiles),
+                (beyond, xrb, bhi, blo, part, l1, l2, xr, own, gsq, safe2),
+                [features(4)] * 2,
             )
         else:
             (part,) = call(
                 main_kernel, (tiles,), (l1, l2, near, xr, whi, wlo), [features(12)], flops=busy, features=scaled_features
             )
             send, mine = call(
-                accel_kernel, accels, (beyond, xrb, bhi, blo, part, l1, l2, xr, grad), [features(4)]
+                accel_kernel, (chunks, cells), (beyond, xrb, bhi, blo, part, l1, l2, xr, grad), [features(4)]
             )
         l1, l2, near = layers(send, mine, (4, 128))
         beyond = from_beyond(l1)

time: 161 us -> 160 us (level)
  no operation moved by 1% of the time
where the time goes in v4:
time: 160 us; the launch traced here: 159 us
  blocking collectives  97.5 us (61%)
  Pallas kernels  26.3 us (16%)
  starting transfers between devices  21.7 us (14%)
  local copies, waits for them, and re-layouts  8.13 us (5%)
  waiting for transfers between devices  3.98 us (2%)
  between operations  1.71 us (1%)
    all_to_all x6, blocking collectives, spread(): return lax.all_to_all(send, GROUP, 0, 0)  97.5 us
    pallas_call x21, Pallas kernels, call(): pl.pallas_call(named, out_shape=outs, in_specs=specs, out_specs=jax.tree....  26.3 us
    all_to_all x1, starting transfers between devices, on_device(): recv = lax.all_to_all(send, 'gx0', 0, 0)  8.94 us
    all_to_all x1, starting transfers between devices, spread(): return lax.all_to_all(send, GROUP, 0, 0)  8.58 us
    unnamed x16, local copies, waits for them, and re-layouts  8.13 us
    ppermute x6, starting transfers between devices, from_beyond(): return lax.ppermute(layer, ('gx0', 'gx1'), across)  4.16 us
    all_to_all x1, waiting for transfers between devices, spread(): return lax.all_to_all(send, GROUP, 0, 0)  3.96 us
  transfers between devices with their start and end apart: 8, of which 1 were waited for; matrix products, arithmetic and copies ran while one was open for 0% of the time, Pallas kernels for 11%

profile of v4, /device:TPU:1, one launch (start us, length us, event | category | flops | bytes accessed | tf_op | source)
XLA Modules:
  0.0 159.2 jit_solution(2019382516339339086)
XLA Ops:
  1.3 1.4 shard_map.112
  2.7 8.6 %all-to-all-start = ((f32[32,8,128]{2,1,0:T(8,128)}), f32[32,8,128]{2,1,0:T(8,128)S(1)}, u32[]{:S(2)}, u32[]{:S(2)}) async-start(f32[32,8,128]{2,1,0:T(8,128)} %get-tuple-element.60), calls=%async_computation | async-start | bytes 262144 | tf_op jit(solution)/shard_map/all_to_all | solution.py:563
  11.2 0.7 collective-permute-start
  11.9 0.0 copy-start
  11.9 0.7 copy-done
  12.6 0.7 copy-done.1
  13.3 0.7 copy-done.2
  14.0 0.7 copy-done.3
  14.7 0.1 shard_map.113
  14.8 0.0 collective-permute-done.refs_1_
  14.8 4.0 %all-to-all-done.refs_0_ = f32[32,8,128]{2,1,0:T(8,128)S(1)} async-done(((f32[32,8,128]{2,1,0:T(8,128)}), f32[32,8,128]{2,1,0:T(8,128)S(1)}, u32[]{:S(2)}, u32[]{:S(2)}) %all-to-all-start) | async-done | bytes 131104 | tf_op jit(solution)/shard_map/all_to_all | solution.py:563
  18.8 1.1 shard_map.114
  19.9 15.1 %all_to_all.40.refs_0_ = f32[32,4,4,128]{3,2,1,0:T(4,128)S(1)} all-to-all(f32[32,4,4,128]{3,2,1,0:T(4,128)S(1)} %get-tuple-element.64), channel_id=1, replica_groups=mesh['gx0'=8,'gx1'=2,'gy'=4,'gz'=4] {'gx1','gy','gz'}, dimensions={0} | all-to-all | bytes 524288 | tf_op jit(solution)/shard_map/all_to_all | solution.py:563
  35.1 0.7 collective-permute-start.1
  35.7 5.5 %shard_map.116 = (bf16[2,2,15,384,128]{4,3,2,1,0:T(8,128)(2,1)S(1)}, bf16[2,2,15,384,128]{4,3,2,1,0:T(8,128)(2,1)S(1)}, f32[48,8,128]{2,1,0:T(8,128)S(1)}, f32[8...) custom-call(f32[16,4,128]{2,1,0:T(4,128)S(1)} %get-tuple-element.66., ...), custom_call_target="tpu_custom_call" | custom-call | flops 12000000000 | tf_op jit(solution)/shard_map/pallas_call | solution.py:540
  41.2 0.0 copy-start.4
  41.2 0.0 copy-start.6
  41.2 0.0 collective-permute-done.1.refs_0_
  41.2 1.1 shard_map.117
  42.3 16.2 %all_to_all.41.refs_0_ = f32[32,4,4,128]{3,2,1,0:T(4,128)S(1)} all-to-all(f32[32,4,4,128]{3,2,1,0:T(4,128)S(1)} %get-tuple-element.75), channel_id=1, replica_groups=mesh['gx0'=8,'gx1'=2,'gy'=4,'gz'=4] {'gx1','gy','gz'}, dimensions={0} | all-to-all | bytes 524288 | tf_op jit(solution)/shard_map/all_to_all | solution.py:563
  58.6 0.7 collective-permute-start.2
  59.2 2.6 %shard_map.119.refs_4_ = f32[8,16,128]{2,1,0:T(8,128)S(1)} custom-call(f32[16,4,128]{2,1,0:T(4,128)S(1)} %get-tuple-element.77.refs_0_.refs_5_, f32[16,4,128]{2,1,0:T(4,128)S(1)} %get-tuple-element.81.refs_1_.refs_6_, f32[16,4,128]{2,1,0:T(4,128)S(1)} %get-tuple-element.82.refs_2_, f32[48,8,128]{2,1,0:T(8,128)S(1)} %get-tuple-element.83.refs_3_.refs_7_, ...), custom_call_target="tpu_custom_call" | custom-call | flops 4000000000 | tf_op jit(solution)/shard_map/pallas_call | solution.py:540
  61.8 0.0 collective-permute-done.2.refs_0_
  61.8 0.6 shard_map.120
  62.5 16.2 %all_to_all.42.refs_0_ = f32[32,4,4,128]{3,2,1,0:T(4,128)S(1)} all-to-all(f32[32,4,4,128]{3,2,1,0:T(4,128)S(1)} %get-tuple-element.88), channel_id=1, replica_groups=mesh['gx0'=8,'gx1'=2,'gy'=4,'gz'=4] {'gx1','gy','gz'}, dimensions={0} | all-to-all | bytes 524288 | tf_op jit(solution)/shard_map/all_to_all | solution.py:563
  78.7 0.7 collective-permute-start.3
  79.3 2.4 %shard_map.122.refs_4_ = f32[8,8,128]{2,1,0:T(8,128)S(1)} custom-call(f32[16,4,128]{2,1,0:T(4,128)S(1)} %get-tuple-element.90.refs_0_.refs_5_, f32[16,4,128]{2,1,0:T(4,128)S(1)} %get-tuple-element.91.refs_1_.refs_6_, f32[16,4,128]{2,1,0:T(4,128)S(1)} %get-tuple-element.92.refs_2_, f32[48,8,128]{2,1,0:T(8,128)S(1)} %get-tuple-element.83.refs_3_.refs_7_, ...), custom_call_target="tpu_custom_call" | custom-call | flops 4000000000 | tf_op jit(solution)/shard_map/pallas_call | solution.py:540
  81.8 0.0 collective-permute-done.3.refs_0_
  81.8 0.6 shard_map.123
  82.4 15.9 %all_to_all.43.refs_0_ = f32[32,4,128]{2,1,0:T(4,128)S(1)} all-to-all(f32[32,4,128]{2,1,0:T(4,128)S(1)} %get-tuple-element.96), channel_id=1, replica_groups=mesh['gx0'=8,'gx1'=2,'gy'=4,'gz'=4] {'gx1','gy','gz'}, dimensions={0} | all-to-all | bytes 131072 | tf_op jit(solution)/shard_map/all_to_all | solution.py:563
  98.3 0.8 collective-permute-start.4
  99.2 2.3 %shard_map.125.refs_4_ = f32[8,8,128]{2,1,0:T(8,128)S(1)} custom-call(f32[16,128]{1,0:T(8,128)S(1)} %get-tuple-element.98.refs_0_.refs_5_, f32[16,128]{1,0:T(8,128)S(1)} %get-tuple-element.99.refs_1_.refs_6_, f32[16,128]{1,0:T(8,128)S(1)} %get-tuple-element.100.refs_2_, f32[48,8,128]{2,1,0:T(8,128)S(1)} %get-tuple-element.83.refs_3_.refs_7_, ...), custom_call_target="tpu_custom_call" | custom-call | flops 4000000000 | tf_op jit(solution)/shard_map/pallas_call | solution.py:540
  101.5 0.0 collective-permute-done.4.refs_0_
  101.5 0.6 shard_map.126
  102.1 16.9 %all_to_all.44.refs_0_ = f32[32,4,4,128]{3,2,1,0:T(4,128)S(1)} all-to-all(f32[32,4,4,128]{3,2,1,0:T(4,128)S(1)} %get-tuple-element.101), channel_id=1, replica_groups=mesh['gx0'=8,'gx1'=2,'gy'=4,'gz'=4] {'gx1','gy','gz'}, dimensions={0} | all-to-all | bytes 524288 | tf_op jit(solution)/shard_map/all_to_all | solution.py:563
  119.1 0.7 collective-permute-start.5
  119.8 0.0 copy-done.4
  119.8 2.4 %shard_map.128.refs_4_ = f32[8,8,128]{2,1,0:T(8,128)S(1)} custom-call(f32[16,4,128]{2,1,0:T(4,128)S(1)} %get-tuple-element.103.refs_0_.refs_5_, f32[16,4,128]{2,1,0:T(4,128)S(1)} %get-tuple-element.104.refs_1_.refs_6_, f32[16,4,128]{2,1,0:T(4,128)S(1)} %get-tuple-element.105.refs_2_, f32[48,8,128]{2,1,0:T(8,128)S(1)} %get-tuple-element.83.refs_3_.refs_7_, ...), custom_call_target="tpu_custom_call" | custom-call | flops 4000000000 | tf_op jit(solution)/shard_map/pallas_call | solution.py:540
  122.2 0.0 collective-permute-done.5.refs_0_
  122.2 1.2 shard_map.129
  123.4 17.1 %all_to_all.45.refs_0_ = f32[32,16,128]{2,1,0:T(8,128)S(1)} all-to-all(f32[32,16,128]{2,1,0:T(8,128)S(1)} %get-tuple-element.109), channel_id=1, replica_groups=mesh['gx0'=8,'gx1'=2,'gy'=4,'gz'=4] {'gx1','gy','gz'}, dimensions={0} | all-to-all | bytes 524288 | tf_op jit(solution)/shard_map/all_to_all | solution.py:563
  140.6 0.7 shard_map.130
  141.3 8.9 %all-to-all-start.7 = ((f32[8,24,128]{2,1,0:T(8,128)}), f32[8,24,128]{2,1,0:T(8,128)S(1)}, u32[]{:S(2)}, u32[]{:S(2)}) async-start(f32[8,24,128]{2,1,0:T(8,128)} %get-tuple-element.111), calls=%async_computation.7 | async-start | bytes 196608 | tf_op jit(solution)/shard_map/all_to_all | solution.py:647
  150.2 2.7 %copy-done.5 = bf16[2,2,15,384,128]{4,3,2,1,0:T(8,128)(2,1)S(1)} copy-done((bf16[2,2,15,384,128]{4,3,2,1,0:T(8,128)(2,1)S(1)}, bf16[2,2,15,384,128]{4,3,2,1,0:T(8,128)(2,1)}, u32[]{:S(2)}) %copy-start.5) | copy-done | bytes 5898264
  152.9 2.7 %copy-done.7 = bf16[2,2,15,384,128]{4,3,2,1,0:T(8,128)(2,1)S(1)} copy-done((bf16[2,2,15,384,128]{4,3,2,1,0:T(8,128)(2,1)S(1)}, bf16[2,2,15,384,128]{4,3,2,1,0:T(8,128)(2,1)}, u32[]{:S(2)}) %copy-start.7) | copy-done | bytes 5898264
  155.5 2.3 %shard_map.131.refs_4_ = f32[8,8,128]{2,1,0:T(8,128)S(1)} custom-call(f32[16,128]{1,0:T(8,128)S(1)} %get-tuple-element.112.refs_0_.refs_5_, f32[16,128]{1,0:T(8,128)S(1)} %get-tuple-element.113.refs_1_.refs_6_, f32[16,128]{1,0:T(8,128)S(1)} %get-tuple-element.114.refs_2_, f32[48,8,128]{2,1,0:T(8,128)S(1)} %get-tuple-element.83.refs_3_.refs_7_, ...), custom_call_target="tpu_custom_call" | custom-call | flops 4000000000 | tf_op jit(solution)/shard_map/pallas_call | solution.py:540
  157.9 0.0 all-to-all-done.7.refs_0_
  157.9 1.2 shard_map.132
  (11 shorter events, 0.2 us)
Async XLA Ops:
  2.7 16.1 %all-to-all-start = ((f32[32,8,128]{2,1,0:T(8,128)}), f32[32,8,128]{2,1,0:T(8,128)S(1)}, u32[]{:S(2)}, u32[]{:S(2)}) async-start(f32[32,8,128]{2,1,0:T(8,128)} %get-tuple-element.60), calls=%async_computation | async-start | bytes 262144 | tf_op jit(solution)/shard_map/all_to_all | solution.py:563
  11.2 3.6 %collective-permute-start = (f32[8,128]{1,0:T(8,128)}, f32[8,128]{1,0:T(8,128)S(1)}, u32[]{:S(2)}, u32[]{:S(2)}) collective-permute-start(f32[8,128]{1,0:T(8,128)} %get-tuple-element.61), channel_id=1, source_target_pairs={{16,32},{48,64},{80,96},{112,128},{144,160},{176,192},{208,224},{3... | collective-permute-start | bytes 12296 | tf_op jit(solution)/shard_map/ppermute | solution.py:566
  11.9 0.7 copy-start
  12.6 0.7 copy-start.1
  13.3 0.7 copy-start.2
  14.0 0.7 copy-start.3
  35.1 6.2 %collective-permute-start.1 = (f32[16,4,128]{2,1,0:T(4,128)S(1)}, f32[16,4,128]{2,1,0:T(4,128)S(1)}, u32[]{:S(2)}, u32[]{:S(2)}) collective-permute-start(f32[16,4,128]{2,1,0:T(4,128)S(1)} %get-tuple-element.66.refs_0_), channel_id=1, source_target_pairs={{16,32},{48,64},{80,96},{112,128},{144,160},{176,192},{208,224},{3... | collective-permute-start | bytes 98312 | tf_op jit(solution)/shard_map/ppermute | solution.py:566
  41.2 78.6 %copy-start.4 = (bf16[2,2,15,384,128]{4,3,2,1,0:T(8,128)(2,1)}, bf16[2,2,15,384,128]{4,3,2,1,0:T(8,128)(2,1)S(1)}, u32[]{:S(2)}) copy-start(bf16[2,2,15,384,128]{4,3,2,1,0:T(8,128)(2,1)S(1)} %get-tuple-element.84.refs_4_) | copy-start | bytes 17694724
  41.2 78.6 %copy-start.6 = (bf16[2,2,15,384,128]{4,3,2,1,0:T(8,128)(2,1)}, bf16[2,2,15,384,128]{4,3,2,1,0:T(8,128)(2,1)S(1)}, u32[]{:S(2)}) copy-start(bf16[2,2,15,384,128]{4,3,2,1,0:T(8,128)(2,1)S(1)} %get-tuple-element.85.refs_5_) | copy-start | bytes 17694724
  58.6 3.2 %collective-permute-start.2 = (f32[16,4,128]{2,1,0:T(4,128)S(1)}, f32[16,4,128]{2,1,0:T(4,128)S(1)}, u32[]{:S(2)}, u32[]{:S(2)}) collective-permute-start(f32[16,4,128]{2,1,0:T(4,128)S(1)} %get-tuple-element.77.refs_0_.refs_5_), channel_id=1, source_target_pairs={{16,32},{48,64},{80,96},{112,128},{144,160},{176,192},{208,224},{3... | collective-permute-start | bytes 98312 | tf_op jit(solution)/shard_map/ppermute | solution.py:566
  78.7 3.1 %collective-permute-start.3 = (f32[16,4,128]{2,1,0:T(4,128)S(1)}, f32[16,4,128]{2,1,0:T(4,128)S(1)}, u32[]{:S(2)}, u32[]{:S(2)}) collective-permute-start(f32[16,4,128]{2,1,0:T(4,128)S(1)} %get-tuple-element.90.refs_0_.refs_5_), channel_id=1, source_target_pairs={{16,32},{48,64},{80,96},{112,128},{144,160},{176,192},{208,224},{3... | collective-permute-start | bytes 98312 | tf_op jit(solution)/shard_map/ppermute | solution.py:566
  98.3 3.2 %collective-permute-start.4 = (f32[16,128]{1,0:T(8,128)S(1)}, f32[16,128]{1,0:T(8,128)S(1)}, u32[]{:S(2)}, u32[]{:S(2)}) collective-permute-start(f32[16,128]{1,0:T(8,128)S(1)} %get-tuple-element.98.refs_0_.refs_5_), channel_id=1, source_target_pairs={{16,32},{48,64},{80,96},{112,128},{144,160},{176,192},{208,224},{3... | collective-permute-start | bytes 24584 | tf_op jit(solution)/shard_map/ppermute | solution.py:566
  119.1 3.1 %collective-permute-start.5 = (f32[16,4,128]{2,1,0:T(4,128)S(1)}, f32[16,4,128]{2,1,0:T(4,128)S(1)}, u32[]{:S(2)}, u32[]{:S(2)}) collective-permute-start(f32[16,4,128]{2,1,0:T(4,128)S(1)} %get-tuple-element.103.refs_0_.refs_5_), channel_id=1, source_target_pairs={{16,32},{48,64},{80,96},{112,128},{144,160},{176,192},{208,224},{3... | collective-permute-start | bytes 98312 | tf_op jit(solution)/shard_map/ppermute | solution.py:566
  141.3 16.6 %all-to-all-start.7 = ((f32[8,24,128]{2,1,0:T(8,128)}), f32[8,24,128]{2,1,0:T(8,128)S(1)}, u32[]{:S(2)}, u32[]{:S(2)}) async-start(f32[8,24,128]{2,1,0:T(8,128)} %get-tuple-element.111), calls=%async_computation.7 | async-start | bytes 196608 | tf_op jit(solution)/shard_map/all_to_all | solution.py:647
  150.2 2.7 %copy-start.5 = (bf16[2,2,15,384,128]{4,3,2,1,0:T(8,128)(2,1)S(1)}, bf16[2,2,15,384,128]{4,3,2,1,0:T(8,128)(2,1)}, u32[]{:S(2)}) copy-start(bf16[2,2,15,384,128]{4,3,2,1,0:T(8,128)(2,1)} %copy-done.4) | copy-start | bytes 17694724
  152.9 2.7 %copy-start.7 = (bf16[2,2,15,384,128]{4,3,2,1,0:T(8,128)(2,1)S(1)}, bf16[2,2,15,384,128]{4,3,2,1,0:T(8,128)(2,1)}, u32[]{:S(2)}) copy-start(bf16[2,2,15,384,128]{4,3,2,1,0:T(8,128)(2,1)} %copy-done.6) | copy-start | bytes 17694724
